TPU v7x, 128 devices: a whole 4x4x4 slice. The times are simulated.
128 devices in a mesh: prow: 4 (over x), pcol: 32 (over z, y, core).
Axes of the slice: x: 4, y: 4, z: 4, core: 2. Of those that a mesh axis runs over, the one named last changes fastest.
Arguments:
- match_tiles: float32 [128, 8, 128, 128], P('pcol', 'prow'), may hold values from 0.05 to 1
- pattern: int32 [128, 8], replicated, may hold values from 0 to 127, as said below
- kept: int32 [128, 8], replicated, may hold values from 0 to 127, as said below
- panel_order: int32 [32], replicated, may hold values from 0 to 31, as said below
Outputs:
- clusters: float32 [128, 8, 128, 128], P('pcol', 'prow')
Inputs may be any that keep to these rules, and one draw needn't show every extreme that they name: `pattern`: slots r * 2 to r * 2 + 1 of a tile column name 2 different tile rows of the r-th of the equal row blocks along prow. Tile column j names itself and tile column j + 1 - 2 * (j % 2) in the row block that holds tile row j. Of the tile columns of one panel, the tile columns of any other panel name at most 1 different ones, and exactly 1 for some pairs of panels. `kept`: as for pattern, with the same 1; every named tile is nonzero in the product of the input matrix with itself. `panel_order`: A permutation in which every entry differs from its index by at most one.
All inputs are finite; a program needn't handle non-finite values.
Results may differ from a plain program's by a relative error of at most 0.0003.
Values sent between devices are 32-bit elements; how exact they have to be, the bound alone decides.
No kernel may reach another device: no remote copies, remote signals or barrier semaphores. Data moves between devices by JAX's collectives and lax.ppermute only.
A program may use at most 64 MiB of HBM per device.

v0:
```python
import functools

import jax
import jax.numpy as jnp
from jax import lax
from jax.experimental import pallas as pl
from jax.experimental.pallas import tpu as pltpu
from jax.sharding import PartitionSpec as P


SMEM = pl.BlockSpec(memory_space=pltpu.SMEM)
VMEM = pl.BlockSpec(memory_space=pltpu.VMEM)
ANY = pl.BlockSpec(memory_space=pl.ANY)

LANES = 128
SEND, FIRST, HOP, SECOND, _ = range(5)
TILE_BIT, SENT_BIT = 4, 8


def ring(size, step):
    return [(i, (i + step) % size) for i in range(size)]


def row_sums(partial_value, size):
    sums = [partial_value]
    for step in range(1, size):
        sums.append(lax.ppermute(partial_value, "prow", ring(size, step)))
    return tuple(sums)


def plan_kernel(
    permuted, whole, scal_ref, order_ref, in_ref, out_ref, plan_ref, grid_ref, line_ref
):
    place, row, _, _, depth = (scal_ref[i] for i in range(5))
    share = in_ref.shape[0] // 4
    shape = (LANES, LANES)
    down = lax.broadcasted_iota(jnp.int32, shape, 0)
    along = lax.broadcasted_iota(jnp.int32, shape, 1)
    line_ref[...] = jnp.full(line_ref.shape, -2, jnp.int32)
    line_ref[:1, : order_ref.shape[1]] = order_ref[...]
    held = jnp.broadcast_to(line_ref[:1, :], shape)
    if permuted:
        diagonal = jnp.where(down == along, held, 0)
        source = jnp.broadcast_to(jnp.sum(diagonal, axis=1, keepdims=True), shape)
    else:
        source = jnp.where(down < depth * 4, down, -1)
    names = in_ref[...]
    panels, inside = names // 4, lax.rem(names, 4)
    groups = (down // 4 == held).astype(jnp.bfloat16)
    level, wide = lax.div(down, depth), lax.div(along, depth)
    same_level = level == wide
    valid = jnp.logical_and(down < depth * 4, along < depth * 4)
    spread = jnp.logical_and(
        jnp.logical_and(lax.rem(down, depth) == lax.rem(along, depth), valid),
        jnp.logical_not(same_level),
    ).astype(jnp.bfloat16)
    other = jnp.logical_and(valid, source != held)

    def product(left, right):
        return jnp.dot(
            left.astype(jnp.bfloat16), right.astype(jnp.bfloat16),
            preferred_element_type=jnp.float32,
        )

    def gathered(block):
        kept = [out_ref[pl.ds(block * share + t, 1), :] for t in range(share)]
        hits = []
        for u in range(share):
            line = jnp.broadcast_to(in_ref[pl.ds(block * share + u, 1), :], names.shape)
            value = jnp.take_along_axis(line, names, axis=1)
            hit = value == kept[0]
            for t in range(1, share):
                hit = jnp.logical_or(hit, value == kept[t])
            hits.append(hit.astype(jnp.float32))
        return hits

    def analyse(block):
        hits = gathered(block)
        zero = jnp.zeros(shape, jnp.float32)
        found, named, column = [zero] * share, zero, zero
        for k in range(names.shape[0]):
            here = (source == panels[k : k + 1, :]).astype(jnp.float32)
            named += here
            column += here * inside[k : k + 1, :].astype(jnp.float32)
            for u in range(share):
                found[u] += here * hits[u][k : k + 1, :]
        found = [jnp.where(other, product(value, groups), 0.0) > 0.5 for value in found]
        named = jnp.maximum(product(named, groups), 1.0)
        column = jnp.floor(product(column, groups) / named + 0.5)
        both = jnp.logical_and(found[0], found[1])
        away = jnp.logical_and(both, jnp.logical_not(same_level)).astype(jnp.float32)
        return found, column, both, away, product(away, spread)

    if whole:
        misfit = jnp.zeros(shape, jnp.float32)
        for block in range(4):
            found, _, both, away, riding = analyse(block)
            need = jnp.logical_or(found[0], found[1])
            crowded = jnp.logical_or(
                riding > 1.5, jnp.logical_and(riding > 0.5, jnp.logical_or(need, both))
            )
            misfit += jnp.where(
                jnp.logical_and(same_level, jnp.logical_or(crowded, both)), 1.0, 0.0
            )
            arriving = product(same_level.astype(jnp.float32), away)
            misfit += jnp.where(jnp.logical_and(valid, arriving > 1.5), 1.0, 0.0)
        total = jnp.sum(jnp.sum(misfit, axis=0, keepdims=True), axis=1, keepdims=True)
        plan_ref[...] = jnp.broadcast_to((total > 0.5).astype(jnp.int32), plan_ref.shape)
        return

    found, column, both, away, riding = analyse(row)
    need = jnp.logical_or(found[0], found[1])
    direct = column + jnp.where(found[0], 0.0, float(TILE_BIT)) + SENT_BIT
    ride = product(away * column, spread) + TILE_BIT + SENT_BIT
    taken = jnp.logical_and(same_level, riding > 0.5)
    code = jnp.where(need, direct, jnp.where(taken, ride, 0.0))
    mine = (lax.broadcasted_iota(jnp.int32, (8, LANES), 1) == place).astype(jnp.float32)
    level_row = (
        lax.div(lax.broadcasted_iota(jnp.int32, (8, LANES), 1), depth) == lax.div(place, depth)
    ).astype(jnp.float32)
    first = lax.dot_general(
        mine.astype(jnp.bfloat16), found[0].astype(jnp.float32).astype(jnp.bfloat16),
        (((1,), (1,)), ((), ())), preferred_element_type=jnp.float32,
    )
    hop = product(level_row, away * (down + 1).astype(jnp.float32))
    grid_ref[0] = code
    grid_ref[1] = jnp.where(both, column + (TILE_BIT + SENT_BIT), 0.0)
    plan_ref[pl.ds(SEND, 1), :] = grid_ref[0, pl.ds(place, 1), :].astype(jnp.int32)
    plan_ref[pl.ds(FIRST, 1), :] = first[:1].astype(jnp.int32)
    plan_ref[pl.ds(HOP, 1), :] = hop[:1].astype(jnp.int32)
    plan_ref[pl.ds(SECOND, 1), :] = grid_ref[1, pl.ds(place, 1), :].astype(jnp.int32)


def plan(permuted, whole, scal, order_line, in_pattern, out_pattern):
    return pl.pallas_call(
        functools.partial(plan_kernel, permuted, whole),
        out_shape=jax.ShapeDtypeStruct((8, LANES), jnp.int32),
        in_specs=[SMEM, VMEM, VMEM, VMEM],
        out_specs=VMEM,
        scratch_shapes=[
            pltpu.VMEM((2, LANES, LANES), jnp.float32),
            pltpu.VMEM((8, LANES), jnp.int32),
        ],
        cost_estimate=pl.CostEstimate(
            flops=(4 if whole else 1) << 23, bytes_accessed=1 << 14, transcendentals=0
        ),
    )(scal, order_line, in_pattern, out_pattern)


def column_kernel(x_ref, part_ref):
    part_ref[...] = jnp.sum(x_ref[...], axis=(1, 2))


def column_partial(x):
    return pl.pallas_call(
        column_kernel,
        out_shape=jax.ShapeDtypeStruct((x.shape[0], x.shape[-1]), jnp.float32),
        in_specs=[VMEM],
        out_specs=VMEM,
        cost_estimate=pl.CostEstimate(flops=x.size, bytes_accessed=4 * x.size, transcendentals=0),
    )(x)


def send_kernel(line, plan_ref, x_ref, *rest):
    *sums, send_ref, normal, sems = rest
    panels = send_ref.shape[0]
    total = sums[0][...]
    for part in sums[1:]:
        total += part[...]
    normal[...] = x_ref[...] / total[:, None, None, :]

    def each(act):
        @pl.loop(0, panels)
        def _(slot):
            code = plan_ref[line, slot]

            @pl.when(code >= SENT_BIT)
            def _():
                tile = normal.at[code & 3, (code // TILE_BIT) & 1]
                act(pltpu.make_async_copy(tile, send_ref.at[slot], sems.at[slot]))

    each(lambda piece: piece.start())
    each(lambda piece: piece.wait())


def prepare(line, steps, x, sums, panels):
    tile = x.shape[-1]
    return pl.pallas_call(
        functools.partial(send_kernel, line),
        out_shape=jax.ShapeDtypeStruct((panels, tile, tile), jnp.float32),
        in_specs=[SMEM, VMEM] + [VMEM] * len(sums),
        out_specs=ANY,
        scratch_shapes=[
            pltpu.VMEM(x.shape, jnp.float32),
            pltpu.SemaphoreType.DMA((panels,)),
        ],
        cost_estimate=pl.CostEstimate(flops=x.size, bytes_accessed=3 << 20, transcendentals=0),
    )(steps, x, *sums)


def hop_kernel(scal_ref, plan_ref, got_ref, *rest):
    *outs, sems = rest
    place, depth = scal_ref[0], scal_ref[4]
    pieces = []
    for step, out in enumerate(outs):
        target = lax.rem(place + (step + 1) * depth, 4 * depth)
        slot = jnp.maximum(plan_ref[HOP, target] - 1, 0)
        pieces.append(pltpu.make_async_copy(got_ref.at[slot], out, sems.at[step]))
    for piece in pieces:
        piece.start()
    for piece in pieces:
        piece.wait()


def hop_tiles(scal, steps, got):
    tile = jax.ShapeDtypeStruct(got.shape[1:], jnp.float32)
    return pl.pallas_call(
        hop_kernel,
        out_shape=(tile,) * 3,
        in_specs=[SMEM, SMEM, ANY],
        out_specs=(VMEM,) * 3,
        scratch_shapes=[pltpu.SemaphoreType.DMA((3,))],
        cost_estimate=pl.CostEstimate(flops=0, bytes_accessed=6 << 16, transcendentals=0),
    )(scal, steps, got)


def split(value):
    high = value.astype(jnp.bfloat16)
    low = (value - high.astype(jnp.float32)).astype(jnp.bfloat16)
    return high, low


def product_kernel(
    permuted, scal_ref, order_ref, plan_ref, in_ref, out_pat_ref,
    own_ref, ahead_ref, behind_ref, far_low_ref, far_high_ref, got_ref, *rest,
):
    *extra_refs, sq_ref, part_ref, left, totals, sems = rest
    cols, share, tile, _ = own_ref.shape
    place, row, rows, depth = scal_ref[0], scal_ref[1], scal_ref[2], scal_ref[4]
    panel = order_ref[place]
    half = cols // 2

    def far_of(j):
        return far_low_ref[j] if j < half else far_high_ref[j - half]

    for j in range(cols):
        total = jnp.zeros((1, tile), jnp.float32)
        for piece in (own_ref[j], ahead_ref[j], behind_ref[j], far_of(j)):
            total += jnp.sum(piece.reshape(share * tile, tile), axis=0, keepdims=True)
        totals[pl.ds(j, 1), :] = total

    def named(j, rel, s):
        block = lax.rem(row + rel, rows)
        column = in_ref[block * share + s, panel * cols + j]
        return column, column // cols == panel

    def found(j, column, t):
        wanted = out_pat_ref[row * share + t, panel * cols + j]
        hit = wanted < 0
        at = 0
        for u in range(share):
            same = in_ref[row * share + u, column] == wanted
            hit = jnp.logical_or(hit, same)
            at = jnp.where(same, u, at)
        return hit, at

    def target_of(j, rel, s, t):
        return (
            left.at[j, rel, pl.ds(t * tile, tile), pl.ds(s * tile, tile)],
            sems.at[j, rel, s, t],
        )

    def start(j, rel, s, t, column, at):
        source = column // cols
        origin = order_ref[source] if permuted else source
        extra = jnp.logical_and(at == 1, plan_ref[FIRST, origin] > 0)
        target, sem = target_of(j, rel, s, t)

        @pl.when(jnp.logical_not(extra))
        def _():
            pltpu.make_async_copy(got_ref.at[origin], target, sem).start()

        if len(extra_refs) == 1:

            @pl.when(extra)
            def _():
                pltpu.make_async_copy(extra_refs[0].at[origin], target, sem).start()

        else:
            step = lax.rem(place // depth - origin // depth + 4, 4)
            for distance, ref in enumerate(extra_refs):

                @pl.when(jnp.logical_and(extra, step == distance + 1))
                def _():
                    pltpu.make_async_copy(ref, target, sem).start()

    @pl.loop(0, cols)
    def _(j):
        for rel in range(4):
            for s in range(share):
                column, is_own = named(j, rel, s)
                for t in range(share):
                    hit, at = found(j, column, t)
                    region = (j, rel, pl.ds(t * tile, tile), pl.ds(s * tile, tile))

                    @pl.when(jnp.logical_and(hit, jnp.logical_not(is_own)))
                    def _():
                        start(j, rel, s, t, column, at)

                    @pl.when(jnp.logical_and(hit, is_own))
                    def _():
                        local = lax.rem(column, cols)
                        left[region] = own_ref[local, at] / totals[pl.ds(local, 1), :]

                    @pl.when(jnp.logical_not(hit))
                    def _():
                        left[region] = jnp.zeros((tile, tile), jnp.float32)

    def column(j, far):
        sq_ref[j] = jnp.zeros((share, tile, tile), jnp.float32)
        for rel in range(4):
            any_hit = False
            for s in range(share):
                source, is_own = named(j, rel, s)
                for t in range(share):
                    hit, _ = found(j, source, t)
                    any_hit = jnp.logical_or(any_hit, hit)

                    @pl.when(jnp.logical_and(hit, jnp.logical_not(is_own)))
                    def _():
                        target, sem = target_of(j, rel, s, t)
                        pltpu.make_async_copy(got_ref.at[0], target, sem).wait()

            @pl.when(any_hit)
            def _():
                right = (own_ref.at[j], ahead_ref.at[j], far, behind_ref.at[j])[rel][...]
                right_high, right_low = split(right.reshape(share * tile, tile))
                left_high, left_low = split(left[j, rel])
                dot = functools.partial(jnp.dot, preferred_element_type=jnp.float32)
                added = (
                    dot(left_low, right_high) + dot(left_high, right_low)
                ) + dot(left_high, right_high)
                sq_ref[j] += added.reshape(share, tile, tile)

        value = sq_ref[j].reshape(share * tile, tile) / totals[pl.ds(j, 1), :]
        square = value * value
        sq_ref[j] = square.reshape(share, tile, tile)
        part_ref[pl.ds(j, 1), :] = jnp.sum(square, axis=0, keepdims=True)

    @pl.loop(0, half)
    def _(j):
        column(j, far_low_ref.at[j])

    @pl.loop(half, cols)
    def _(j):
        column(j, far_high_ref.at[j - half])


def multiply(permuted, scal, order, steps, in_pattern, out_pattern, own, gathered, got, extra):
    cols, share, tile, _ = own.shape
    depth = share * tile
    place_of_extra = [ANY] if len(extra) == 1 else [VMEM] * len(extra)
    return pl.pallas_call(
        functools.partial(product_kernel, permuted),
        out_shape=(
            jax.ShapeDtypeStruct(own.shape, jnp.float32),
            jax.ShapeDtypeStruct((cols, tile), jnp.float32),
        ),
        in_specs=[SMEM] * 5 + [VMEM] * 5 + [ANY] + place_of_extra,
        out_specs=(VMEM, VMEM),
        scratch_shapes=[
            pltpu.VMEM((cols, 4, depth, depth), jnp.float32),
            pltpu.VMEM((cols, tile), jnp.float32),
            pltpu.SemaphoreType.DMA((cols, 4, share, share)),
        ],
        cost_estimate=pl.CostEstimate(
            flops=cols * 12 * depth * depth * tile, bytes_accessed=6 << 20, transcendentals=0
        ),
    )(scal, order, steps, in_pattern, out_pattern, own, *gathered, got, *extra)


def divide_kernel(x_ref, *rest):
    *sums, out_ref = rest
    total = sums[0][...]
    for part in sums[1:]:
        total += part[...]
    out_ref[...] = x_ref[...] / total[:, None, None, :]


def divided(x, sums):
    return pl.pallas_call(
        divide_kernel,
        out_shape=jax.ShapeDtypeStruct(x.shape, jnp.float32),
        in_specs=[VMEM] * (1 + len(sums)),
        out_specs=VMEM,
        cost_estimate=pl.CostEstimate(flops=x.size, bytes_accessed=1 << 20, transcendentals=0),
    )(x, *sums)


def gather_rows(own, size):
    half = own.shape[0] // 2
    behind = lax.ppermute(own, "prow", ring(size, 1))
    ahead = lax.ppermute(own, "prow", ring(size, -1))
    far_low = lax.ppermute(behind[:half], "prow", ring(size, 1))
    far_high = lax.ppermute(ahead[half:], "prow", ring(size, -1))
    return ahead, behind, far_low, far_high


def expand(permuted, scal, order, steps, misfit, in_pattern, out_pattern, x, sums, own, rows):
    panels = order.shape[0]
    depth = panels // 4
    send = prepare(SEND, steps, x, sums, panels)
    got = lax.all_to_all(send, "pcol", 0, 0, tiled=True)
    gathered = gather_rows(own, rows)
    finish = functools.partial(
        multiply, permuted, scal, order, steps, in_pattern, out_pattern, own, gathered, got
    )

    def by_level(_):
        tiles = hop_tiles(scal, steps, got)
        return finish(
            tuple(
                lax.ppermute(tile, "pcol", ring(panels, (step + 1) * depth))
                for step, tile in enumerate(tiles)
            )
        )

    def by_second(_):
        more = prepare(SECOND, steps, x, sums, panels)
        return finish((lax.all_to_all(more, "pcol", 0, 0, tiled=True),))

    return lax.cond(misfit[0, 0] > 0, by_second, by_level, 0)


def local(match_tiles, pattern, kept, panel_order):
    cols = match_tiles.shape[0]
    panels = panel_order.shape[0]
    row = lax.axis_index("prow")
    rows = lax.axis_size("prow")
    place = lax.axis_index("pcol")
    panel = panel_order[place]
    order = panel_order
    order_line = order[None]
    pattern_rows = pattern.T
    kept_rows = kept.T
    scal = jnp.stack(
        [place, row, jnp.int32(rows), jnp.int32(cols), jnp.int32(panels // 4)]
    )
    first_plan = plan(False, False, scal, order_line, pattern_rows, kept_rows)

    sums = row_sums(column_partial(match_tiles), rows)
    below = [(i, i + 1) for i in range(panels - 1)]
    from_below = lax.ppermute(match_tiles, "pcol", below)
    from_above = lax.ppermute(match_tiles, "pcol", [(j, i) for i, j in below])
    own = jnp.where(panel == place, match_tiles, jnp.where(panel < place, from_below, from_above))
    sums, own = lax.optimization_barrier((sums, own))
    first_misfit = plan(False, True, scal, order_line, pattern_rows, kept_rows)
    second_plan = plan(True, False, scal, order_line, kept_rows, kept_rows)
    second_misfit = plan(True, True, scal, order_line, kept_rows, kept_rows)
    square, part = expand(
        False, scal, order, first_plan, first_misfit, pattern_rows, kept_rows,
        match_tiles, sums, own, rows,
    )
    sums = row_sums(part, rows)
    square, part = expand(
        True, scal, order, second_plan, second_misfit, kept_rows, kept_rows,
        square, sums, square, rows,
    )
    return divided(square, row_sums(part, rows))


def solution(mesh):
    in_specs = (P("pcol", "prow", None, None), P(), P(), P())
    out_specs = P("pcol", "prow", None, None)
    return jax.shard_map(local, mesh=mesh, in_specs=in_specs, out_specs=out_specs, check_vma=False)
```

profile of v0, /device:TPU:0, one launch (start us, length us, event | category | flops | bytes accessed | tf_op | source)
XLA Modules:
  0.0 149.4 jit_solution(17662648681404746017)
XLA Ops:
  0.0 1.4 collective-permute-start.10
  1.4 3.1 %collective-permute-start.9 = (f32[4,2,128,128]{3,2,1,0:T(8,128)}, f32[4,2,128,128]{3,2,1,0:T(8,128)S(1)}, u32[]{:S(2)}, u32[]{:S(2)}) collective-permute-start(f32[4,2,128,128]{3,2,1,0:T(8,128)} %x_ref.3), channel_id=1, source_target_pairs={{0,1},{1,2},{2,3},{3,4},{4,5},{5,6},{6,7},{7,8},{8,9},{9,10},{10,1... | collective-permute-start | bytes 1572872 | tf_op jit(solution)/shard_map/ppermute | solution.py:453
  4.5 1.1 shard_map.50.rest_0_
  5.6 1.7 %collective-permute-start.6 = (f32[4,128]{1,0:T(4,128)S(1)}, f32[4,128]{1,0:T(4,128)S(1)}, u32[]{:S(2)}, u32[]{:S(2)}) collective-permute-start(f32[4,128]{1,0:T(4,128)S(1)} %shard_map.50.rest_0_), channel_id=1, source_target_pairs={{0,32},{32,64},{64,96},{96,0},{1,33},{33,65},{65,97},{97,1},{2,34}... | collective-permute-start | bytes 6152 | tf_op jit(solution)/shard_map/ppermute | solution.py:27
  7.3 2.7 %collective-permute-start.7 = (f32[4,128]{1,0:T(4,128)S(1)}, f32[4,128]{1,0:T(4,128)S(1)}, u32[]{:S(2)}, u32[]{:S(2)}) collective-permute-start(f32[4,128]{1,0:T(4,128)S(1)} %shard_map.50.rest_0_), channel_id=1, source_target_pairs={{0,64},{32,96},{64,0},{96,32},{1,65},{33,97},{65,1},{97,33},{2,66}... | collective-permute-start | bytes 6152 | tf_op jit(solution)/shard_map/ppermute | solution.py:27
  10.0 1.4 collective-permute-start.8
  11.4 1.2 dynamic_slice.3
  14.1 1.8 %shard_map.49.plan_ref = s32[8,128]{1,0:T(8,128)S(1)} custom-call(s32[5]{0:T(128)S(1)} %pad_add_fusion.scal_ref, s32[1,32]{1,0:T(1,128)} %bitcast.22, s32[8,128]{1,0:T(8,128)} %bitcast.18, s32[8,128]{1,0:T(8,128)} %bitcast.8), custom_call_target="tpu_custom_call" | custom-call | flops 8388608 | bytes 16384 | tf_op jit(solution)/shard_map/pallas_call | solution.py:135
  15.9 1.1 select_select_fusion
  17.6 2.0 %shard_map.51 = f32[32,128,128]{2,1,0:T(8,128)} custom-call(s32[8,128]{1,0:T(8,128)S(1)} %shard_map.49.plan_ref, f32[4,2,128,128]{3,2,1,0:T(8,128)S(1)} %copy-done, f32[4,128]{1,0:T(4,128)S(1)} %shard_map.50.rest_0_, f32[4,128]{1,0:T(4,128)S(1)} %collective-permute-done.6.rest_1_, f32[4,128]{1,0:T(4,128)S(1)} %collective-permute-done.7.rest_2_, ...), custom_call_target="tpu_custom_call" | custom-call | flops 131072 | bytes 3145728 | tf_op jit(solution)/shard_map/pallas_call | solution.py:188
  19.6 10.0 %all-to-all-start.2 = ((f32[32,128,128]{2,1,0:T(8,128)}), f32[32,128,128]{2,1,0:T(8,128)S(1)}, u32[]{:S(2)}, u32[]{:S(2)}) async-start(f32[32,128,128]{2,1,0:T(8,128)} %shard_map.51), calls=%async_computation.2 | async-start | bytes 4194304 | tf_op jit(solution)/shard_map/all_to_all | solution.py:413
  30.3 2.7 %collective-permute-start.11 = (f32[4,2,128,128]{3,2,1,0:T(8,128)S(1)}, f32[4,2,128,128]{3,2,1,0:T(8,128)S(1)}, u32[]{:S(2)}, u32[]{:S(2)}) collective-permute-start(f32[4,2,128,128]{3,2,1,0:T(8,128)S(1)} %select_select_fusion), channel_id=1, source_target_pairs={{0,96},{32,0},{64,32},{96,64},{1,97},{33,1},{65,33},{97,65},{2,98}... | collective-permute-start | bytes 1572872 | tf_op jit(solution)/shard_map/ppermute | solution.py:403
  32.9 12.1 %collective-permute-done.12 = f32[4,2,128,128]{3,2,1,0:T(8,128)S(1)} collective-permute-done((f32[4,2,128,128]{3,2,1,0:T(8,128)S(1)}, f32[4,2,128,128]{3,2,1,0:T(8,128)S(1)}, u32[]{:S(2)}, u32[]{:S(2)}) %collective-permute-start.12) | collective-permute-done | bytes 524320 | tf_op jit(solution)/shard_map/ppermute | solution.py:402
  46.8 3.1 %collective-permute-start.14 = (f32[2,2,128,128]{3,2,1,0:T(8,128)}, f32[2,2,128,128]{3,2,1,0:T(8,128)}, u32[]{:S(2)}, u32[]{:S(2)}) collective-permute-start(f32[2,2,128,128]{3,2,1,0:T(8,128)} %slice.25), channel_id=1, source_target_pairs={{0,96},{32,0},{64,32},{96,64},{1,97},{33,1},{65,33},{97,65},{2,98}... | collective-permute-start | bytes 786440 | tf_op jit(solution)/shard_map/ppermute | solution.py:405
  49.9 2.8 %shard_map.48 = s32[8,128]{1,0:T(8,128)} custom-call(s32[5]{0:T(128)S(1)} %pad_add_fusion.scal_ref, s32[1,32]{1,0:T(1,128)S(1)} %bitcast.24, s32[8,128]{1,0:T(8,128)S(1)} %bitcast.19, s32[8,128]{1,0:T(8,128)S(1)} %bitcast.9), custom_call_target="tpu_custom_call" | custom-call | flops 33554432 | bytes 16384 | tf_op jit(solution)/shard_map/pallas_call | solution.py:135
  52.7 1.2 slice.19
  55.1 4.6 %all-to-all-done.2 = f32[32,128,128]{2,1,0:T(8,128)S(1)} async-done(((f32[32,128,128]{2,1,0:T(8,128)}), f32[32,128,128]{2,1,0:T(8,128)S(1)}, u32[]{:S(2)}, u32[]{:S(2)}) %all-to-all-start.2) | async-done | bytes 2097184 | tf_op jit(solution)/shard_map/all_to_all | solution.py:413
  59.7 17.2 %conditional.2 = ((f32[4,2,128,128]{3,2,1,0:T(8,128)S(1)}, f32[4,128]{1,0:T(4,128)})) conditional(s32[]{:T(128)} %bitcast.6, (s32[5]{0:T(128)S(1)}, s32[8,128]{1,0:T(8,128)S(1)}, f32[32,128,128]{2,1,0:T(8,128)S(1)}, s32[32]{0:T(128)S(1)}, s32[8,128]{1,0:T(8,128)S(1)}, /*index=5*/s32[8,128]{1,0:T(8,128)S(1)}, f32[4,2,128,128]{3,2,1,0:T(8,128)S(1)}, ...), branch_computations={%region_0.1_spmd, %region_1.2_spmd} | conditional | flops 402784256 | bytes 17825856 | solution.py:432
  59.7 1.6 %branch_0_fun.4 = (f32[128,128]{1,0:T(8,128)}, f32[128,128]{1,0:T(8,128)}, f32[128,128]{1,0:T(8,128)}) custom-call(s32[5]{0:T(128)S(1)} %get-tuple-element.107.scal_ref, s32[8,128]{1,0:T(8,128)S(1)} %get-tuple-element.109.plan_ref, f32[32,128,128]{2,1,0:T(8,128)S(1)} %get-tuple-element.117.got_ref), custom_call_target="tpu_custom_call" | custom-call | bytes 393216 | tf_op jit(solution)/shard_map/cond/branch_0_fun/pallas_call | solution.py:217
  61.4 1.5 %collective-permute-start.1 = (f32[128,128]{1,0:T(8,128)}, f32[128,128]{1,0:T(8,128)S(1)}, u32[]{:S(2)}, u32[]{:S(2)}) collective-permute-start(f32[128,128]{1,0:T(8,128)} %get-tuple-element.119), channel_id=1, source_target_pairs={{0,16},{1,17},{2,18},{3,19},{4,20},{5,21},{6,22},{7,23},{8,24},{9,... | collective-permute-start | bytes 196616 | tf_op jit(solution)/shard_map/cond/branch_0_fun/ppermute | solution.py:423
  62.9 2.1 %collective-permute-start.2 = (f32[128,128]{1,0:T(8,128)}, f32[128,128]{1,0:T(8,128)S(1)}, u32[]{:S(2)}, u32[]{:S(2)}) collective-permute-start(f32[128,128]{1,0:T(8,128)} %get-tuple-element.120), channel_id=1, source_target_pairs={{0,24},{1,25},{2,26},{3,27},{4,28},{5,29},{6,30},{7,31},{8,0},{9,1... | collective-permute-start | bytes 196616 | tf_op jit(solution)/shard_map/cond/branch_0_fun/ppermute | solution.py:423
  65.1 2.7 %collective-permute-done.rest_0_ = f32[128,128]{1,0:T(8,128)S(1)} collective-permute-done((f32[128,128]{1,0:T(8,128)}, f32[128,128]{1,0:T(8,128)S(1)}, u32[]{:S(2)}, u32[]{:S(2)}) %collective-permute-start) | collective-permute-done | bytes 65568 | tf_op jit(solution)/shard_map/cond/branch_0_fun/ppermute | solution.py:423
  67.8 0.8 collective-permute-done.2.rest_2_
  69.3 7.3 %branch_0_fun.5 = (f32[4,2,128,128]{3,2,1,0:T(8,128)S(1)}, f32[4,128]{1,0:T(4,128)}) custom-call(s32[5]{0:T(128)S(1)} %get-tuple-element.107.scal_ref, s32[32]{0:T(128)} %copy-done.19, s32[8,128]{1,0:T(8,128)S(1)} %get-tuple-element.109.plan_ref, s32[8,128]{1,0:T(8,128)} %copy-done.15, s32[8,128]{1,0:T(8,128)S(1)} %get-tuple-element.111.out_pat_ref, ...), custom_call_target="tpu_custom_call" | custom-call | flops 402653184 | bytes 6291456 | tf_op jit(solution)/shard_map/cond/branch_0_fun/pallas_call | solution.py:363
  76.9 1.6 %collective-permute-start.15 = (f32[4,128]{1,0:T(4,128)}, f32[4,128]{1,0:T(4,128)S(1)}, u32[]{:S(2)}, u32[]{:S(2)}) collective-permute-start(f32[4,128]{1,0:T(4,128)} %get-tuple-element.179.rest_0_), channel_id=1, source_target_pairs={{0,32},{32,64},{64,96},{96,0},{1,33},{33,65},{65,97},{97,1},{2,34}... | collective-permute-start | bytes 6152 | tf_op jit(solution)/shard_map/ppermute | solution.py:27
  78.9 2.4 %collective-permute-start.17 = (f32[4,128]{1,0:T(4,128)}, f32[4,128]{1,0:T(4,128)S(1)}, u32[]{:S(2)}, u32[]{:S(2)}) collective-permute-start(f32[4,128]{1,0:T(4,128)} %get-tuple-element.179.rest_0_), channel_id=1, source_target_pairs={{0,96},{32,0},{64,32},{96,64},{1,97},{33,1},{65,33},{97,65},{2,98}... | collective-permute-start | bytes 6152 | tf_op jit(solution)/shard_map/ppermute | solution.py:27
  81.3 1.7 %shard_map.47.plan_ref = s32[8,128]{1,0:T(8,128)S(1)} custom-call(s32[5]{0:T(128)S(1)} %pad_add_fusion.scal_ref, s32[1,32]{1,0:T(1,128)} %bitcast.23, s32[8,128]{1,0:T(8,128)S(1)} %bitcast.12, s32[8,128]{1,0:T(8,128)S(1)} %bitcast.13), custom_call_target="tpu_custom_call" | custom-call | flops 8388608 | bytes 16384 | tf_op jit(solution)/shard_map/pallas_call | solution.py:135
  83.7 2.3 %shard_map.52 = f32[32,128,128]{2,1,0:T(8,128)} custom-call(s32[8,128]{1,0:T(8,128)S(1)} %shard_map.47.plan_ref, f32[4,2,128,128]{3,2,1,0:T(8,128)S(1)} %get-tuple-element.178.x_ref, f32[4,128]{1,0:T(4,128)} %get-tuple-element.179.rest_0_, f32[4,128]{1,0:T(4,128)S(1)} %collective-permute-done.15.rest_1_, f32[4,128]{1,0:T(4,128)S(1)} %collective-permute-done.16.rest_2_, ...), custom_call_target="tpu_custom_call" | custom-call | flops 131072 | bytes 3145728 | tf_op jit(solution)/shard_map/pallas_call | solution.py:188
  86.0 6.0 %all-to-all-start.3 = ((f32[32,128,128]{2,1,0:T(8,128)}), f32[32,128,128]{2,1,0:T(8,128)S(1)}, u32[]{:S(2)}, u32[]{:S(2)}) async-start(f32[32,128,128]{2,1,0:T(8,128)} %shard_map.52), calls=%async_computation.3 | async-start | bytes 4194304 | tf_op jit(solution)/shard_map/all_to_all | solution.py:413
  92.2 3.1 %collective-permute-start.18 = (f32[4,2,128,128]{3,2,1,0:T(8,128)S(1)}, f32[4,2,128,128]{3,2,1,0:T(8,128)S(1)}, u32[]{:S(2)}, u32[]{:S(2)}) collective-permute-start(f32[4,2,128,128]{3,2,1,0:T(8,128)S(1)} %get-tuple-element.178.x_ref), channel_id=1, source_target_pairs={{0,96},{32,0},{64,32},{96,64},{1,97},{33,1},{65,33},{97,65},{2,98}... | collective-permute-start | bytes 1572872 | tf_op jit(solution)/shard_map/ppermute | solution.py:403
  95.3 12.1 %collective-permute-done.19 = f32[4,2,128,128]{3,2,1,0:T(8,128)S(1)} collective-permute-done((f32[4,2,128,128]{3,2,1,0:T(8,128)S(1)}, f32[4,2,128,128]{3,2,1,0:T(8,128)S(1)}, u32[]{:S(2)}, u32[]{:S(2)}) %collective-permute-start.19) | collective-permute-done | bytes 524320 | tf_op jit(solution)/shard_map/ppermute | solution.py:402
  108.2 0.8 copy-done.6
  109.7 3.2 %collective-permute-start.21 = (f32[2,2,128,128]{3,2,1,0:T(8,128)}, f32[2,2,128,128]{3,2,1,0:T(8,128)}, u32[]{:S(2)}, u32[]{:S(2)}) collective-permute-start(f32[2,2,128,128]{3,2,1,0:T(8,128)} %slice.27), channel_id=1, source_target_pairs={{0,96},{32,0},{64,32},{96,64},{1,97},{33,1},{65,33},{97,65},{2,98}... | collective-permute-start | bytes 786440 | tf_op jit(solution)/shard_map/ppermute | solution.py:405
  112.9 2.8 %shard_map.46 = s32[8,128]{1,0:T(8,128)} custom-call(s32[5]{0:T(128)S(1)} %pad_add_fusion.scal_ref, s32[1,32]{1,0:T(1,128)S(1)} %bitcast.25, s32[8,128]{1,0:T(8,128)S(1)} %bitcast.14, s32[8,128]{1,0:T(8,128)S(1)} %bitcast.15), custom_call_target="tpu_custom_call" | custom-call | flops 33554432 | bytes 16384 | tf_op jit(solution)/shard_map/pallas_call | solution.py:135
  115.7 1.2 slice.18
  118.1 4.0 %all-to-all-done.3 = f32[32,128,128]{2,1,0:T(8,128)S(1)} async-done(((f32[32,128,128]{2,1,0:T(8,128)}), f32[32,128,128]{2,1,0:T(8,128)S(1)}, u32[]{:S(2)}, u32[]{:S(2)}) %all-to-all-start.3) | async-done | bytes 2097184 | tf_op jit(solution)/shard_map/all_to_all | solution.py:413
  122.1 16.5 %conditional.3 = ((f32[4,2,128,128]{3,2,1,0:T(8,128)}, f32[4,128]{1,0:T(4,128)S(1)})) conditional(s32[]{:T(128)} %bitcast.4, (s32[5]{0:T(128)S(1)}, s32[8,128]{1,0:T(8,128)S(1)}, f32[32,128,128]{2,1,0:T(8,128)S(1)}, s32[32]{0:T(128)S(1)}, s32[8,128]{1,0:T(8,128)S(1)}, /*index=5*/f32[4,2,128,128]{3,2,1,0:T(8,128)S(1)}, f32[4,2,128,128]{3,2,1,0:T(8,128)}, ...), branch_computations={%region_2.3_spmd, %region_3.4_spmd} | conditional | flops 402784256 | bytes 13631496 | solution.py:432
  122.1 1.6 %branch_0_fun.6 = (f32[128,128]{1,0:T(8,128)}, f32[128,128]{1,0:T(8,128)}, f32[128,128]{1,0:T(8,128)}) custom-call(s32[5]{0:T(128)S(1)} %get-tuple-element.137.scal_ref, s32[8,128]{1,0:T(8,128)S(1)} %get-tuple-element.139.plan_ref, f32[32,128,128]{2,1,0:T(8,128)S(1)} %get-tuple-element.146.got_ref), custom_call_target="tpu_custom_call" | custom-call | bytes 393216 | tf_op jit(solution)/shard_map/cond/branch_0_fun/pallas_call | solution.py:217
  123.8 1.5 %collective-permute-start.4 = (f32[128,128]{1,0:T(8,128)}, f32[128,128]{1,0:T(8,128)S(1)}, u32[]{:S(2)}, u32[]{:S(2)}) collective-permute-start(f32[128,128]{1,0:T(8,128)} %get-tuple-element.148), channel_id=1, source_target_pairs={{0,16},{1,17},{2,18},{3,19},{4,20},{5,21},{6,22},{7,23},{8,24},{9,... | collective-permute-start | bytes 196616 | tf_op jit(solution)/shard_map/cond/branch_0_fun/ppermute | solution.py:423
  125.3 2.1 %collective-permute-start.5 = (f32[128,128]{1,0:T(8,128)}, f32[128,128]{1,0:T(8,128)}, u32[]{:S(2)}, u32[]{:S(2)}) collective-permute-start(f32[128,128]{1,0:T(8,128)} %get-tuple-element.149), channel_id=1, source_target_pairs={{0,24},{1,25},{2,26},{3,27},{4,28},{5,29},{6,30},{7,31},{8,0},{9,1... | collective-permute-start | bytes 196616 | tf_op jit(solution)/shard_map/cond/branch_0_fun/ppermute | solution.py:423
  127.4 2.7 %collective-permute-done.3.rest_0_ = f32[128,128]{1,0:T(8,128)S(1)} collective-permute-done((f32[128,128]{1,0:T(8,128)}, f32[128,128]{1,0:T(8,128)S(1)}, u32[]{:S(2)}, u32[]{:S(2)}) %collective-permute-start.3) | collective-permute-done | bytes 65568 | tf_op jit(solution)/shard_map/cond/branch_0_fun/ppermute | solution.py:423
  130.2 1.0 collective-permute-done.5.rest_2_
  131.1 7.1 %branch_0_fun.7 = (f32[4,2,128,128]{3,2,1,0:T(8,128)}, f32[4,128]{1,0:T(4,128)S(1)}) custom-call(s32[5]{0:T(128)S(1)} %get-tuple-element.137.scal_ref, s32[32]{0:T(128)} %copy-done.20, s32[8,128]{1,0:T(8,128)S(1)} %get-tuple-element.139.plan_ref, s32[8,128]{1,0:T(8,128)S(1)} %get-tuple-element.140.in_ref.out_pat_ref, ...), custom_call_target="tpu_custom_call" | custom-call | flops 402653184 | bytes 6291456 | tf_op jit(solution)/shard_map/cond/branch_0_fun/pallas_call | solution.py:363
  138.6 1.3 collective-permute-start.22
  139.9 3.4 %collective-permute-start.23 = (f32[4,128]{1,0:T(4,128)S(1)}, f32[4,128]{1,0:T(4,128)S(1)}, u32[]{:S(2)}, u32[]{:S(2)}) collective-permute-start(f32[4,128]{1,0:T(4,128)S(1)} %get-tuple-element.181.rest_0_), channel_id=1, source_target_pairs={{0,64},{32,96},{64,0},{96,32},{1,65},{33,97},{65,1},{97,33},{2,66}... | collective-permute-start | bytes 6152 | tf_op jit(solution)/shard_map/ppermute | solution.py:27
  143.3 1.4 collective-permute-start.24
  145.0 1.9 %collective-permute-done.24.rest_3_ = f32[4,128]{1,0:T(4,128)S(1)} collective-permute-done((f32[4,128]{1,0:T(4,128)S(1)}, f32[4,128]{1,0:T(4,128)S(1)}, u32[]{:S(2)}, u32[]{:S(2)}) %collective-permute-start.24) | collective-permute-done | bytes 2080 | tf_op jit(solution)/shard_map/ppermute | solution.py:27
  147.5 1.9 %shard_map.53 = f32[4,2,128,128]{3,2,1,0:T(8,128)} custom-call(f32[4,2,128,128]{3,2,1,0:T(8,128)} %get-tuple-element.180.x_ref, f32[4,128]{1,0:T(4,128)S(1)} %get-tuple-element.181.rest_0_, f32[4,128]{1,0:T(4,128)} %copy-done.21, f32[4,128]{1,0:T(4,128)} %copy-done.22, f32[4,128]{1,0:T(4,128)} %copy-done.23), custom_call_target="tpu_custom_call" | custom-call | flops 131072 | bytes 1048576 | tf_op jit(solution)/shard_map/pallas_call | solution.py:391
  (74 shorter events, 8.8 us)
Async XLA Ops:
  0.0 17.6 %copy-start = (f32[4,2,128,128]{3,2,1,0:T(8,128)S(1)}, f32[4,2,128,128]{3,2,1,0:T(8,128)}, u32[]{:S(2)}) copy-start(f32[4,2,128,128]{3,2,1,0:T(8,128)} %x_ref.3) | copy-start | bytes 1572868
  0.0 15.8 %collective-permute-start.10 = (f32[4,2,128,128]{3,2,1,0:T(8,128)}, f32[4,2,128,128]{3,2,1,0:T(8,128)S(1)}, u32[]{:S(2)}, u32[]{:S(2)}) collective-permute-start(f32[4,2,128,128]{3,2,1,0:T(8,128)} %x_ref.3), channel_id=1, source_target_pairs={{1,0},{2,1},{3,2},{4,3},{5,4},{6,5},{7,6},{8,7},{9,8},{10,9},{11,1... | collective-permute-start | bytes 1572872 | tf_op jit(solution)/shard_map/ppermute | solution.py:454
  1.4 14.4 %collective-permute-start.9 = (f32[4,2,128,128]{3,2,1,0:T(8,128)}, f32[4,2,128,128]{3,2,1,0:T(8,128)S(1)}, u32[]{:S(2)}, u32[]{:S(2)}) collective-permute-start(f32[4,2,128,128]{3,2,1,0:T(8,128)} %x_ref.3), channel_id=1, source_target_pairs={{0,1},{1,2},{2,3},{3,4},{4,5},{5,6},{6,7},{7,8},{8,9},{9,10},{10,1... | collective-permute-start | bytes 1572872 | tf_op jit(solution)/shard_map/ppermute | solution.py:453
  5.6 11.4 %collective-permute-start.6 = (f32[4,128]{1,0:T(4,128)S(1)}, f32[4,128]{1,0:T(4,128)S(1)}, u32[]{:S(2)}, u32[]{:S(2)}) collective-permute-start(f32[4,128]{1,0:T(4,128)S(1)} %shard_map.50.rest_0_), channel_id=1, source_target_pairs={{0,32},{32,64},{64,96},{96,0},{1,33},{33,65},{65,97},{97,1},{2,34}... | collective-permute-start | bytes 6152 | tf_op jit(solution)/shard_map/ppermute | solution.py:27
  7.3 9.8 %collective-permute-start.7 = (f32[4,128]{1,0:T(4,128)S(1)}, f32[4,128]{1,0:T(4,128)S(1)}, u32[]{:S(2)}, u32[]{:S(2)}) collective-permute-start(f32[4,128]{1,0:T(4,128)S(1)} %shard_map.50.rest_0_), channel_id=1, source_target_pairs={{0,64},{32,96},{64,0},{96,32},{1,65},{33,97},{65,1},{97,33},{2,66}... | collective-permute-start | bytes 6152 | tf_op jit(solution)/shard_map/ppermute | solution.py:27
  10.0 7.0 %collective-permute-start.8 = (f32[4,128]{1,0:T(4,128)S(1)}, f32[4,128]{1,0:T(4,128)S(1)}, u32[]{:S(2)}, u32[]{:S(2)}) collective-permute-start(f32[4,128]{1,0:T(4,128)S(1)} %shard_map.50.rest_0_), channel_id=1, source_target_pairs={{0,96},{32,0},{64,32},{96,64},{1,97},{33,1},{65,33},{97,65},{2,98}... | collective-permute-start | bytes 6152 | tf_op jit(solution)/shard_map/ppermute | solution.py:27
  19.6 30.3 %copy-start.8 = (s32[128,8]{0,1:T(8,128)S(1)}, s32[128,8]{0,1:T(8,128)}, u32[]{:S(2)}) copy-start(s32[128,8]{0,1:T(8,128)} %param.10) | copy-start | bytes 12292
  19.6 30.3 %copy-start.14 = (s32[128,8]{0,1:T(8,128)S(1)}, s32[128,8]{0,1:T(8,128)}, u32[]{:S(2)}) copy-start(s32[128,8]{0,1:T(8,128)} %param.9) | copy-start | bytes 12292
  19.6 30.3 %copy-start.17 = (s32[32]{0:T(128)S(1)}, s32[32]{0:T(128)}, u32[]{:S(2)}) copy-start(s32[32]{0:T(128)} %param.11) | copy-start | bytes 388
  19.6 40.1 %all-to-all-start.2 = ((f32[32,128,128]{2,1,0:T(8,128)}), f32[32,128,128]{2,1,0:T(8,128)S(1)}, u32[]{:S(2)}, u32[]{:S(2)}) async-start(f32[32,128,128]{2,1,0:T(8,128)} %shard_map.51), calls=%async_computation.2 | async-start | bytes 4194304 | tf_op jit(solution)/shard_map/all_to_all | solution.py:413
  29.6 15.4 %collective-permute-start.12 = (f32[4,2,128,128]{3,2,1,0:T(8,128)S(1)}, f32[4,2,128,128]{3,2,1,0:T(8,128)S(1)}, u32[]{:S(2)}, u32[]{:S(2)}) collective-permute-start(f32[4,2,128,128]{3,2,1,0:T(8,128)S(1)} %select_select_fusion), channel_id=1, source_target_pairs={{0,32},{32,64},{64,96},{96,0},{1,33},{33,65},{65,97},{97,1},{2,34}... | collective-permute-start | bytes 1572872 | tf_op jit(solution)/shard_map/ppermute | solution.py:402
  30.3 15.5 %collective-permute-start.11 = (f32[4,2,128,128]{3,2,1,0:T(8,128)S(1)}, f32[4,2,128,128]{3,2,1,0:T(8,128)S(1)}, u32[]{:S(2)}, u32[]{:S(2)}) collective-permute-start(f32[4,2,128,128]{3,2,1,0:T(8,128)S(1)} %select_select_fusion), channel_id=1, source_target_pairs={{0,96},{32,0},{64,32},{96,64},{1,97},{33,1},{65,33},{97,65},{2,98}... | collective-permute-start | bytes 1572872 | tf_op jit(solution)/shard_map/ppermute | solution.py:403
  45.0 0.9 copy-start.3
  45.8 9.1 %collective-permute-start.13 = (f32[2,2,128,128]{3,2,1,0:T(8,128)}, f32[2,2,128,128]{3,2,1,0:T(8,128)S(1)}, u32[]{:S(2)}, u32[]{:S(2)}) collective-permute-start(f32[2,2,128,128]{3,2,1,0:T(8,128)} %slice.24), channel_id=1, source_target_pairs={{0,32},{32,64},{64,96},{96,0},{1,33},{33,65},{65,97},{97,1},{2,34}... | collective-permute-start | bytes 786440 | tf_op jit(solution)/shard_map/ppermute | solution.py:404
  45.9 0.9 copy-start.7
  46.8 8.3 %collective-permute-start.14 = (f32[2,2,128,128]{3,2,1,0:T(8,128)}, f32[2,2,128,128]{3,2,1,0:T(8,128)}, u32[]{:S(2)}, u32[]{:S(2)}) collective-permute-start(f32[2,2,128,128]{3,2,1,0:T(8,128)} %slice.25), channel_id=1, source_target_pairs={{0,96},{32,0},{64,32},{96,64},{1,97},{33,1},{65,33},{97,65},{2,98}... | collective-permute-start | bytes 786440 | tf_op jit(solution)/shard_map/ppermute | solution.py:405
  59.7 1.6 %copy-start.15 = (s32[8,128]{1,0:T(8,128)}, s32[8,128]{1,0:T(8,128)S(1)}, u32[]{:S(2)}) copy-start(s32[8,128]{1,0:T(8,128)S(1)} %get-tuple-element.110.in_ref) | copy-start | bytes 12292 | tf_op jit(solution)/shard_map/cond
  59.7 1.6 %copy-start.19 = (s32[32]{0:T(128)}, s32[32]{0:T(128)S(1)}, u32[]{:S(2)}) copy-start(s32[32]{0:T(128)S(1)} %get-tuple-element.108.order_ref) | copy-start | bytes 388 | tf_op jit(solution)/shard_map/cond
  59.7 9.0 %copy-start.1 = (f32[4,2,128,128]{3,2,1,0:T(8,128)}, f32[4,2,128,128]{3,2,1,0:T(8,128)S(1)}, u32[]{:S(2)}) copy-start(f32[4,2,128,128]{3,2,1,0:T(8,128)S(1)} %get-tuple-element.112.own_ref) | copy-start | bytes 1572868 | tf_op jit(solution)/shard_map/cond
  59.7 9.6 %copy-start.4 = (f32[4,2,128,128]{3,2,1,0:T(8,128)S(1)}, f32[4,2,128,128]{3,2,1,0:T(8,128)}, u32[]{:S(2)}) copy-start(f32[4,2,128,128]{3,2,1,0:T(8,128)} %get-tuple-element.114.behind_ref) | copy-start | bytes 1572868 | tf_op jit(solution)/shard_map/cond
  61.3 6.5 %collective-permute-start = (f32[128,128]{1,0:T(8,128)}, f32[128,128]{1,0:T(8,128)S(1)}, u32[]{:S(2)}, u32[]{:S(2)}) collective-permute-start(f32[128,128]{1,0:T(8,128)} %get-tuple-element.118), channel_id=1, source_target_pairs={{0,8},{1,9},{2,10},{3,11},{4,12},{5,13},{6,14},{7,15},{8,16},{9,17... | collective-permute-start | bytes 196616 | tf_op jit(solution)/shard_map/cond/branch_0_fun/ppermute | solution.py:423
  61.4 6.4 %collective-permute-start.1 = (f32[128,128]{1,0:T(8,128)}, f32[128,128]{1,0:T(8,128)S(1)}, u32[]{:S(2)}, u32[]{:S(2)}) collective-permute-start(f32[128,128]{1,0:T(8,128)} %get-tuple-element.119), channel_id=1, source_target_pairs={{0,16},{1,17},{2,18},{3,19},{4,20},{5,21},{6,22},{7,23},{8,24},{9,... | collective-permute-start | bytes 196616 | tf_op jit(solution)/shard_map/cond/branch_0_fun/ppermute | solution.py:423
  62.9 5.7 %collective-permute-start.2 = (f32[128,128]{1,0:T(8,128)}, f32[128,128]{1,0:T(8,128)S(1)}, u32[]{:S(2)}, u32[]{:S(2)}) collective-permute-start(f32[128,128]{1,0:T(8,128)} %get-tuple-element.120), channel_id=1, source_target_pairs={{0,24},{1,25},{2,26},{3,27},{4,28},{5,29},{6,30},{7,31},{8,0},{9,1... | collective-permute-start | bytes 196616 | tf_op jit(solution)/shard_map/cond/branch_0_fun/ppermute | solution.py:423
  67.8 1.5 %copy-start.9 = (f32[128,128]{1,0:T(8,128)}, f32[128,128]{1,0:T(8,128)S(1)}, u32[]{:S(2)}) copy-start(f32[128,128]{1,0:T(8,128)S(1)} %collective-permute-done.rest_0_) | copy-start | bytes 196612 | tf_op jit(solution)/shard_map/cond
  67.8 1.5 copy-start.11
  68.7 0.6 copy-start.13
  76.9 6.1 %collective-permute-start.15 = (f32[4,128]{1,0:T(4,128)}, f32[4,128]{1,0:T(4,128)S(1)}, u32[]{:S(2)}, u32[]{:S(2)}) collective-permute-start(f32[4,128]{1,0:T(4,128)} %get-tuple-element.179.rest_0_), channel_id=1, source_target_pairs={{0,32},{32,64},{64,96},{96,0},{1,33},{33,65},{65,97},{97,1},{2,34}... | collective-permute-start | bytes 6152 | tf_op jit(solution)/shard_map/ppermute | solution.py:27
  78.4 5.3 %collective-permute-start.16 = (f32[4,128]{1,0:T(4,128)}, f32[4,128]{1,0:T(4,128)S(1)}, u32[]{:S(2)}, u32[]{:S(2)}) collective-permute-start(f32[4,128]{1,0:T(4,128)} %get-tuple-element.179.rest_0_), channel_id=1, source_target_pairs={{0,64},{32,96},{64,0},{96,32},{1,65},{33,97},{65,1},{97,33},{2,66}... | collective-permute-start | bytes 6152 | tf_op jit(solution)/shard_map/ppermute | solution.py:27
  78.9 4.8 %collective-permute-start.17 = (f32[4,128]{1,0:T(4,128)}, f32[4,128]{1,0:T(4,128)S(1)}, u32[]{:S(2)}, u32[]{:S(2)}) collective-permute-start(f32[4,128]{1,0:T(4,128)} %get-tuple-element.179.rest_0_), channel_id=1, source_target_pairs={{0,96},{32,0},{64,32},{96,64},{1,97},{33,1},{65,33},{97,65},{2,98}... | collective-permute-start | bytes 6152 | tf_op jit(solution)/shard_map/ppermute | solution.py:27
  86.0 26.9 %copy-start.18 = (s32[32]{0:T(128)S(1)}, s32[32]{0:T(128)}, u32[]{:S(2)}) copy-start(s32[32]{0:T(128)} %param.11) | copy-start | bytes 388
  86.0 36.1 %all-to-all-start.3 = ((f32[32,128,128]{2,1,0:T(8,128)}), f32[32,128,128]{2,1,0:T(8,128)S(1)}, u32[]{:S(2)}, u32[]{:S(2)}) async-start(f32[32,128,128]{2,1,0:T(8,128)} %shard_map.52), calls=%async_computation.3 | async-start | bytes 4194304 | tf_op jit(solution)/shard_map/all_to_all | solution.py:413
  92.0 15.4 %collective-permute-start.19 = (f32[4,2,128,128]{3,2,1,0:T(8,128)S(1)}, f32[4,2,128,128]{3,2,1,0:T(8,128)S(1)}, u32[]{:S(2)}, u32[]{:S(2)}) collective-permute-start(f32[4,2,128,128]{3,2,1,0:T(8,128)S(1)} %get-tuple-element.178.x_ref), channel_id=1, source_target_pairs={{0,32},{32,64},{64,96},{96,0},{1,33},{33,65},{65,97},{97,1},{2,34}... | collective-permute-start | bytes 1572872 | tf_op jit(solution)/shard_map/ppermute | solution.py:402
  92.2 15.9 %collective-permute-start.18 = (f32[4,2,128,128]{3,2,1,0:T(8,128)S(1)}, f32[4,2,128,128]{3,2,1,0:T(8,128)S(1)}, u32[]{:S(2)}, u32[]{:S(2)}) collective-permute-start(f32[4,2,128,128]{3,2,1,0:T(8,128)S(1)} %get-tuple-element.178.x_ref), channel_id=1, source_target_pairs={{0,96},{32,0},{64,32},{96,64},{1,97},{33,1},{65,33},{97,65},{2,98}... | collective-permute-start | bytes 1572872 | tf_op jit(solution)/shard_map/ppermute | solution.py:403
  108.1 9.4 %collective-permute-start.20 = (f32[2,2,128,128]{3,2,1,0:T(8,128)}, f32[2,2,128,128]{3,2,1,0:T(8,128)S(1)}, u32[]{:S(2)}, u32[]{:S(2)}) collective-permute-start(f32[2,2,128,128]{3,2,1,0:T(8,128)} %slice.26), channel_id=1, source_target_pairs={{0,32},{32,64},{64,96},{96,0},{1,33},{33,65},{65,97},{97,1},{2,34}... | collective-permute-start | bytes 786440 | tf_op jit(solution)/shard_map/ppermute | solution.py:404
  108.1 0.8 copy-start.6
  109.7 8.4 %collective-permute-start.21 = (f32[2,2,128,128]{3,2,1,0:T(8,128)}, f32[2,2,128,128]{3,2,1,0:T(8,128)}, u32[]{:S(2)}, u32[]{:S(2)}) collective-permute-start(f32[2,2,128,128]{3,2,1,0:T(8,128)} %slice.27), channel_id=1, source_target_pairs={{0,96},{32,0},{64,32},{96,64},{1,97},{33,1},{65,33},{97,65},{2,98}... | collective-permute-start | bytes 786440 | tf_op jit(solution)/shard_map/ppermute | solution.py:405
  122.1 1.6 %copy-start.20 = (s32[32]{0:T(128)}, s32[32]{0:T(128)S(1)}, u32[]{:S(2)}) copy-start(s32[32]{0:T(128)S(1)} %get-tuple-element.138.order_ref) | copy-start | bytes 388 | tf_op jit(solution)/shard_map/cond
  123.7 6.5 %collective-permute-start.3 = (f32[128,128]{1,0:T(8,128)}, f32[128,128]{1,0:T(8,128)S(1)}, u32[]{:S(2)}, u32[]{:S(2)}) collective-permute-start(f32[128,128]{1,0:T(8,128)} %get-tuple-element.147), channel_id=1, source_target_pairs={{0,8},{1,9},{2,10},{3,11},{4,12},{5,13},{6,14},{7,15},{8,16},{9,17... | collective-permute-start | bytes 196616 | tf_op jit(solution)/shard_map/cond/branch_0_fun/ppermute | solution.py:423
  123.8 6.4 %collective-permute-start.4 = (f32[128,128]{1,0:T(8,128)}, f32[128,128]{1,0:T(8,128)S(1)}, u32[]{:S(2)}, u32[]{:S(2)}) collective-permute-start(f32[128,128]{1,0:T(8,128)} %get-tuple-element.148), channel_id=1, source_target_pairs={{0,16},{1,17},{2,18},{3,19},{4,20},{5,21},{6,22},{7,23},{8,24},{9,... | collective-permute-start | bytes 196616 | tf_op jit(solution)/shard_map/cond/branch_0_fun/ppermute | solution.py:423
  125.3 5.8 %collective-permute-start.5 = (f32[128,128]{1,0:T(8,128)}, f32[128,128]{1,0:T(8,128)}, u32[]{:S(2)}, u32[]{:S(2)}) collective-permute-start(f32[128,128]{1,0:T(8,128)} %get-tuple-element.149), channel_id=1, source_target_pairs={{0,24},{1,25},{2,26},{3,27},{4,28},{5,29},{6,30},{7,31},{8,0},{9,1... | collective-permute-start | bytes 196616 | tf_op jit(solution)/shard_map/cond/branch_0_fun/ppermute | solution.py:423
  130.2 1.0 copy-start.10
  130.2 1.0 copy-start.12
  138.6 6.2 %collective-permute-start.22 = (f32[4,128]{1,0:T(4,128)S(1)}, f32[4,128]{1,0:T(4,128)S(1)}, u32[]{:S(2)}, u32[]{:S(2)}) collective-permute-start(f32[4,128]{1,0:T(4,128)S(1)} %get-tuple-element.181.rest_0_), channel_id=1, source_target_pairs={{0,32},{32,64},{64,96},{96,0},{1,33},{33,65},{65,97},{97,1},{2,34}... | collective-permute-start | bytes 6152 | tf_op jit(solution)/shard_map/ppermute | solution.py:27
  139.9 5.1 %collective-permute-start.23 = (f32[4,128]{1,0:T(4,128)S(1)}, f32[4,128]{1,0:T(4,128)S(1)}, u32[]{:S(2)}, u32[]{:S(2)}) collective-permute-start(f32[4,128]{1,0:T(4,128)S(1)} %get-tuple-element.181.rest_0_), channel_id=1, source_target_pairs={{0,64},{32,96},{64,0},{96,32},{1,65},{33,97},{65,1},{97,33},{2,66}... | collective-permute-start | bytes 6152 | tf_op jit(solution)/shard_map/ppermute | solution.py:27
  143.3 3.6 %collective-permute-start.24 = (f32[4,128]{1,0:T(4,128)S(1)}, f32[4,128]{1,0:T(4,128)S(1)}, u32[]{:S(2)}, u32[]{:S(2)}) collective-permute-start(f32[4,128]{1,0:T(4,128)S(1)} %get-tuple-element.181.rest_0_), channel_id=1, source_target_pairs={{0,96},{32,0},{64,32},{96,64},{1,97},{33,1},{65,33},{97,65},{2,98}... | collective-permute-start | bytes 6152 | tf_op jit(solution)/shard_map/ppermute | solution.py:27
  144.8 2.1 %copy-start.21 = (f32[4,128]{1,0:T(4,128)}, f32[4,128]{1,0:T(4,128)S(1)}, u32[]{:S(2)}) copy-start(f32[4,128]{1,0:T(4,128)S(1)} %collective-permute-done.22.rest_1_) | copy-start | bytes 6148
  145.0 1.9 %copy-start.22 = (f32[4,128]{1,0:T(4,128)}, f32[4,128]{1,0:T(4,128)S(1)}, u32[]{:S(2)}) copy-start(f32[4,128]{1,0:T(4,128)S(1)} %collective-permute-done.23.rest_2_) | copy-start | bytes 6148
  146.9 0.6 copy-start.23
  (1 other events, 0.6 us)
where the time goes:
time: 150 us; the launch traced here: 149 us
  starting transfers between devices  57.3 us (38%)
  waiting for transfers between devices  44.1 us (29%)
  Pallas kernels  34 us (23%)
  local copies, waits for them, and re-layouts  9.46 us (6%)
  between operations  2.71 us (2%)
    ppermute x2, waiting for transfers between devices, gather_rows(): behind = lax.ppermute(own, 'prow', ring(size, 1))  24.2 us
    ppermute x9, starting transfers between devices, row_sums(): sums.append(lax.ppermute(partial_value, 'prow', ring(size, step)))  16.4 us
    all_to_all x2, starting transfers between devices, expand(): got = lax.all_to_all(send, 'pcol', 0, 0, tiled=True)  16 us
    pallas_call x2, Pallas kernels, multiply(): pl.pallas_call(functools.partial(product_kernel, permuted), out_shape=(ja...  14.5 us
    pallas_call x4, Pallas kernels, plan(): pl.pallas_call(functools.partial(plan_kernel, permuted, whole), out_shape...  9.13 us
    all_to_all x2, waiting for transfers between devices, expand(): got = lax.all_to_all(send, 'pcol', 0, 0, tiled=True)  8.62 us
    ppermute x6, starting transfers between devices, by_level(): lax.ppermute(tile, 'pcol', ring(panels, (step + 1) * depth))  7.41 us
    ppermute x6, waiting for transfers between devices, by_level(): lax.ppermute(tile, 'pcol', ring(panels, (step + 1) * depth))  7.3 us
  transfers between devices with their start and end apart: 27, of which 14 were waited for; matrix products, arithmetic and copies ran while one was open for 5% of the time, Pallas kernels for 7%

commit v1 on v0

--- a/solution.py
+++ b/solution.py
@@ -13,7 +13,7 @@
 ANY = pl.BlockSpec(memory_space=pl.ANY)
 
 LANES = 128
-SEND, FIRST, HOP, SECOND, _ = range(5)
+SEND, FIRST, HOP, SECOND, MISFIT = range(5)
 TILE_BIT, SENT_BIT = 4, 8
 
 
@@ -29,7 +29,7 @@
 
 
 def plan_kernel(
-    permuted, whole, scal_ref, order_ref, in_ref, out_ref, plan_ref, grid_ref, line_ref
+    permuted, steps, whole, scal_ref, order_ref, in_ref, out_ref, plan_ref, grid_ref, line_ref
 ):
     place, row, _, _, depth = (scal_ref[i] for i in range(5))
     share = in_ref.shape[0] // 4
@@ -91,7 +91,7 @@
         away = jnp.logical_and(both, jnp.logical_not(same_level)).astype(jnp.float32)
         return found, column, both, away, product(away, spread)
 
-    if whole:
+    def fits():
         misfit = jnp.zeros(shape, jnp.float32)
         for block in range(4):
             found, _, both, away, riding = analyse(block)
@@ -105,7 +105,12 @@
             arriving = product(same_level.astype(jnp.float32), away)
             misfit += jnp.where(jnp.logical_and(valid, arriving > 1.5), 1.0, 0.0)
         total = jnp.sum(jnp.sum(misfit, axis=0, keepdims=True), axis=1, keepdims=True)
-        plan_ref[...] = jnp.broadcast_to((total > 0.5).astype(jnp.int32), plan_ref.shape)
+        line = jnp.broadcast_to((total > 0.5).astype(jnp.int32), (1, LANES))
+        plan_ref[pl.ds(MISFIT, 1), :] = line
+
+    if whole:
+        fits()
+    if steps is False:
         return
 
     found, column, both, away, riding = analyse(row)
@@ -131,20 +136,30 @@
     plan_ref[pl.ds(SECOND, 1), :] = grid_ref[1, pl.ds(place, 1), :].astype(jnp.int32)
 
 
-def plan(permuted, whole, scal, order_line, in_pattern, out_pattern):
-    return pl.pallas_call(
-        functools.partial(plan_kernel, permuted, whole),
-        out_shape=jax.ShapeDtypeStruct((8, LANES), jnp.int32),
+def plans_kernel(parts, scal_ref, order_ref, first_ref, second_ref, *rest):
+    *plan_refs, grid_ref, line_ref = rest
+    for (permuted, steps, whole), plan_ref in zip(parts, plan_refs):
+        plan_kernel(
+            permuted, steps, whole, scal_ref, order_ref,
+            second_ref if permuted else first_ref, second_ref, plan_ref, grid_ref, line_ref,
+        )
+
+
+def plans(parts, scal, order_line, first_rows, second_rows):
+    work = sum((1 if steps else 0) + (4 if whole else 0) for _, steps, whole in parts)
+    return pl.pallas_call(
+        functools.partial(plans_kernel, parts),
+        out_shape=(jax.ShapeDtypeStruct((8, LANES), jnp.int32),) * len(parts),
         in_specs=[SMEM, VMEM, VMEM, VMEM],
-        out_specs=VMEM,
+        out_specs=(VMEM,) * len(parts),
         scratch_shapes=[
             pltpu.VMEM((2, LANES, LANES), jnp.float32),
             pltpu.VMEM((8, LANES), jnp.int32),
         ],
         cost_estimate=pl.CostEstimate(
-            flops=(4 if whole else 1) << 23, bytes_accessed=1 << 14, transcendentals=0
+            flops=work << 23, bytes_accessed=1 << 14, transcendentals=0
         ),
-    )(scal, order_line, in_pattern, out_pattern)
+    )(scal, order_line, first_rows, second_rows)
 
 
 def column_kernel(x_ref, part_ref):
@@ -230,29 +245,37 @@
     return high, low
 
 
-def product_kernel(
+def dot_exactly(left, right):
+    left_high, left_low = split(left)
+    right_high, right_low = split(right)
+    dot = functools.partial(jnp.dot, preferred_element_type=jnp.float32)
+    return (dot(left_low, right_high) + dot(left_high, right_low)) + dot(left_high, right_high)
+
+
+FIRSTS, SECONDS, LIST = 2, 64, 128
+
+
+def own_kernel(
     permuted, scal_ref, order_ref, plan_ref, in_ref, out_pat_ref,
-    own_ref, ahead_ref, behind_ref, far_low_ref, far_high_ref, got_ref, *rest,
+    own_ref, ahead_ref, behind_ref, far_low_ref, far_high_ref,
+    base_ref, totals_ref, right_ref, list_ref,
 ):
-    *extra_refs, sq_ref, part_ref, left, totals, sems = rest
     cols, share, tile, _ = own_ref.shape
-    place, row, rows, depth = scal_ref[0], scal_ref[1], scal_ref[2], scal_ref[4]
+    place, row, depth = scal_ref[0], scal_ref[1], scal_ref[4]
+    rows = right_ref.shape[1] // share
     panel = order_ref[place]
+    home = panel // depth
     half = cols // 2
 
-    def far_of(j):
-        return far_low_ref[j] if j < half else far_high_ref[j - half]
-
+    for rel in range(4):
+        first = lax.rem(row + rel, rows) * share
+        for j in range(cols):
+            far = far_low_ref.at[j] if j < half else far_high_ref.at[j - half]
+            piece = (own_ref.at[j], ahead_ref.at[j], far, behind_ref.at[j])[rel]
+            right_ref[j, pl.ds(first, share)] = piece[...]
     for j in range(cols):
-        total = jnp.zeros((1, tile), jnp.float32)
-        for piece in (own_ref[j], ahead_ref[j], behind_ref[j], far_of(j)):
-            total += jnp.sum(piece.reshape(share * tile, tile), axis=0, keepdims=True)
-        totals[pl.ds(j, 1), :] = total
-
-    def named(j, rel, s):
-        block = lax.rem(row + rel, rows)
-        column = in_ref[block * share + s, panel * cols + j]
-        return column, column // cols == panel
+        whole = right_ref[j].reshape(rows * share * tile, tile)
+        totals_ref[pl.ds(j, 1), :] = jnp.sum(whole, axis=0, keepdims=True)
 
     def found(j, column, t):
         wanted = out_pat_ref[row * share + t, panel * cols + j]
@@ -264,119 +287,168 @@
             at = jnp.where(same, u, at)
         return hit, at
 
-    def target_of(j, rel, s, t):
-        return (
-            left.at[j, rel, pl.ds(t * tile, tile), pl.ds(s * tile, tile)],
-            sems.at[j, rel, s, t],
-        )
-
-    def start(j, rel, s, t, column, at):
+    def remote(place_of, counts):
+        j, k = place_of // (rows * share), lax.rem(place_of, rows * share)
+        column = in_ref[k, panel * cols + j]
         source = column // cols
         origin = order_ref[source] if permuted else source
-        extra = jnp.logical_and(at == 1, plan_ref[FIRST, origin] > 0)
-        target, sem = target_of(j, rel, s, t)
-
-        @pl.when(jnp.logical_not(extra))
-        def _():
-            pltpu.make_async_copy(got_ref.at[origin], target, sem).start()
-
-        if len(extra_refs) == 1:
+        firsts, seconds = counts
+        for t in range(share):
+            hit, at = found(j, column, t)
+            hit = jnp.logical_and(hit, source != panel)
+            extra = jnp.logical_and(hit, jnp.logical_and(at == 1, plan_ref[FIRST, origin] > 0))
+            simple = jnp.logical_and(hit, jnp.logical_not(extra))
+            entry = (place_of * share + t) * 32 + origin
+
+            @pl.when(simple)
+            def _():
+                list_ref[FIRSTS + firsts] = entry
 
             @pl.when(extra)
             def _():
-                pltpu.make_async_copy(extra_refs[0].at[origin], target, sem).start()
-
-        else:
-            step = lax.rem(place // depth - origin // depth + 4, 4)
-            for distance, ref in enumerate(extra_refs):
-
-                @pl.when(jnp.logical_and(extra, step == distance + 1))
-                def _():
-                    pltpu.make_async_copy(ref, target, sem).start()
+                list_ref[SECONDS + seconds] = entry
+
+            firsts = firsts + simple.astype(jnp.int32)
+            seconds = seconds + extra.astype(jnp.int32)
+        return firsts, seconds
+
+    firsts, seconds = lax.fori_loop(
+        0, cols * rows * share, remote, (jnp.int32(0), jnp.int32(0))
+    )
+    list_ref[0] = firsts
+    list_ref[1] = seconds
 
     @pl.loop(0, cols)
     def _(j):
-        for rel in range(4):
-            for s in range(share):
-                column, is_own = named(j, rel, s)
-                for t in range(share):
-                    hit, at = found(j, column, t)
-                    region = (j, rel, pl.ds(t * tile, tile), pl.ds(s * tile, tile))
-
-                    @pl.when(jnp.logical_and(hit, jnp.logical_not(is_own)))
-                    def _():
-                        start(j, rel, s, t, column, at)
-
-                    @pl.when(jnp.logical_and(hit, is_own))
-                    def _():
-                        local = lax.rem(column, cols)
-                        left[region] = own_ref[local, at] / totals[pl.ds(local, 1), :]
-
-                    @pl.when(jnp.logical_not(hit))
-                    def _():
-                        left[region] = jnp.zeros((tile, tile), jnp.float32)
-
-    def column(j, far):
-        sq_ref[j] = jnp.zeros((share, tile, tile), jnp.float32)
-        for rel in range(4):
-            any_hit = False
-            for s in range(share):
-                source, is_own = named(j, rel, s)
-                for t in range(share):
-                    hit, _ = found(j, source, t)
-                    any_hit = jnp.logical_or(any_hit, hit)
-
-                    @pl.when(jnp.logical_and(hit, jnp.logical_not(is_own)))
-                    def _():
-                        target, sem = target_of(j, rel, s, t)
-                        pltpu.make_async_copy(got_ref.at[0], target, sem).wait()
-
-            @pl.when(any_hit)
+        base_ref[j] = jnp.zeros((share, tile, tile), jnp.float32)
+        for s in range(share):
+            k = home * share + s
+            column = in_ref[k, panel * cols + j]
+            local = lax.rem(column, cols)
+            for t in range(share):
+                hit, at = found(j, column, t)
+
+                @pl.when(jnp.logical_and(hit, column // cols == panel))
+                def _():
+                    left = own_ref[local, at] / totals_ref[pl.ds(local, 1), :]
+                    base_ref[j, t] += dot_exactly(left, right_ref[j, k])
+
+
+def own_products(permuted, scal, order, steps, in_pattern, out_pattern, own, gathered):
+    cols, share, tile, _ = own.shape
+    return pl.pallas_call(
+        functools.partial(own_kernel, permuted),
+        out_shape=(
+            jax.ShapeDtypeStruct(own.shape, jnp.float32),
+            jax.ShapeDtypeStruct((cols, tile), jnp.float32),
+            jax.ShapeDtypeStruct((cols, 4 * share, tile, tile), jnp.float32),
+            jax.ShapeDtypeStruct((LIST,), jnp.int32),
+        ),
+        in_specs=[SMEM] * 5 + [VMEM] * 5,
+        out_specs=(VMEM, VMEM, VMEM, SMEM),
+        cost_estimate=pl.CostEstimate(flops=1 << 26, bytes_accessed=5 << 20, transcendentals=0),
+    )(scal, order, steps, in_pattern, out_pattern, own, *gathered)
+
+
+def add_listed(list_ref, number, first, right_ref, acc_ref, fetch, lefts, rights, sems):
+    share = acc_ref.shape[1]
+    names = right_ref.shape[1]
+    count = list_ref[number]
+
+    def where(i):
+        entry = list_ref[first + i]
+        spot = entry // 32
+        column_slot = spot // share
+        return (
+            column_slot // names, lax.rem(column_slot, names), lax.rem(spot, share),
+            lax.rem(entry, 32),
+        )
+
+    def right_copy(i, j, k):
+        return pltpu.make_async_copy(right_ref.at[j, k], rights.at[i], sems.at[1, i])
+
+    @pl.loop(0, count)
+    def _(i):
+        j, k, _, origin = where(i)
+        right_copy(i, j, k).start()
+        fetch(i, origin)
+
+    @pl.loop(0, count)
+    def _(i):
+        j, k, t, _ = where(i)
+        right_copy(i, j, k).wait()
+        pltpu.make_async_copy(right_ref.at[j, k], lefts.at[i], sems.at[0, i]).wait()
+        acc_ref[j, t] += dot_exactly(lefts[i], rights[i])
+
+
+def main_kernel(list_ref, base_ref, right_ref, got_ref, acc_ref, lefts, rights, sems):
+    acc_ref[...] = base_ref[...]
+
+    def fetch(i, origin):
+        pltpu.make_async_copy(got_ref.at[origin], lefts.at[i], sems.at[0, i]).start()
+
+    add_listed(list_ref, 0, FIRSTS, right_ref, acc_ref, fetch, lefts, rights, sems)
+
+
+def last_kernel(scal_ref, list_ref, acc_in_ref, totals_ref, right_ref, *rest):
+    *extra_refs, sq_ref, part_ref, lefts, rights, sems = rest
+    cols, share, tile, _ = acc_in_ref.shape
+    place, depth = scal_ref[0], scal_ref[4]
+    sq_ref[...] = acc_in_ref[...]
+
+    def fetch(i, origin):
+        if len(extra_refs) == 1:
+            pltpu.make_async_copy(extra_refs[0].at[origin], lefts.at[i], sems.at[0, i]).start()
+            return
+        step = lax.rem(place // depth - origin // depth + 4, 4)
+        for distance, ref in enumerate(extra_refs):
+
+            @pl.when(step == distance + 1)
             def _():
-                right = (own_ref.at[j], ahead_ref.at[j], far, behind_ref.at[j])[rel][...]
-                right_high, right_low = split(right.reshape(share * tile, tile))
-                left_high, left_low = split(left[j, rel])
-                dot = functools.partial(jnp.dot, preferred_element_type=jnp.float32)
-                added = (
-                    dot(left_low, right_high) + dot(left_high, right_low)
-                ) + dot(left_high, right_high)
-                sq_ref[j] += added.reshape(share, tile, tile)
-
-        value = sq_ref[j].reshape(share * tile, tile) / totals[pl.ds(j, 1), :]
+                pltpu.make_async_copy(ref, lefts.at[i], sems.at[0, i]).start()
+
+    add_listed(list_ref, 1, SECONDS, right_ref, sq_ref, fetch, lefts, rights, sems)
+    for j in range(cols):
+        value = sq_ref[j].reshape(share * tile, tile) / totals_ref[pl.ds(j, 1), :]
         square = value * value
         sq_ref[j] = square.reshape(share, tile, tile)
         part_ref[pl.ds(j, 1), :] = jnp.sum(square, axis=0, keepdims=True)
 
-    @pl.loop(0, half)
-    def _(j):
-        column(j, far_low_ref.at[j])
-
-    @pl.loop(half, cols)
-    def _(j):
-        column(j, far_high_ref.at[j - half])
-
-
-def multiply(permuted, scal, order, steps, in_pattern, out_pattern, own, gathered, got, extra):
-    cols, share, tile, _ = own.shape
-    depth = share * tile
-    place_of_extra = [ANY] if len(extra) == 1 else [VMEM] * len(extra)
-    return pl.pallas_call(
-        functools.partial(product_kernel, permuted),
+
+def list_scratch(right):
+    _, _, tile, _ = right.shape
+    most = SECONDS - FIRSTS - 2
+    return [
+        pltpu.VMEM((most, tile, tile), jnp.float32),
+        pltpu.VMEM((most, tile, tile), jnp.float32),
+        pltpu.SemaphoreType.DMA((2, most)),
+    ]
+
+
+def main_products(tiles, base, right, got):
+    return pl.pallas_call(
+        main_kernel,
+        out_shape=jax.ShapeDtypeStruct(base.shape, jnp.float32),
+        in_specs=[SMEM, VMEM, ANY, ANY],
+        out_specs=VMEM,
+        scratch_shapes=list_scratch(right),
+        cost_estimate=pl.CostEstimate(flops=1 << 30, bytes_accessed=3 << 20, transcendentals=0),
+    )(tiles, base, right, got)
+
+
+def last_products(scal, tiles, acc, totals, right, extra):
+    cols, _, tile, _ = acc.shape
+    return pl.pallas_call(
+        last_kernel,
         out_shape=(
-            jax.ShapeDtypeStruct(own.shape, jnp.float32),
+            jax.ShapeDtypeStruct(acc.shape, jnp.float32),
             jax.ShapeDtypeStruct((cols, tile), jnp.float32),
         ),
-        in_specs=[SMEM] * 5 + [VMEM] * 5 + [ANY] + place_of_extra,
+        in_specs=[SMEM, SMEM, VMEM, VMEM, ANY] + [ANY] * len(extra),
         out_specs=(VMEM, VMEM),
-        scratch_shapes=[
-            pltpu.VMEM((cols, 4, depth, depth), jnp.float32),
-            pltpu.VMEM((cols, tile), jnp.float32),
-            pltpu.SemaphoreType.DMA((cols, 4, share, share)),
-        ],
-        cost_estimate=pl.CostEstimate(
-            flops=cols * 12 * depth * depth * tile, bytes_accessed=6 << 20, transcendentals=0
-        ),
-    )(scal, order, steps, in_pattern, out_pattern, own, *gathered, got, *extra)
+        scratch_shapes=list_scratch(right),
+        cost_estimate=pl.CostEstimate(flops=1 << 24, bytes_accessed=2 << 20, transcendentals=0),
+    )(scal, tiles, acc, totals, right, *extra)
 
 
 def divide_kernel(x_ref, *rest):
@@ -412,24 +484,26 @@
     send = prepare(SEND, steps, x, sums, panels)
     got = lax.all_to_all(send, "pcol", 0, 0, tiled=True)
     gathered = gather_rows(own, rows)
-    finish = functools.partial(
-        multiply, permuted, scal, order, steps, in_pattern, out_pattern, own, gathered, got
+    base, totals, right, tiles = own_products(
+        permuted, scal, order, steps, in_pattern, out_pattern, own, gathered
     )
 
     def by_level(_):
-        tiles = hop_tiles(scal, steps, got)
-        return finish(
-            tuple(
-                lax.ppermute(tile, "pcol", ring(panels, (step + 1) * depth))
-                for step, tile in enumerate(tiles)
-            )
+        hops = hop_tiles(scal, steps, got)
+        extra = tuple(
+            lax.ppermute(tile, "pcol", ring(panels, (step + 1) * depth))
+            for step, tile in enumerate(hops)
         )
+        acc = main_products(tiles, base, right, got)
+        return last_products(scal, tiles, acc, totals, right, extra)
 
     def by_second(_):
         more = prepare(SECOND, steps, x, sums, panels)
-        return finish((lax.all_to_all(more, "pcol", 0, 0, tiled=True),))
-
-    return lax.cond(misfit[0, 0] > 0, by_second, by_level, 0)
+        extra = (lax.all_to_all(more, "pcol", 0, 0, tiled=True),)
+        acc = main_products(tiles, base, right, got)
+        return last_products(scal, tiles, acc, totals, right, extra)
+
+    return lax.cond(misfit > 0, by_second, by_level, 0)
 
 
 def local(match_tiles, pattern, kept, panel_order):
@@ -446,7 +520,8 @@
     scal = jnp.stack(
         [place, row, jnp.int32(rows), jnp.int32(cols), jnp.int32(panels // 4)]
     )
-    first_plan = plan(False, False, scal, order_line, pattern_rows, kept_rows)
+    tables = (scal, order_line, pattern_rows, kept_rows)
+    (first_plan,) = plans(((False, True, False),), *tables)
 
     sums = row_sums(column_partial(match_tiles), rows)
     below = [(i, i + 1) for i in range(panels - 1)]
@@ -454,9 +529,8 @@
     from_above = lax.ppermute(match_tiles, "pcol", [(j, i) for i, j in below])
     own = jnp.where(panel == place, match_tiles, jnp.where(panel < place, from_below, from_above))
     sums, own = lax.optimization_barrier((sums, own))
-    first_misfit = plan(False, True, scal, order_line, pattern_rows, kept_rows)
-    second_plan = plan(True, False, scal, order_line, kept_rows, kept_rows)
-    second_misfit = plan(True, True, scal, order_line, kept_rows, kept_rows)
+    check, second_plan = plans(((False, False, True), (True, True, True)), *tables)
+    first_misfit, second_misfit = check[MISFIT, 0], second_plan[MISFIT, 0]
     square, part = expand(
         False, scal, order, first_plan, first_misfit, pattern_rows, kept_rows,
         match_tiles, sums, own, rows,

time: 150 us -> 148 us (0.987)
  Pallas kernels: 34 us -> 41.8 us
  waiting for transfers between devices: 44.1 us -> 36.9 us
  local copies, waits for them, and re-layouts: 9.46 us -> 6.6 us
    all_to_all x2, waiting for transfers between devices: 8.62 us -> 0.01 us  [expand(): got = lax.all_to_all(send, 'pcol', 0, 0, tiled=True)]
    pallas_call x6 -> x8, Pallas kernels: 23.6 us -> 31.7 us  [the longest x2 14.6 us: own_products(): pl.pallas_call(functools.partial(own_kernel, permuted), out_shape=(jax.Sh...]
    ppermute x6, waiting for transfers between devices: 7.3 us -> 0.02 us  [by_level(): lax.ppermute(tile, 'pcol', ring(panels, (step + 1) * depth))]
    ppermute x9, waiting for transfers between devices: 2.86 us -> 8.27 us  [row_sums(): sums.append(lax.ppermute(partial_value, 'prow', ring(size, step)))]
    ppermute x2, waiting for transfers between devices: 0.42 us -> 4.43 us  [gather_rows(): far_low = lax.ppermute(behind[:half], 'prow', ring(size, 1))]
    ppermute x9, starting transfers between devices: 16.4 us -> 14.5 us  [row_sums(): sums.append(lax.ppermute(partial_value, 'prow', ring(size, step)))]
  transfers between devices with their start and end apart: 27 -> 27, of which waited for: 14 -> 8; matrix products, arithmetic and copies ran while one was open for 5% -> 3% of each run, Pallas kernels for 7% -> 19%
where the time goes in v1:
time: 148 us; the launch traced here: 146 us
  starting transfers between devices  57 us (39%)
  Pallas kernels  41.8 us (28%)
  waiting for transfers between devices  36.9 us (25%)
  local copies, waits for them, and re-layouts  6.6 us (4%)
  between operations  2.83 us (2%)
    ppermute x2, waiting for transfers between devices, gather_rows(): behind = lax.ppermute(own, 'prow', ring(size, 1))  24.1 us
    all_to_all x2, starting transfers between devices, expand(): got = lax.all_to_all(send, 'pcol', 0, 0, tiled=True)  16 us
    pallas_call x2, Pallas kernels, own_products(): pl.pallas_call(functools.partial(own_kernel, permuted), out_shape=(jax.Sh...  14.6 us
    ppermute x9, starting transfers between devices, row_sums(): sums.append(lax.ppermute(partial_value, 'prow', ring(size, step)))  14.5 us
    ppermute x6, starting transfers between devices, by_level(): lax.ppermute(tile, 'pcol', ring(panels, (step + 1) * depth))  8.88 us
    ppermute x9, waiting for transfers between devices, row_sums(): sums.append(lax.ppermute(partial_value, 'prow', ring(size, step)))  8.27 us
    pallas_call x2, Pallas kernels, main_products(): pl.pallas_call(main_kernel, out_shape=jax.ShapeDtypeStruct(base.shape, jn...  7.14 us
    ppermute x2, starting transfers between devices, gather_rows(): far_high = lax.ppermute(ahead[half:], 'prow', ring(size, -1))  5.8 us
  transfers between devices with their start and end apart: 27, of which 8 were waited for; matrix products, arithmetic and copies ran while one was open for 3% of the time, Pallas kernels for 19%

profile of v1, /device:TPU:0, one launch (start us, length us, event | category | flops | bytes accessed | tf_op | source)
XLA Modules:
  0.0 146.5 jit_solution(6857012206017929023)
XLA Ops:
  0.0 1.4 collective-permute-start.10
  1.4 3.1 %collective-permute-start.9 = (f32[4,2,128,128]{3,2,1,0:T(8,128)}, f32[4,2,128,128]{3,2,1,0:T(8,128)S(1)}, u32[]{:S(2)}, u32[]{:S(2)}) collective-permute-start(f32[4,2,128,128]{3,2,1,0:T(8,128)} %x_ref.3), channel_id=1, source_target_pairs={{0,1},{1,2},{2,3},{3,4},{4,5},{5,6},{6,7},{7,8},{8,9},{9,10},{10,1... | collective-permute-start | bytes 1572872 | tf_op jit(solution)/shard_map/ppermute | solution.py:528
  4.5 1.1 shard_map.48.rest_0_
  5.6 2.9 %collective-permute-start.8 = (f32[4,128]{1,0:T(4,128)S(1)}, f32[4,128]{1,0:T(4,128)S(1)}, u32[]{:S(2)}, u32[]{:S(2)}) collective-permute-start(f32[4,128]{1,0:T(4,128)S(1)} %shard_map.48.rest_0_), channel_id=1, source_target_pairs={{0,96},{32,0},{64,32},{96,64},{1,97},{33,1},{65,33},{97,65},{2,98}... | collective-permute-start | bytes 6152 | tf_op jit(solution)/shard_map/ppermute | solution.py:27
  8.5 0.8 collective-permute-start.7
  9.3 0.9 collective-permute-start.6
  10.2 1.2 dynamic_slice.3
  12.8 1.8 %shard_map.47.plan_ref = s32[8,128]{1,0:T(8,128)S(1)} custom-call(s32[5]{0:T(128)S(1)} %pad_add_fusion.scal_ref, s32[1,32]{1,0:T(1,128)} %bitcast.16, s32[8,128]{1,0:T(8,128)} %bitcast.13, s32[8,128]{1,0:T(8,128)} %bitcast.8), custom_call_target="tpu_custom_call" | custom-call | flops 8388608 | bytes 16384 | tf_op jit(solution)/shard_map/pallas_call | solution.py:150
  14.7 1.1 select_select_fusion.own_ref
  15.8 2.0 %shard_map.50 = f32[32,128,128]{2,1,0:T(8,128)} custom-call(s32[8,128]{1,0:T(8,128)S(1)} %shard_map.47.plan_ref, f32[4,2,128,128]{3,2,1,0:T(8,128)S(1)} %copy-done, f32[4,128]{1,0:T(4,128)S(1)} %shard_map.48.rest_0_, f32[4,128]{1,0:T(4,128)S(1)} %collective-permute-done.6.rest_1_, f32[4,128]{1,0:T(4,128)S(1)} %collective-permute-done.7.rest_2_, ...), custom_call_target="tpu_custom_call" | custom-call | flops 131072 | bytes 3145728 | tf_op jit(solution)/shard_map/pallas_call | solution.py:203
  17.9 9.8 %all-to-all-start.2 = ((f32[32,128,128]{2,1,0:T(8,128)}), f32[32,128,128]{2,1,0:T(8,128)S(1)}, u32[]{:S(2)}, u32[]{:S(2)}) async-start(f32[32,128,128]{2,1,0:T(8,128)} %shard_map.50), calls=%async_computation.2 | async-start | bytes 4194304 | tf_op jit(solution)/shard_map/all_to_all | solution.py:485
  27.7 1.9 %collective-permute-start.12 = (f32[4,2,128,128]{3,2,1,0:T(8,128)S(1)}, f32[4,2,128,128]{3,2,1,0:T(8,128)S(1)}, u32[]{:S(2)}, u32[]{:S(2)}) collective-permute-start(f32[4,2,128,128]{3,2,1,0:T(8,128)S(1)} %select_select_fusion.own_ref), channel_id=1, source_target_pairs={{0,32},{32,64},{64,96},{96,0},{1,33},{33,65},{65,97},{97,1},{2,34}... | collective-permute-start | bytes 1572872 | tf_op jit(solution)/shard_map/ppermute | solution.py:474
  29.6 1.4 collective-permute-start.11
  31.0 12.1 %collective-permute-done.12.behind_ref = f32[4,2,128,128]{3,2,1,0:T(8,128)S(1)} collective-permute-done((f32[4,2,128,128]{3,2,1,0:T(8,128)S(1)}, f32[4,2,128,128]{3,2,1,0:T(8,128)S(1)}, u32[]{:S(2)}, u32[]{:S(2)}) %collective-permute-start.12) | collective-permute-done | bytes 524320 | tf_op jit(solution)/shard_map/ppermute | solution.py:474
  43.1 0.7 collective-permute-start.13
  43.9 0.8 copy-done.3
  44.7 2.5 %collective-permute-start.14 = (f32[2,2,128,128]{3,2,1,0:T(8,128)S(1)}, f32[2,2,128,128]{3,2,1,0:T(8,128)}, u32[]{:S(2)}, u32[]{:S(2)}) collective-permute-start(f32[2,2,128,128]{3,2,1,0:T(8,128)S(1)} %slice.25), channel_id=1, source_target_pairs={{0,96},{32,0},{64,32},{96,64},{1,97},{33,1},{65,33},{97,65},{2,98}... | collective-permute-start | bytes 786440 | tf_op jit(solution)/shard_map/ppermute | solution.py:477
  47.2 3.6 %shard_map.46 = (s32[8,128]{1,0:T(8,128)}, s32[8,128]{1,0:T(8,128)S(1)}) custom-call(s32[5]{0:T(128)S(1)} %pad_add_fusion.scal_ref, s32[1,32]{1,0:T(1,128)} %bitcast.17, s32[8,128]{1,0:T(8,128)} %bitcast.14, s32[8,128]{1,0:T(8,128)} %bitcast.9), custom_call_target="tpu_custom_call" | custom-call | flops 75497472 | bytes 16384 | tf_op jit(solution)/shard_map/pallas_call | solution.py:150
  50.9 1.3 slice.19
  52.9 7.4 %shard_map.49 = (f32[4,2,128,128]{3,2,1,0:T(8,128)S(1)}, f32[4,128]{1,0:T(4,128)S(1)}, f32[4,8,128,128]{3,2,1,0:T(8,128)}, s32[128]{0:T(128)S(1)}) custom-call(s32[5]{0:T(128)S(1)} %pad_add_fusion.scal_ref, s32[32]{0:T(128)} %order_ref.3, s32[8,128]{1,0:T(8,128)S(1)} %shard_map.47.plan_ref, s32[8,128]{1,0:T(8,128)} %bitcast.15, s32[8,128]{1,0:T(8,128)} %bitcast.10, ...), custom_call_target="tpu_custom_call" | custom-call | flops 67108864 | bytes 5242880 | tf_op jit(solution)/shard_map/pallas_call | solution.py:339
  60.3 12.8 %conditional.2 = ((f32[4,2,128,128]{3,2,1,0:T(8,128)S(1)}, f32[4,128]{1,0:T(4,128)S(1)})) conditional(s32[]{:T(128)} %bitcast.6, (s32[128]{0:T(128)S(1)}, f32[4,2,128,128]{3,2,1,0:T(8,128)S(1)}, f32[4,8,128,128]{3,2,1,0:T(8,128)}, f32[32,128,128]{2,1,0:T(8,128)S(1)}, s32[5]{0:T(128)S(1)}, /*index=5*/s32[8,128]{1,0:T(8,128)S(1)}, ...), branch_computations={%region_0.1_spmd, %region_1.2_spmd} | conditional | flops 1090650112 | bytes 14680104 | solution.py:506
  60.3 1.6 %branch_0_fun.7 = (f32[128,128]{1,0:T(8,128)}, f32[128,128]{1,0:T(8,128)}, f32[128,128]{1,0:T(8,128)}) custom-call(s32[5]{0:T(128)S(1)} %get-tuple-element.81.scal_ref, s32[8,128]{1,0:T(8,128)S(1)} %get-tuple-element.87.plan_ref, f32[32,128,128]{2,1,0:T(8,128)S(1)} %get-tuple-element.85.got_ref), custom_call_target="tpu_custom_call" | custom-call | bytes 393216 | tf_op jit(solution)/shard_map/cond/branch_0_fun/pallas_call | solution.py:232
  62.3 2.7 %collective-permute-start.1 = (f32[128,128]{1,0:T(8,128)}, f32[128,128]{1,0:T(8,128)S(1)}, u32[]{:S(2)}, u32[]{:S(2)}) collective-permute-start(f32[128,128]{1,0:T(8,128)} %get-tuple-element.89), channel_id=1, source_target_pairs={{0,16},{1,17},{2,18},{3,19},{4,20},{5,21},{6,22},{7,23},{8,24},{9,... | collective-permute-start | bytes 196616 | tf_op jit(solution)/shard_map/cond/branch_0_fun/ppermute | solution.py:494
  65.0 1.4 collective-permute-start.2
  66.4 3.7 %branch_0_fun.6.acc_in_ref = f32[4,2,128,128]{3,2,1,0:T(8,128)} custom-call(s32[128]{0:T(128)S(1)} %get-tuple-element.82.list_ref, f32[4,2,128,128]{3,2,1,0:T(8,128)S(1)} %get-tuple-element.83.base_ref, f32[4,8,128,128]{3,2,1,0:T(8,128)} %get-tuple-element.84.right_ref, f32[32,128,128]{2,1,0:T(8,128)S(1)} %get-tuple-element.85.got_ref), custom_call_target="tpu_custom_call" | custom-call | flops 1073741824 | bytes 3145728 | tf_op jit(solution)/shard_map/cond/branch_0_fun/pallas_call | solution.py:429
  70.8 2.3 %branch_0_fun.8 = (f32[4,2,128,128]{3,2,1,0:T(8,128)S(1)}, f32[4,128]{1,0:T(4,128)S(1)}) custom-call(s32[5]{0:T(128)S(1)} %get-tuple-element.81.scal_ref, s32[128]{0:T(128)S(1)} %get-tuple-element.82.list_ref, f32[4,2,128,128]{3,2,1,0:T(8,128)} %branch_0_fun.6.acc_in_ref, f32[4,128]{1,0:T(4,128)S(1)} %get-tuple-element.86.totals_ref, ...), custom_call_target="tpu_custom_call" | custom-call | flops 16777216 | bytes 2097152 | tf_op jit(solution)/shard_map/cond/branch_0_fun/pallas_call | solution.py:441
  73.0 3.6 %collective-permute-start.21 = (f32[4,128]{1,0:T(4,128)S(1)}, f32[4,128]{1,0:T(4,128)S(1)}, u32[]{:S(2)}, u32[]{:S(2)}) collective-permute-start(f32[4,128]{1,0:T(4,128)S(1)} %get-tuple-element.159.rest_0_), channel_id=1, source_target_pairs={{0,96},{32,0},{64,32},{96,64},{1,97},{33,1},{65,33},{97,65},{2,98}... | collective-permute-start | bytes 6152 | tf_op jit(solution)/shard_map/ppermute | solution.py:27
  77.1 0.7 collective-permute-start.19
  77.9 3.8 %collective-permute-done.20.rest_2_ = f32[4,128]{1,0:T(4,128)S(1)} collective-permute-done((f32[4,128]{1,0:T(4,128)S(1)}, f32[4,128]{1,0:T(4,128)S(1)}, u32[]{:S(2)}, u32[]{:S(2)}) %collective-permute-start.20) | collective-permute-done | bytes 2080 | tf_op jit(solution)/shard_map/ppermute | solution.py:27
  81.9 2.2 %shard_map.52 = f32[32,128,128]{2,1,0:T(8,128)} custom-call(s32[8,128]{1,0:T(8,128)S(1)} %get-tuple-element.144.plan_ref, f32[4,2,128,128]{3,2,1,0:T(8,128)S(1)} %get-tuple-element.155.own_ref.x_ref, f32[4,128]{1,0:T(4,128)S(1)} %get-tuple-element.159.rest_0_, f32[4,128]{1,0:T(4,128)S(1)} %collective-permute-done.19.rest_1_, ...), custom_call_target="tpu_custom_call" | custom-call | flops 131072 | bytes 3145728 | tf_op jit(solution)/shard_map/pallas_call | solution.py:203
  84.1 6.2 %all-to-all-start.3 = ((f32[32,128,128]{2,1,0:T(8,128)}), f32[32,128,128]{2,1,0:T(8,128)S(1)}, u32[]{:S(2)}, u32[]{:S(2)}) async-start(f32[32,128,128]{2,1,0:T(8,128)} %shard_map.52), calls=%async_computation.3 | async-start | bytes 4194304 | tf_op jit(solution)/shard_map/all_to_all | solution.py:485
  90.4 3.2 %collective-permute-start.15 = (f32[4,2,128,128]{3,2,1,0:T(8,128)S(1)}, f32[4,2,128,128]{3,2,1,0:T(8,128)S(1)}, u32[]{:S(2)}, u32[]{:S(2)}) collective-permute-start(f32[4,2,128,128]{3,2,1,0:T(8,128)S(1)} %get-tuple-element.155.own_ref.x_ref), channel_id=1, source_target_pairs={{0,96},{32,0},{64,32},{96,64},{1,97},{33,1},{65,33},{97,65},{2,98}... | collective-permute-start | bytes 1572872 | tf_op jit(solution)/shard_map/ppermute | solution.py:475
  93.6 12.1 %collective-permute-done.16.behind_ref = f32[4,2,128,128]{3,2,1,0:T(8,128)S(1)} collective-permute-done((f32[4,2,128,128]{3,2,1,0:T(8,128)S(1)}, f32[4,2,128,128]{3,2,1,0:T(8,128)S(1)}, u32[]{:S(2)}, u32[]{:S(2)}) %collective-permute-start.16) | collective-permute-done | bytes 524320 | tf_op jit(solution)/shard_map/ppermute | solution.py:474
  105.8 3.3 %collective-permute-start.18 = (f32[2,2,128,128]{3,2,1,0:T(8,128)S(1)}, f32[2,2,128,128]{3,2,1,0:T(8,128)}, u32[]{:S(2)}, u32[]{:S(2)}) collective-permute-start(f32[2,2,128,128]{3,2,1,0:T(8,128)S(1)} %slice.27), channel_id=1, source_target_pairs={{0,96},{32,0},{64,32},{96,64},{1,97},{33,1},{65,33},{97,65},{2,98}... | collective-permute-start | bytes 786440 | tf_op jit(solution)/shard_map/ppermute | solution.py:477
  110.2 4.4 %collective-permute-done.17.far_low_ref = f32[2,2,128,128]{3,2,1,0:T(8,128)S(1)} collective-permute-done((f32[2,2,128,128]{3,2,1,0:T(8,128)S(1)}, f32[2,2,128,128]{3,2,1,0:T(8,128)S(1)}, u32[]{:S(2)}, u32[]{:S(2)}) %collective-permute-start.17) | collective-permute-done | bytes 262176 | tf_op jit(solution)/shard_map/ppermute | solution.py:476
  114.6 0.7 copy-done.6
  115.3 7.3 %shard_map.51 = (f32[4,2,128,128]{3,2,1,0:T(8,128)S(1)}, f32[4,128]{1,0:T(4,128)S(1)}, f32[4,8,128,128]{3,2,1,0:T(8,128)}, s32[128]{0:T(128)S(1)}) custom-call(s32[5]{0:T(128)S(1)} %pad_add_fusion.scal_ref, s32[32]{0:T(128)} %order_ref.3, s32[8,128]{1,0:T(8,128)S(1)} %get-tuple-element.144.plan_ref, s32[8,128]{1,0:T(8,128)} %bitcast.11, s32[8,128]{1,0:T(8,128)} %bitcast.12, ...), custom_call_target="tpu_custom_call" | custom-call | flops 67108864 | bytes 5242880 | tf_op jit(solution)/shard_map/pallas_call | solution.py:339
  122.6 12.4 %conditional.3 = ((f32[4,2,128,128]{3,2,1,0:T(8,128)S(1)}, f32[4,128]{1,0:T(4,128)S(1)})) conditional(s32[]{:T(128)} %bitcast.5, (s32[128]{0:T(128)S(1)}, f32[4,2,128,128]{3,2,1,0:T(8,128)S(1)}, f32[4,8,128,128]{3,2,1,0:T(8,128)}, f32[32,128,128]{2,1,0:T(8,128)S(1)}, s32[5]{0:T(128)S(1)}, /*index=5*/s32[8,128]{1,0:T(8,128)S(1)}, ...), branch_computations={%region_2.3_spmd, %region_3.4_spmd} | conditional | flops 1090650112 | bytes 14680104 | solution.py:506
  122.6 1.6 %branch_0_fun.10 = (f32[128,128]{1,0:T(8,128)}, f32[128,128]{1,0:T(8,128)}, f32[128,128]{1,0:T(8,128)}) custom-call(s32[5]{0:T(128)S(1)} %get-tuple-element.103.scal_ref, s32[8,128]{1,0:T(8,128)S(1)} %get-tuple-element.109.plan_ref, f32[32,128,128]{2,1,0:T(8,128)S(1)} %get-tuple-element.107.got_ref), custom_call_target="tpu_custom_call" | custom-call | bytes 393216 | tf_op jit(solution)/shard_map/cond/branch_0_fun/pallas_call | solution.py:232
  124.5 2.7 %collective-permute-start.4 = (f32[128,128]{1,0:T(8,128)}, f32[128,128]{1,0:T(8,128)S(1)}, u32[]{:S(2)}, u32[]{:S(2)}) collective-permute-start(f32[128,128]{1,0:T(8,128)} %get-tuple-element.111), channel_id=1, source_target_pairs={{0,16},{1,17},{2,18},{3,19},{4,20},{5,21},{6,22},{7,23},{8,24},{9,... | collective-permute-start | bytes 196616 | tf_op jit(solution)/shard_map/cond/branch_0_fun/ppermute | solution.py:494
  127.2 1.4 collective-permute-start.5
  128.6 3.5 %branch_0_fun.9.acc_in_ref = f32[4,2,128,128]{3,2,1,0:T(8,128)} custom-call(s32[128]{0:T(128)S(1)} %get-tuple-element.104.list_ref, f32[4,2,128,128]{3,2,1,0:T(8,128)S(1)} %get-tuple-element.105.base_ref, f32[4,8,128,128]{3,2,1,0:T(8,128)} %get-tuple-element.106.right_ref, f32[32,128,128]{2,1,0:T(8,128)S(1)} %get-tuple-element.107.got_ref), custom_call_target="tpu_custom_call" | custom-call | flops 1073741824 | bytes 3145728 | tf_op jit(solution)/shard_map/cond/branch_0_fun/pallas_call | solution.py:429
  132.8 2.3 %branch_0_fun.11 = (f32[4,2,128,128]{3,2,1,0:T(8,128)S(1)}, f32[4,128]{1,0:T(4,128)S(1)}) custom-call(s32[5]{0:T(128)S(1)} %get-tuple-element.103.scal_ref, s32[128]{0:T(128)S(1)} %get-tuple-element.104.list_ref, f32[4,2,128,128]{3,2,1,0:T(8,128)} %branch_0_fun.9.acc_in_ref, f32[4,128]{1,0:T(4,128)S(1)} %get-tuple-element.108.totals_ref, ...), custom_call_target="tpu_custom_call" | custom-call | flops 16777216 | bytes 2097152 | tf_op jit(solution)/shard_map/cond/branch_0_fun/pallas_call | solution.py:441
  135.0 4.2 %collective-permute-start.24 = (f32[4,128]{1,0:T(4,128)S(1)}, f32[4,128]{1,0:T(4,128)S(1)}, u32[]{:S(2)}, u32[]{:S(2)}) collective-permute-start(f32[4,128]{1,0:T(4,128)S(1)} %get-tuple-element.162.rest_0_), channel_id=1, source_target_pairs={{0,96},{32,0},{64,32},{96,64},{1,97},{33,1},{65,33},{97,65},{2,98}... | collective-permute-start | bytes 6152 | tf_op jit(solution)/shard_map/ppermute | solution.py:27
  139.3 0.9 collective-permute-start.22
  140.6 3.8 %collective-permute-done.23.rest_2_ = f32[4,128]{1,0:T(4,128)S(1)} collective-permute-done((f32[4,128]{1,0:T(4,128)S(1)}, f32[4,128]{1,0:T(4,128)S(1)}, u32[]{:S(2)}, u32[]{:S(2)}) %collective-permute-start.23) | collective-permute-done | bytes 2080 | tf_op jit(solution)/shard_map/ppermute | solution.py:27
  144.4 0.6 copy-done.14
  144.9 1.5 %shard_map.53 = f32[4,2,128,128]{3,2,1,0:T(8,128)} custom-call(f32[4,2,128,128]{3,2,1,0:T(8,128)S(1)} %get-tuple-element.161.x_ref, f32[4,128]{1,0:T(4,128)S(1)} %get-tuple-element.162.rest_0_, f32[4,128]{1,0:T(4,128)} %copy-done.15, f32[4,128]{1,0:T(4,128)} %copy-done.14, f32[4,128]{1,0:T(4,128)} %copy-done.13), custom_call_target="tpu_custom_call" | custom-call | flops 131072 | bytes 1048576 | tf_op jit(solution)/shard_map/pallas_call | solution.py:463
  (64 shorter events, 4.1 us)
Async XLA Ops:
  0.0 15.8 %copy-start = (f32[4,2,128,128]{3,2,1,0:T(8,128)S(1)}, f32[4,2,128,128]{3,2,1,0:T(8,128)}, u32[]{:S(2)}) copy-start(f32[4,2,128,128]{3,2,1,0:T(8,128)} %x_ref.3) | copy-start | bytes 1572868
  0.0 14.6 %collective-permute-start.10 = (f32[4,2,128,128]{3,2,1,0:T(8,128)}, f32[4,2,128,128]{3,2,1,0:T(8,128)S(1)}, u32[]{:S(2)}, u32[]{:S(2)}) collective-permute-start(f32[4,2,128,128]{3,2,1,0:T(8,128)} %x_ref.3), channel_id=1, source_target_pairs={{1,0},{2,1},{3,2},{4,3},{5,4},{6,5},{7,6},{8,7},{9,8},{10,9},{11,1... | collective-permute-start | bytes 1572872 | tf_op jit(solution)/shard_map/ppermute | solution.py:529
  1.4 13.2 %collective-permute-start.9 = (f32[4,2,128,128]{3,2,1,0:T(8,128)}, f32[4,2,128,128]{3,2,1,0:T(8,128)S(1)}, u32[]{:S(2)}, u32[]{:S(2)}) collective-permute-start(f32[4,2,128,128]{3,2,1,0:T(8,128)} %x_ref.3), channel_id=1, source_target_pairs={{0,1},{1,2},{2,3},{3,4},{4,5},{5,6},{6,7},{7,8},{8,9},{9,10},{10,1... | collective-permute-start | bytes 1572872 | tf_op jit(solution)/shard_map/ppermute | solution.py:528
  5.6 10.2 %collective-permute-start.8 = (f32[4,128]{1,0:T(4,128)S(1)}, f32[4,128]{1,0:T(4,128)S(1)}, u32[]{:S(2)}, u32[]{:S(2)}) collective-permute-start(f32[4,128]{1,0:T(4,128)S(1)} %shard_map.48.rest_0_), channel_id=1, source_target_pairs={{0,96},{32,0},{64,32},{96,64},{1,97},{33,1},{65,33},{97,65},{2,98}... | collective-permute-start | bytes 6152 | tf_op jit(solution)/shard_map/ppermute | solution.py:27
  8.5 7.3 %collective-permute-start.7 = (f32[4,128]{1,0:T(4,128)S(1)}, f32[4,128]{1,0:T(4,128)S(1)}, u32[]{:S(2)}, u32[]{:S(2)}) collective-permute-start(f32[4,128]{1,0:T(4,128)S(1)} %shard_map.48.rest_0_), channel_id=1, source_target_pairs={{0,64},{32,96},{64,0},{96,32},{1,65},{33,97},{65,1},{97,33},{2,66}... | collective-permute-start | bytes 6152 | tf_op jit(solution)/shard_map/ppermute | solution.py:27
  9.3 6.5 %collective-permute-start.6 = (f32[4,128]{1,0:T(4,128)S(1)}, f32[4,128]{1,0:T(4,128)S(1)}, u32[]{:S(2)}, u32[]{:S(2)}) collective-permute-start(f32[4,128]{1,0:T(4,128)S(1)} %shard_map.48.rest_0_), channel_id=1, source_target_pairs={{0,32},{32,64},{64,96},{96,0},{1,33},{33,65},{65,97},{97,1},{2,34}... | collective-permute-start | bytes 6152 | tf_op jit(solution)/shard_map/ppermute | solution.py:27
  15.8 13.8 %copy-start.1 = (f32[4,2,128,128]{3,2,1,0:T(8,128)}, f32[4,2,128,128]{3,2,1,0:T(8,128)S(1)}, u32[]{:S(2)}) copy-start(f32[4,2,128,128]{3,2,1,0:T(8,128)S(1)} %select_select_fusion.own_ref) | copy-start | bytes 1572868
  17.9 42.4 %all-to-all-start.2 = ((f32[32,128,128]{2,1,0:T(8,128)}), f32[32,128,128]{2,1,0:T(8,128)S(1)}, u32[]{:S(2)}, u32[]{:S(2)}) async-start(f32[32,128,128]{2,1,0:T(8,128)} %shard_map.50), calls=%async_computation.2 | async-start | bytes 4194304 | tf_op jit(solution)/shard_map/all_to_all | solution.py:485
  27.7 15.4 %collective-permute-start.12 = (f32[4,2,128,128]{3,2,1,0:T(8,128)S(1)}, f32[4,2,128,128]{3,2,1,0:T(8,128)S(1)}, u32[]{:S(2)}, u32[]{:S(2)}) collective-permute-start(f32[4,2,128,128]{3,2,1,0:T(8,128)S(1)} %select_select_fusion.own_ref), channel_id=1, source_target_pairs={{0,32},{32,64},{64,96},{96,0},{1,33},{33,65},{65,97},{97,1},{2,34}... | collective-permute-start | bytes 1572872 | tf_op jit(solution)/shard_map/ppermute | solution.py:474
  29.6 14.2 %collective-permute-start.11 = (f32[4,2,128,128]{3,2,1,0:T(8,128)S(1)}, f32[4,2,128,128]{3,2,1,0:T(8,128)S(1)}, u32[]{:S(2)}, u32[]{:S(2)}) collective-permute-start(f32[4,2,128,128]{3,2,1,0:T(8,128)S(1)} %select_select_fusion.own_ref), channel_id=1, source_target_pairs={{0,96},{32,0},{64,32},{96,64},{1,97},{33,1},{65,33},{97,65},{2,98}... | collective-permute-start | bytes 1572872 | tf_op jit(solution)/shard_map/ppermute | solution.py:475
  43.1 0.8 copy-start.2
  43.1 9.7 %collective-permute-start.13 = (f32[2,2,128,128]{3,2,1,0:T(8,128)S(1)}, f32[2,2,128,128]{3,2,1,0:T(8,128)}, u32[]{:S(2)}, u32[]{:S(2)}) collective-permute-start(f32[2,2,128,128]{3,2,1,0:T(8,128)S(1)} %slice.24), channel_id=1, source_target_pairs={{0,32},{32,64},{64,96},{96,0},{1,33},{33,65},{65,97},{97,1},{2,34}... | collective-permute-start | bytes 786440 | tf_op jit(solution)/shard_map/ppermute | solution.py:476
  43.9 0.8 copy-start.3
  44.7 8.2 %collective-permute-start.14 = (f32[2,2,128,128]{3,2,1,0:T(8,128)S(1)}, f32[2,2,128,128]{3,2,1,0:T(8,128)}, u32[]{:S(2)}, u32[]{:S(2)}) collective-permute-start(f32[2,2,128,128]{3,2,1,0:T(8,128)S(1)} %slice.25), channel_id=1, source_target_pairs={{0,96},{32,0},{64,32},{96,64},{1,97},{33,1},{65,33},{97,65},{2,98}... | collective-permute-start | bytes 786440 | tf_op jit(solution)/shard_map/ppermute | solution.py:477
  61.9 8.2 %collective-permute-start = (f32[128,128]{1,0:T(8,128)}, f32[128,128]{1,0:T(8,128)S(1)}, u32[]{:S(2)}, u32[]{:S(2)}) collective-permute-start(f32[128,128]{1,0:T(8,128)} %get-tuple-element.88), channel_id=1, source_target_pairs={{0,8},{1,9},{2,10},{3,11},{4,12},{5,13},{6,14},{7,15},{8,16},{9,17... | collective-permute-start | bytes 196616 | tf_op jit(solution)/shard_map/cond/branch_0_fun/ppermute | solution.py:494
  62.3 7.8 %collective-permute-start.1 = (f32[128,128]{1,0:T(8,128)}, f32[128,128]{1,0:T(8,128)S(1)}, u32[]{:S(2)}, u32[]{:S(2)}) collective-permute-start(f32[128,128]{1,0:T(8,128)} %get-tuple-element.89), channel_id=1, source_target_pairs={{0,16},{1,17},{2,18},{3,19},{4,20},{5,21},{6,22},{7,23},{8,24},{9,... | collective-permute-start | bytes 196616 | tf_op jit(solution)/shard_map/cond/branch_0_fun/ppermute | solution.py:494
  65.0 5.1 %collective-permute-start.2 = (f32[128,128]{1,0:T(8,128)}, f32[128,128]{1,0:T(8,128)S(1)}, u32[]{:S(2)}, u32[]{:S(2)}) collective-permute-start(f32[128,128]{1,0:T(8,128)} %get-tuple-element.90), channel_id=1, source_target_pairs={{0,24},{1,25},{2,26},{3,27},{4,28},{5,29},{6,30},{7,31},{8,0},{9,1... | collective-permute-start | bytes 196616 | tf_op jit(solution)/shard_map/cond/branch_0_fun/ppermute | solution.py:494
  70.1 0.6 copy-start.7
  70.1 0.6 copy-start.9
  70.1 0.6 copy-start.11
  73.0 4.9 %collective-permute-start.21 = (f32[4,128]{1,0:T(4,128)S(1)}, f32[4,128]{1,0:T(4,128)S(1)}, u32[]{:S(2)}, u32[]{:S(2)}) collective-permute-start(f32[4,128]{1,0:T(4,128)S(1)} %get-tuple-element.159.rest_0_), channel_id=1, source_target_pairs={{0,96},{32,0},{64,32},{96,64},{1,97},{33,1},{65,33},{97,65},{2,98}... | collective-permute-start | bytes 6152 | tf_op jit(solution)/shard_map/ppermute | solution.py:27
  76.6 5.1 %collective-permute-start.20 = (f32[4,128]{1,0:T(4,128)S(1)}, f32[4,128]{1,0:T(4,128)S(1)}, u32[]{:S(2)}, u32[]{:S(2)}) collective-permute-start(f32[4,128]{1,0:T(4,128)S(1)} %get-tuple-element.159.rest_0_), channel_id=1, source_target_pairs={{0,64},{32,96},{64,0},{96,32},{1,65},{33,97},{65,1},{97,33},{2,66}... | collective-permute-start | bytes 6152 | tf_op jit(solution)/shard_map/ppermute | solution.py:27
  77.1 4.8 %collective-permute-start.19 = (f32[4,128]{1,0:T(4,128)S(1)}, f32[4,128]{1,0:T(4,128)S(1)}, u32[]{:S(2)}, u32[]{:S(2)}) collective-permute-start(f32[4,128]{1,0:T(4,128)S(1)} %get-tuple-element.159.rest_0_), channel_id=1, source_target_pairs={{0,32},{32,64},{64,96},{96,0},{1,33},{33,65},{65,97},{97,1},{2,34}... | collective-permute-start | bytes 6152 | tf_op jit(solution)/shard_map/ppermute | solution.py:27
  84.1 38.5 %all-to-all-start.3 = ((f32[32,128,128]{2,1,0:T(8,128)}), f32[32,128,128]{2,1,0:T(8,128)S(1)}, u32[]{:S(2)}, u32[]{:S(2)}) async-start(f32[32,128,128]{2,1,0:T(8,128)} %shard_map.52), calls=%async_computation.3 | async-start | bytes 4194304 | tf_op jit(solution)/shard_map/all_to_all | solution.py:485
  90.3 15.4 %collective-permute-start.16 = (f32[4,2,128,128]{3,2,1,0:T(8,128)S(1)}, f32[4,2,128,128]{3,2,1,0:T(8,128)S(1)}, u32[]{:S(2)}, u32[]{:S(2)}) collective-permute-start(f32[4,2,128,128]{3,2,1,0:T(8,128)S(1)} %get-tuple-element.155.own_ref.x_ref), channel_id=1, source_target_pairs={{0,32},{32,64},{64,96},{96,0},{1,33},{33,65},{65,97},{97,1},{2,34}... | collective-permute-start | bytes 1572872 | tf_op jit(solution)/shard_map/ppermute | solution.py:474
  90.4 15.4 %collective-permute-start.15 = (f32[4,2,128,128]{3,2,1,0:T(8,128)S(1)}, f32[4,2,128,128]{3,2,1,0:T(8,128)S(1)}, u32[]{:S(2)}, u32[]{:S(2)}) collective-permute-start(f32[4,2,128,128]{3,2,1,0:T(8,128)S(1)} %get-tuple-element.155.own_ref.x_ref), channel_id=1, source_target_pairs={{0,96},{32,0},{64,32},{96,64},{1,97},{33,1},{65,33},{97,65},{2,98}... | collective-permute-start | bytes 1572872 | tf_op jit(solution)/shard_map/ppermute | solution.py:475
  105.7 8.9 %copy-start.4 = (f32[4,2,128,128]{3,2,1,0:T(8,128)}, f32[4,2,128,128]{3,2,1,0:T(8,128)S(1)}, u32[]{:S(2)}) copy-start(f32[4,2,128,128]{3,2,1,0:T(8,128)S(1)} %collective-permute-done.16.behind_ref) | copy-start | bytes 1572868
  105.7 8.9 %collective-permute-start.17 = (f32[2,2,128,128]{3,2,1,0:T(8,128)S(1)}, f32[2,2,128,128]{3,2,1,0:T(8,128)S(1)}, u32[]{:S(2)}, u32[]{:S(2)}) collective-permute-start(f32[2,2,128,128]{3,2,1,0:T(8,128)S(1)} %slice.26), channel_id=1, source_target_pairs={{0,32},{32,64},{64,96},{96,0},{1,33},{33,65},{65,97},{97,1},{2,34}... | collective-permute-start | bytes 786440 | tf_op jit(solution)/shard_map/ppermute | solution.py:476
  105.8 8.8 %copy-start.5 = (f32[4,2,128,128]{3,2,1,0:T(8,128)}, f32[4,2,128,128]{3,2,1,0:T(8,128)S(1)}, u32[]{:S(2)}) copy-start(f32[4,2,128,128]{3,2,1,0:T(8,128)S(1)} %collective-permute-done.15.ahead_ref) | copy-start | bytes 1572868
  105.8 8.8 %collective-permute-start.18 = (f32[2,2,128,128]{3,2,1,0:T(8,128)S(1)}, f32[2,2,128,128]{3,2,1,0:T(8,128)}, u32[]{:S(2)}, u32[]{:S(2)}) collective-permute-start(f32[2,2,128,128]{3,2,1,0:T(8,128)S(1)} %slice.27), channel_id=1, source_target_pairs={{0,96},{32,0},{64,32},{96,64},{1,97},{33,1},{65,33},{97,65},{2,98}... | collective-permute-start | bytes 786440 | tf_op jit(solution)/shard_map/ppermute | solution.py:477
  114.6 0.7 copy-start.6
  124.2 7.8 %collective-permute-start.3 = (f32[128,128]{1,0:T(8,128)}, f32[128,128]{1,0:T(8,128)S(1)}, u32[]{:S(2)}, u32[]{:S(2)}) collective-permute-start(f32[128,128]{1,0:T(8,128)} %get-tuple-element.110), channel_id=1, source_target_pairs={{0,8},{1,9},{2,10},{3,11},{4,12},{5,13},{6,14},{7,15},{8,16},{9,17... | collective-permute-start | bytes 196616 | tf_op jit(solution)/shard_map/cond/branch_0_fun/ppermute | solution.py:494
  124.5 7.6 %collective-permute-start.4 = (f32[128,128]{1,0:T(8,128)}, f32[128,128]{1,0:T(8,128)S(1)}, u32[]{:S(2)}, u32[]{:S(2)}) collective-permute-start(f32[128,128]{1,0:T(8,128)} %get-tuple-element.111), channel_id=1, source_target_pairs={{0,16},{1,17},{2,18},{3,19},{4,20},{5,21},{6,22},{7,23},{8,24},{9,... | collective-permute-start | bytes 196616 | tf_op jit(solution)/shard_map/cond/branch_0_fun/ppermute | solution.py:494
  127.2 4.9 %collective-permute-start.5 = (f32[128,128]{1,0:T(8,128)}, f32[128,128]{1,0:T(8,128)S(1)}, u32[]{:S(2)}, u32[]{:S(2)}) collective-permute-start(f32[128,128]{1,0:T(8,128)} %get-tuple-element.112), channel_id=1, source_target_pairs={{0,24},{1,25},{2,26},{3,27},{4,28},{5,29},{6,30},{7,31},{8,0},{9,1... | collective-permute-start | bytes 196616 | tf_op jit(solution)/shard_map/cond/branch_0_fun/ppermute | solution.py:494
  132.1 0.6 copy-start.8
  132.1 0.6 copy-start.10
  132.1 0.6 copy-start.12
  135.0 5.5 %collective-permute-start.24 = (f32[4,128]{1,0:T(4,128)S(1)}, f32[4,128]{1,0:T(4,128)S(1)}, u32[]{:S(2)}, u32[]{:S(2)}) collective-permute-start(f32[4,128]{1,0:T(4,128)S(1)} %get-tuple-element.162.rest_0_), channel_id=1, source_target_pairs={{0,96},{32,0},{64,32},{96,64},{1,97},{33,1},{65,33},{97,65},{2,98}... | collective-permute-start | bytes 6152 | tf_op jit(solution)/shard_map/ppermute | solution.py:27
  139.3 5.1 %collective-permute-start.23 = (f32[4,128]{1,0:T(4,128)S(1)}, f32[4,128]{1,0:T(4,128)S(1)}, u32[]{:S(2)}, u32[]{:S(2)}) collective-permute-start(f32[4,128]{1,0:T(4,128)S(1)} %get-tuple-element.162.rest_0_), channel_id=1, source_target_pairs={{0,64},{32,96},{64,0},{96,32},{1,65},{33,97},{65,1},{97,33},{2,66}... | collective-permute-start | bytes 6152 | tf_op jit(solution)/shard_map/ppermute | solution.py:27
  139.3 5.1 %collective-permute-start.22 = (f32[4,128]{1,0:T(4,128)S(1)}, f32[4,128]{1,0:T(4,128)S(1)}, u32[]{:S(2)}, u32[]{:S(2)}) collective-permute-start(f32[4,128]{1,0:T(4,128)S(1)} %get-tuple-element.162.rest_0_), channel_id=1, source_target_pairs={{0,32},{32,64},{64,96},{96,0},{1,33},{33,65},{65,97},{97,1},{2,34}... | collective-permute-start | bytes 6152 | tf_op jit(solution)/shard_map/ppermute | solution.py:27
  140.6 3.8 %copy-start.13 = (f32[4,128]{1,0:T(4,128)}, f32[4,128]{1,0:T(4,128)S(1)}, u32[]{:S(2)}) copy-start(f32[4,128]{1,0:T(4,128)S(1)} %collective-permute-done.24.rest_3_) | copy-start | bytes 6148
  144.3 0.6 copy-start.14
  144.4 0.6 copy-start.15

commit v2 on v1

--- a/solution.py
+++ b/solution.py
@@ -29,21 +29,22 @@
 
 
 def plan_kernel(
-    permuted, steps, whole, scal_ref, order_ref, in_ref, out_ref, plan_ref, grid_ref, line_ref
+    moved, steps, whole, order_ref, in_ref, out_ref, plan_ref, grid_ref, line_ref
 ):
-    place, row, _, _, depth = (scal_ref[i] for i in range(5))
+    place, row = lax.axis_index("pcol"), lax.axis_index("prow")
+    panels_all = order_ref.shape[1]
+    depth = panels_all // 4
     share = in_ref.shape[0] // 4
     shape = (LANES, LANES)
     down = lax.broadcasted_iota(jnp.int32, shape, 0)
     along = lax.broadcasted_iota(jnp.int32, shape, 1)
-    line_ref[...] = jnp.full(line_ref.shape, -2, jnp.int32)
-    line_ref[:1, : order_ref.shape[1]] = order_ref[...]
-    held = jnp.broadcast_to(line_ref[:1, :], shape)
-    if permuted:
-        diagonal = jnp.where(down == along, held, 0)
-        source = jnp.broadcast_to(jnp.sum(diagonal, axis=1, keepdims=True), shape)
+    if moved:
+        line_ref[...] = jnp.full(line_ref.shape, -2, jnp.int32)
+        line_ref[:1, :panels_all] = order_ref[...]
+        held = jnp.broadcast_to(line_ref[:1, :], shape)
     else:
-        source = jnp.where(down < depth * 4, down, -1)
+        held = jnp.where(along < panels_all, along, -2)
+    source = jnp.where(down < panels_all, down, -1)
     names = in_ref[...]
     panels, inside = names // 4, lax.rem(names, 4)
     groups = (down // 4 == held).astype(jnp.bfloat16)
@@ -136,21 +137,21 @@
     plan_ref[pl.ds(SECOND, 1), :] = grid_ref[1, pl.ds(place, 1), :].astype(jnp.int32)
 
 
-def plans_kernel(parts, scal_ref, order_ref, first_ref, second_ref, *rest):
+def plans_kernel(parts, order_ref, first_ref, second_ref, *rest):
     *plan_refs, grid_ref, line_ref = rest
-    for (permuted, steps, whole), plan_ref in zip(parts, plan_refs):
+    for (moved, steps, whole), plan_ref in zip(parts, plan_refs):
+        in_ref = second_ref if moved else first_ref
         plan_kernel(
-            permuted, steps, whole, scal_ref, order_ref,
-            second_ref if permuted else first_ref, second_ref, plan_ref, grid_ref, line_ref,
+            moved, steps, whole, order_ref, in_ref, second_ref, plan_ref, grid_ref, line_ref
         )
 
 
-def plans(parts, scal, order_line, first_rows, second_rows):
+def plans(parts, order_line, first_rows, second_rows):
     work = sum((1 if steps else 0) + (4 if whole else 0) for _, steps, whole in parts)
     return pl.pallas_call(
         functools.partial(plans_kernel, parts),
         out_shape=(jax.ShapeDtypeStruct((8, LANES), jnp.int32),) * len(parts),
-        in_specs=[SMEM, VMEM, VMEM, VMEM],
+        in_specs=[VMEM, VMEM, VMEM],
         out_specs=(VMEM,) * len(parts),
         scratch_shapes=[
             pltpu.VMEM((2, LANES, LANES), jnp.float32),
@@ -159,7 +160,7 @@
         cost_estimate=pl.CostEstimate(
             flops=work << 23, bytes_accessed=1 << 14, transcendentals=0
         ),
-    )(scal, order_line, first_rows, second_rows)
+    )(order_line, first_rows, second_rows)
 
 
 def column_kernel(x_ref, part_ref):
@@ -213,9 +214,10 @@
     )(steps, x, *sums)
 
 
-def hop_kernel(scal_ref, plan_ref, got_ref, *rest):
+def hop_kernel(plan_ref, got_ref, *rest):
     *outs, sems = rest
-    place, depth = scal_ref[0], scal_ref[4]
+    place = lax.axis_index("pcol")
+    depth = got_ref.shape[0] // 4
     pieces = []
     for step, out in enumerate(outs):
         target = lax.rem(place + (step + 1) * depth, 4 * depth)
@@ -227,16 +229,16 @@
         piece.wait()
 
 
-def hop_tiles(scal, steps, got):
+def hop_tiles(steps, got):
     tile = jax.ShapeDtypeStruct(got.shape[1:], jnp.float32)
     return pl.pallas_call(
         hop_kernel,
         out_shape=(tile,) * 3,
-        in_specs=[SMEM, SMEM, ANY],
+        in_specs=[SMEM, ANY],
         out_specs=(VMEM,) * 3,
         scratch_shapes=[pltpu.SemaphoreType.DMA((3,))],
         cost_estimate=pl.CostEstimate(flops=0, bytes_accessed=6 << 16, transcendentals=0),
-    )(scal, steps, got)
+    )(steps, got)
 
 
 def split(value):
@@ -255,16 +257,76 @@
 FIRSTS, SECONDS, LIST = 2, 64, 128
 
 
+def matched(in_ref, out_pat_ref, row, share, own_column, column, t):
+    wanted = out_pat_ref[row * share + t, own_column]
+    hit = wanted < 0
+    at = 0
+    for u in range(share):
+        same = in_ref[row * share + u, column] == wanted
+        hit = jnp.logical_or(hit, same)
+        at = jnp.where(same, u, at)
+    return hit, at
+
+
+def held_panel(moved, order_ref):
+    place = lax.axis_index("pcol")
+    return order_ref[place] if moved else place
+
+
+def list_kernel(moved, cols, share, order_ref, plan_ref, in_ref, out_pat_ref, list_ref):
+    row = lax.axis_index("prow")
+    panel = held_panel(moved, order_ref)
+    names = in_ref.shape[0]
+
+    def remote(place_of, counts):
+        own_column = panel * cols + place_of // names
+        column = in_ref[lax.rem(place_of, names), own_column]
+        origin = column // cols
+        firsts, seconds = counts
+        for t in range(share):
+            hit, at = matched(in_ref, out_pat_ref, row, share, own_column, column, t)
+            hit = jnp.logical_and(hit, origin != panel)
+            extra = jnp.logical_and(hit, jnp.logical_and(at == 1, plan_ref[FIRST, origin] > 0))
+            simple = jnp.logical_and(hit, jnp.logical_not(extra))
+            entry = (place_of * share + t) * 32 + origin
+
+            @pl.when(simple)
+            def _():
+                list_ref[FIRSTS + firsts] = entry
+
+            @pl.when(extra)
+            def _():
+                list_ref[SECONDS + seconds] = entry
+
+            firsts = firsts + simple.astype(jnp.int32)
+            seconds = seconds + extra.astype(jnp.int32)
+        return firsts, seconds
+
+    firsts, seconds = lax.fori_loop(0, cols * names, remote, (jnp.int32(0), jnp.int32(0)))
+    list_ref[0] = firsts
+    list_ref[1] = seconds
+
+
+def tile_list(moved, cols, share, order, steps, in_pattern, out_pattern):
+    return pl.pallas_call(
+        functools.partial(list_kernel, moved, cols, share),
+        out_shape=jax.ShapeDtypeStruct((LIST,), jnp.int32),
+        in_specs=[SMEM] * 4,
+        out_specs=SMEM,
+        cost_estimate=pl.CostEstimate(flops=1 << 28, bytes_accessed=1 << 14, transcendentals=0),
+    )(order, steps, in_pattern, out_pattern)
+
+
 def own_kernel(
-    permuted, scal_ref, order_ref, plan_ref, in_ref, out_pat_ref,
+    moved, order_ref, in_ref, out_pat_ref,
     own_ref, ahead_ref, behind_ref, far_low_ref, far_high_ref,
-    base_ref, totals_ref, right_ref, list_ref,
+    base_ref, totals_ref, right_ref,
 ):
     cols, share, tile, _ = own_ref.shape
-    place, row, depth = scal_ref[0], scal_ref[1], scal_ref[4]
+    row = lax.axis_index("prow")
     rows = right_ref.shape[1] // share
-    panel = order_ref[place]
-    home = panel // depth
+    panel = held_panel(moved, order_ref)
+    home = panel // (order_ref.shape[0] // rows)
     half = cols // 2
 
     for rel in range(4):
@@ -277,56 +339,16 @@
         whole = right_ref[j].reshape(rows * share * tile, tile)
         totals_ref[pl.ds(j, 1), :] = jnp.sum(whole, axis=0, keepdims=True)
 
-    def found(j, column, t):
-        wanted = out_pat_ref[row * share + t, panel * cols + j]
-        hit = wanted < 0
-        at = 0
-        for u in range(share):
-            same = in_ref[row * share + u, column] == wanted
-            hit = jnp.logical_or(hit, same)
-            at = jnp.where(same, u, at)
-        return hit, at
-
-    def remote(place_of, counts):
-        j, k = place_of // (rows * share), lax.rem(place_of, rows * share)
-        column = in_ref[k, panel * cols + j]
-        source = column // cols
-        origin = order_ref[source] if permuted else source
-        firsts, seconds = counts
-        for t in range(share):
-            hit, at = found(j, column, t)
-            hit = jnp.logical_and(hit, source != panel)
-            extra = jnp.logical_and(hit, jnp.logical_and(at == 1, plan_ref[FIRST, origin] > 0))
-            simple = jnp.logical_and(hit, jnp.logical_not(extra))
-            entry = (place_of * share + t) * 32 + origin
-
-            @pl.when(simple)
-            def _():
-                list_ref[FIRSTS + firsts] = entry
-
-            @pl.when(extra)
-            def _():
-                list_ref[SECONDS + seconds] = entry
-
-            firsts = firsts + simple.astype(jnp.int32)
-            seconds = seconds + extra.astype(jnp.int32)
-        return firsts, seconds
-
-    firsts, seconds = lax.fori_loop(
-        0, cols * rows * share, remote, (jnp.int32(0), jnp.int32(0))
-    )
-    list_ref[0] = firsts
-    list_ref[1] = seconds
-
     @pl.loop(0, cols)
     def _(j):
         base_ref[j] = jnp.zeros((share, tile, tile), jnp.float32)
         for s in range(share):
             k = home * share + s
-            column = in_ref[k, panel * cols + j]
+            own_column = panel * cols + j
+            column = in_ref[k, own_column]
             local = lax.rem(column, cols)
             for t in range(share):
-                hit, at = found(j, column, t)
+                hit, at = matched(in_ref, out_pat_ref, row, share, own_column, column, t)
 
                 @pl.when(jnp.logical_and(hit, column // cols == panel))
                 def _():
@@ -334,20 +356,47 @@
                     base_ref[j, t] += dot_exactly(left, right_ref[j, k])
 
 
-def own_products(permuted, scal, order, steps, in_pattern, out_pattern, own, gathered):
+def own_products(moved, order, in_pattern, out_pattern, own, gathered):
     cols, share, tile, _ = own.shape
     return pl.pallas_call(
-        functools.partial(own_kernel, permuted),
+        functools.partial(own_kernel, moved),
         out_shape=(
             jax.ShapeDtypeStruct(own.shape, jnp.float32),
             jax.ShapeDtypeStruct((cols, tile), jnp.float32),
             jax.ShapeDtypeStruct((cols, 4 * share, tile, tile), jnp.float32),
-            jax.ShapeDtypeStruct((LIST,), jnp.int32),
         ),
-        in_specs=[SMEM] * 5 + [VMEM] * 5,
-        out_specs=(VMEM, VMEM, VMEM, SMEM),
+        in_specs=[SMEM] * 3 + [VMEM] * 5,
+        out_specs=(VMEM, VMEM, VMEM),
         cost_estimate=pl.CostEstimate(flops=1 << 26, bytes_accessed=5 << 20, transcendentals=0),
-    )(scal, order, steps, in_pattern, out_pattern, own, *gathered)
+    )(order, in_pattern, out_pattern, own, *gathered)
+
+
+def pick_kernel(order_ref, held_ref, below_ref, above_ref, out_ref, sem):
+    place = lax.axis_index("pcol")
+    panel = order_ref[place]
+    for chosen, ref in (
+        (panel == place, held_ref), (panel < place, below_ref), (panel > place, above_ref)
+    ):
+
+        @pl.when(chosen)
+        def _():
+            pltpu.make_async_copy(ref, out_ref, sem).start()
+
+    pltpu.make_async_copy(held_ref, out_ref, sem).wait()
+
+
+def shifted(order, x):
+    up = [(i, i + 1) for i in range(order.shape[0] - 1)]
+    from_below = lax.ppermute(x, "pcol", up)
+    from_above = lax.ppermute(x, "pcol", [(j, i) for i, j in up])
+    return pl.pallas_call(
+        pick_kernel,
+        out_shape=jax.ShapeDtypeStruct(x.shape, jnp.float32),
+        in_specs=[SMEM, ANY, ANY, ANY],
+        out_specs=VMEM,
+        scratch_shapes=[pltpu.SemaphoreType.DMA],
+        cost_estimate=pl.CostEstimate(flops=0, bytes_accessed=1 << 20, transcendentals=0),
+    )(order, x, from_below, from_above)
 
 
 def add_listed(list_ref, number, first, right_ref, acc_ref, fetch, lefts, rights, sems):
@@ -390,10 +439,10 @@
     add_listed(list_ref, 0, FIRSTS, right_ref, acc_ref, fetch, lefts, rights, sems)
 
 
-def last_kernel(scal_ref, list_ref, acc_in_ref, totals_ref, right_ref, *rest):
+def last_kernel(depth, list_ref, acc_in_ref, totals_ref, right_ref, *rest):
     *extra_refs, sq_ref, part_ref, lefts, rights, sems = rest
     cols, share, tile, _ = acc_in_ref.shape
-    place, depth = scal_ref[0], scal_ref[4]
+    place = lax.axis_index("pcol")
     sq_ref[...] = acc_in_ref[...]
 
     def fetch(i, origin):
@@ -436,19 +485,19 @@
     )(tiles, base, right, got)
 
 
-def last_products(scal, tiles, acc, totals, right, extra):
+def last_products(depth, tiles, acc, totals, right, extra):
     cols, _, tile, _ = acc.shape
     return pl.pallas_call(
-        last_kernel,
+        functools.partial(last_kernel, depth),
         out_shape=(
             jax.ShapeDtypeStruct(acc.shape, jnp.float32),
             jax.ShapeDtypeStruct((cols, tile), jnp.float32),
         ),
-        in_specs=[SMEM, SMEM, VMEM, VMEM, ANY] + [ANY] * len(extra),
+        in_specs=[SMEM, VMEM, VMEM, ANY] + [ANY] * len(extra),
         out_specs=(VMEM, VMEM),
         scratch_shapes=list_scratch(right),
         cost_estimate=pl.CostEstimate(flops=1 << 24, bytes_accessed=2 << 20, transcendentals=0),
-    )(scal, tiles, acc, totals, right, *extra)
+    )(tiles, acc, totals, right, *extra)
 
 
 def divide_kernel(x_ref, *rest):
@@ -478,67 +527,51 @@
     return ahead, behind, far_low, far_high
 
 
-def expand(permuted, scal, order, steps, misfit, in_pattern, out_pattern, x, sums, own, rows):
+def expand(moved, order, steps, misfit, in_pattern, out_pattern, x, sums, own, rows):
+    cols, share = x.shape[:2]
     panels = order.shape[0]
     depth = panels // 4
     send = prepare(SEND, steps, x, sums, panels)
     got = lax.all_to_all(send, "pcol", 0, 0, tiled=True)
+    tiles = tile_list(moved, cols, share, order, steps, in_pattern, out_pattern)
     gathered = gather_rows(own, rows)
-    base, totals, right, tiles = own_products(
-        permuted, scal, order, steps, in_pattern, out_pattern, own, gathered
-    )
+    base, totals, right = own_products(moved, order, in_pattern, out_pattern, own, gathered)
 
     def by_level(_):
-        hops = hop_tiles(scal, steps, got)
+        hops = hop_tiles(steps, got)
         extra = tuple(
             lax.ppermute(tile, "pcol", ring(panels, (step + 1) * depth))
             for step, tile in enumerate(hops)
         )
         acc = main_products(tiles, base, right, got)
-        return last_products(scal, tiles, acc, totals, right, extra)
+        return last_products(depth, tiles, acc, totals, right, extra)
 
     def by_second(_):
         more = prepare(SECOND, steps, x, sums, panels)
         extra = (lax.all_to_all(more, "pcol", 0, 0, tiled=True),)
         acc = main_products(tiles, base, right, got)
-        return last_products(scal, tiles, acc, totals, right, extra)
+        return last_products(depth, tiles, acc, totals, right, extra)
 
     return lax.cond(misfit > 0, by_second, by_level, 0)
 
 
 def local(match_tiles, pattern, kept, panel_order):
-    cols = match_tiles.shape[0]
-    panels = panel_order.shape[0]
-    row = lax.axis_index("prow")
     rows = lax.axis_size("prow")
-    place = lax.axis_index("pcol")
-    panel = panel_order[place]
     order = panel_order
-    order_line = order[None]
     pattern_rows = pattern.T
     kept_rows = kept.T
-    scal = jnp.stack(
-        [place, row, jnp.int32(rows), jnp.int32(cols), jnp.int32(panels // 4)]
-    )
-    tables = (scal, order_line, pattern_rows, kept_rows)
+    tables = (order[None], pattern_rows, kept_rows)
     (first_plan,) = plans(((False, True, False),), *tables)
-
     sums = row_sums(column_partial(match_tiles), rows)
-    below = [(i, i + 1) for i in range(panels - 1)]
-    from_below = lax.ppermute(match_tiles, "pcol", below)
-    from_above = lax.ppermute(match_tiles, "pcol", [(j, i) for i, j in below])
-    own = jnp.where(panel == place, match_tiles, jnp.where(panel < place, from_below, from_above))
-    sums, own = lax.optimization_barrier((sums, own))
     check, second_plan = plans(((False, False, True), (True, True, True)), *tables)
-    first_misfit, second_misfit = check[MISFIT, 0], second_plan[MISFIT, 0]
     square, part = expand(
-        False, scal, order, first_plan, first_misfit, pattern_rows, kept_rows,
-        match_tiles, sums, own, rows,
+        False, order, first_plan, check[MISFIT, 0], pattern_rows, kept_rows,
+        match_tiles, sums, match_tiles, rows,
     )
     sums = row_sums(part, rows)
     square, part = expand(
-        True, scal, order, second_plan, second_misfit, kept_rows, kept_rows,
-        square, sums, square, rows,
+        True, order, second_plan, second_plan[MISFIT, 0], kept_rows, kept_rows,
+        square, sums, shifted(order, square), rows,
     )
     return divided(square, row_sums(part, rows))
 

time: 148 us -> 176 us (1.19)
  starting transfers between devices: 57 us -> 86.7 us
  waiting for transfers between devices: 36.9 us -> 32.8 us
  Pallas kernels: 41.8 us -> 44.8 us
  local copies, waits for them, and re-layouts: 6.6 us -> 8.51 us
    ppermute x6, starting transfers between devices: 8.88 us -> 40.7 us  [by_level(): lax.ppermute(tile, 'pcol', ring(panels, (step + 1) * depth))]
    ppermute x2, waiting for transfers between devices: 24.1 us -> 19.4 us  [gather_rows(): behind = lax.ppermute(own, 'prow', ring(size, 1))]
    pallas_call x6 -> x9, Pallas kernels: 22.4 us -> 26.9 us  [the longest x2 12.1 us: own_products(): pl.pallas_call(functools.partial(own_kernel, moved), out_shape=(jax.Shape...]
    ppermute x2, waiting for transfers between devices: 4.43 us -> 0.01 us  [gather_rows(): far_low = lax.ppermute(behind[:half], 'prow', ring(size, 1))]
    ppermute x9, waiting for transfers between devices: 8.27 us -> 11.2 us  [row_sums(): sums.append(lax.ppermute(partial_value, 'prow', ring(size, step)))]
    pallas_call x2, Pallas kernels: 5.42 us -> 3.49 us  [plans(): pl.pallas_call(functools.partial(plans_kernel, parts), out_shape=(jax.Sha...]
    all_to_all x2, starting transfers between devices: 16 us -> 14.2 us  [expand(): got = lax.all_to_all(send, 'pcol', 0, 0, tiled=True)]
    unnamed x20 -> x22, local copies, waits for them, and re-layouts: 2.22 us -> 3.92 us
  transfers between devices with their start and end apart: 27 -> 27, of which waited for: 8 -> 12; matrix products, arithmetic and copies ran while one was open for 3% -> 2% of each run, Pallas kernels for 19% -> 17%
where the time goes in v2:
time: 176 us; the launch traced here: 174 us
  starting transfers between devices  86.7 us (49%)
  Pallas kernels  44.8 us (25%)
  waiting for transfers between devices  32.8 us (19%)
  local copies, waits for them, and re-layouts  8.51 us (5%)
    ppermute x6, starting transfers between devices, by_level(): lax.ppermute(tile, 'pcol', ring(panels, (step + 1) * depth))  40.7 us
    ppermute x2, waiting for transfers between devices, gather_rows(): behind = lax.ppermute(own, 'prow', ring(size, 1))  19.4 us
    all_to_all x2, starting transfers between devices, expand(): got = lax.all_to_all(send, 'pcol', 0, 0, tiled=True)  14.2 us
    ppermute x9, starting transfers between devices, row_sums(): sums.append(lax.ppermute(partial_value, 'prow', ring(size, step)))  14.2 us
    pallas_call x2, Pallas kernels, own_products(): pl.pallas_call(functools.partial(own_kernel, moved), out_shape=(jax.Shape...  12.1 us
    ppermute x9, waiting for transfers between devices, row_sums(): sums.append(lax.ppermute(partial_value, 'prow', ring(size, step)))  11.2 us
    pallas_call x2, Pallas kernels, main_products(): pl.pallas_call(main_kernel, out_shape=jax.ShapeDtypeStruct(base.shape, jn...  7.14 us
    ppermute x2, starting transfers between devices, gather_rows(): ahead = lax.ppermute(own, 'prow', ring(size, -1))  6.17 us
  transfers between devices with their start and end apart: 27, of which 12 were waited for; matrix products, arithmetic and copies ran while one was open for 2% of the time, Pallas kernels for 17%

profile of v2, /device:TPU:0, one launch (start us, length us, event | category | flops | bytes accessed | tf_op | source)
XLA Modules:
  0.0 174.4 jit_solution(10105827414456683598)
XLA Ops:
  0.0 1.1 shard_map.51.rest_0_
  1.1 2.9 %collective-permute-start.12 = (f32[4,128]{1,0:T(4,128)S(1)}, f32[4,128]{1,0:T(4,128)S(1)}, u32[]{:S(2)}, u32[]{:S(2)}) collective-permute-start(f32[4,128]{1,0:T(4,128)S(1)} %shard_map.51.rest_0_), channel_id=1, source_target_pairs={{0,96},{32,0},{64,32},{96,64},{1,97},{33,1},{65,33},{97,65},{2,98}... | collective-permute-start | bytes 6152 | tf_op jit(solution)/shard_map/ppermute | solution.py:27
  4.0 0.8 collective-permute-start.11
  4.8 0.9 collective-permute-start.10
  5.7 1.1 shard_map.48.plan_ref
  6.8 2.3 %collective-permute-done.11.rest_2_ = f32[4,128]{1,0:T(4,128)S(1)} collective-permute-done((f32[4,128]{1,0:T(4,128)S(1)}, f32[4,128]{1,0:T(4,128)S(1)}, u32[]{:S(2)}, u32[]{:S(2)}) %collective-permute-start.11) | collective-permute-done | bytes 2080 | tf_op jit(solution)/shard_map/ppermute | solution.py:27
  9.6 2.5 %shard_map.52 = f32[32,128,128]{2,1,0:T(8,128)} custom-call(s32[8,128]{1,0:T(8,128)S(1)} %shard_map.48.plan_ref, f32[4,2,128,128]{3,2,1,0:T(8,128)} %x_ref.3, f32[4,128]{1,0:T(4,128)S(1)} %shard_map.51.rest_0_, f32[4,128]{1,0:T(4,128)S(1)} %collective-permute-done.10.rest_1_, f32[4,128]{1,0:T(4,128)S(1)} %collective-permute-done.11.rest_2_, ...), custom_call_target="tpu_custom_call" | custom-call | flops 131072 | bytes 3145728 | tf_op jit(solution)/shard_map/pallas_call | solution.py:204
  12.1 8.3 %all-to-all-start.2 = ((f32[32,128,128]{2,1,0:T(8,128)}), f32[32,128,128]{2,1,0:T(8,128)S(1)}, u32[]{:S(2)}, u32[]{:S(2)}) async-start(f32[32,128,128]{2,1,0:T(8,128)} %shard_map.52), calls=%async_computation.2 | async-start | bytes 4194304 | tf_op jit(solution)/shard_map/all_to_all | solution.py:535
  20.5 3.2 %collective-permute-start.6 = (f32[4,2,128,128]{3,2,1,0:T(8,128)S(1)}, f32[4,2,128,128]{3,2,1,0:T(8,128)S(1)}, u32[]{:S(2)}, u32[]{:S(2)}) collective-permute-start(f32[4,2,128,128]{3,2,1,0:T(8,128)S(1)} %copy-done), channel_id=1, source_target_pairs={{0,96},{32,0},{64,32},{96,64},{1,97},{33,1},{65,33},{97,65},{2,98}... | collective-permute-start | bytes 1572872 | tf_op jit(solution)/shard_map/ppermute | solution.py:524
  23.7 12.1 %collective-permute-done.7.behind_ref = f32[4,2,128,128]{3,2,1,0:T(8,128)S(1)} collective-permute-done((f32[4,2,128,128]{3,2,1,0:T(8,128)S(1)}, f32[4,2,128,128]{3,2,1,0:T(8,128)S(1)}, u32[]{:S(2)}, u32[]{:S(2)}) %collective-permute-start.7) | collective-permute-done | bytes 524320 | tf_op jit(solution)/shard_map/ppermute | solution.py:523
  37.4 2.5 %collective-permute-start.9 = (f32[2,2,128,128]{3,2,1,0:T(8,128)S(1)}, f32[2,2,128,128]{3,2,1,0:T(8,128)}, u32[]{:S(2)}, u32[]{:S(2)}) collective-permute-start(f32[2,2,128,128]{3,2,1,0:T(8,128)S(1)} %slice.25), channel_id=1, source_target_pairs={{0,96},{32,0},{64,32},{96,64},{1,97},{33,1},{65,33},{97,65},{2,98}... | collective-permute-start | bytes 786440 | tf_op jit(solution)/shard_map/ppermute | solution.py:526
  40.0 2.4 %shard_map.46 = (s32[8,128]{1,0:T(8,128)}, s32[8,128]{1,0:T(8,128)S(1)}) custom-call(s32[1,32]{1,0:T(1,128)} %bitcast.14, s32[8,128]{1,0:T(8,128)} %bitcast.16, s32[8,128]{1,0:T(8,128)} %bitcast.6), custom_call_target="tpu_custom_call" | custom-call | flops 75497472 | bytes 16384 | tf_op jit(solution)/shard_map/pallas_call | solution.py:151
  42.3 1.3 slice.19
  44.3 2.8 %shard_map.49 = s32[128]{0:T(128)S(1)} custom-call(s32[32]{0:T(128)} %order_ref.9, s32[8,128]{1,0:T(8,128)S(1)} %shard_map.48.plan_ref, s32[8,128]{1,0:T(8,128)} %bitcast.17, s32[8,128]{1,0:T(8,128)} %bitcast.7), custom_call_target="tpu_custom_call" | custom-call | flops 268435456 | bytes 16384 | tf_op jit(solution)/shard_map/pallas_call | solution.py:311
  47.8 6.0 %shard_map.50 = (f32[4,2,128,128]{3,2,1,0:T(8,128)S(1)}, f32[4,128]{1,0:T(4,128)S(1)}, f32[4,8,128,128]{3,2,1,0:T(8,128)}) custom-call(s32[32]{0:T(128)} %order_ref.9, s32[8,128]{1,0:T(8,128)} %bitcast.18, s32[8,128]{1,0:T(8,128)} %bitcast.8, f32[4,2,128,128]{3,2,1,0:T(8,128)S(1)} %copy-done, f32[4,2,128,128]{3,2,1,0:T(8,128)} %copy-done.3, ...), custom_call_target="tpu_custom_call" | custom-call | flops 67108864 | bytes 5242880 | tf_op jit(solution)/shard_map/pallas_call | solution.py:361
  53.8 12.8 %conditional.2 = ((f32[4,2,128,128]{3,2,1,0:T(8,128)S(1)}, f32[4,128]{1,0:T(4,128)S(1)})) conditional(s32[]{:T(128)} %bitcast.4, (s32[128]{0:T(128)S(1)}, f32[4,2,128,128]{3,2,1,0:T(8,128)S(1)}, f32[4,8,128,128]{3,2,1,0:T(8,128)}, f32[32,128,128]{2,1,0:T(8,128)S(1)}, s32[8,128]{1,0:T(8,128)S(1)}, /*index=5*/f32[4,128]{1,0:T(4,128)S(1)}) %tuple.17, ...), branch_computations={%region_0.0_spmd, %region_1.0_spmd} | conditional | flops 1090650112 | bytes 14680104 | solution.py:555
  53.8 1.6 branch_0_fun.7
  55.8 2.7 %collective-permute-start.1 = (f32[128,128]{1,0:T(8,128)}, f32[128,128]{1,0:T(8,128)S(1)}, u32[]{:S(2)}, u32[]{:S(2)}) collective-permute-start(f32[128,128]{1,0:T(8,128)} %get-tuple-element.80), channel_id=1, source_target_pairs={{0,16},{1,17},{2,18},{3,19},{4,20},{5,21},{6,22},{7,23},{8,24},{9,... | collective-permute-start | bytes 196616 | tf_op jit(solution)/shard_map/cond/branch_0_fun/ppermute | solution.py:543
  58.5 1.4 collective-permute-start.2
  59.9 3.7 %branch_0_fun.6.acc_in_ref = f32[4,2,128,128]{3,2,1,0:T(8,128)} custom-call(s32[128]{0:T(128)S(1)} %get-tuple-element.73.list_ref, f32[4,2,128,128]{3,2,1,0:T(8,128)S(1)} %get-tuple-element.74.base_ref, f32[4,8,128,128]{3,2,1,0:T(8,128)} %get-tuple-element.75.right_ref, f32[32,128,128]{2,1,0:T(8,128)S(1)} %get-tuple-element.76.got_ref), custom_call_target="tpu_custom_call" | custom-call | flops 1073741824 | bytes 3145728 | tf_op jit(solution)/shard_map/cond/branch_0_fun/pallas_call | solution.py:478
  64.3 2.2 %branch_0_fun.8 = (f32[4,2,128,128]{3,2,1,0:T(8,128)S(1)}, f32[4,128]{1,0:T(4,128)S(1)}) custom-call(s32[128]{0:T(128)S(1)} %get-tuple-element.73.list_ref, f32[4,2,128,128]{3,2,1,0:T(8,128)} %branch_0_fun.6.acc_in_ref, f32[4,128]{1,0:T(4,128)S(1)} %get-tuple-element.77.totals_ref, f32[4,8,128,128]{3,2,1,0:T(8,128)} %get-tuple-element.75.right_ref, ...), custom_call_target="tpu_custom_call" | custom-call | flops 16777216 | bytes 2097152 | tf_op jit(solution)/shard_map/cond/branch_0_fun/pallas_call | solution.py:490
  66.5 1.4 collective-permute-start.21
  67.9 0.8 collective-permute-start.20
  69.3 0.9 collective-permute-done.21.rest_3_
  70.2 2.8 %collective-permute-done.20.rest_2_ = f32[4,128]{1,0:T(4,128)S(1)} collective-permute-done((f32[4,128]{1,0:T(4,128)S(1)}, f32[4,128]{1,0:T(4,128)S(1)}, u32[]{:S(2)}, u32[]{:S(2)}) %collective-permute-start.20) | collective-permute-done | bytes 2080 | tf_op jit(solution)/shard_map/ppermute | solution.py:27
  73.6 2.2 %shard_map.55 = f32[32,128,128]{2,1,0:T(8,128)} custom-call(s32[8,128]{1,0:T(8,128)S(1)} %get-tuple-element.125.plan_ref, f32[4,2,128,128]{3,2,1,0:T(8,128)S(1)} %get-tuple-element.130.held_ref.x_ref, f32[4,128]{1,0:T(4,128)S(1)} %get-tuple-element.133.rest_0_, f32[4,128]{1,0:T(4,128)S(1)} %collective-permute-done.19.rest_1_, ...), custom_call_target="tpu_custom_call" | custom-call | flops 131072 | bytes 3145728 | tf_op jit(solution)/shard_map/pallas_call | solution.py:204
  75.8 5.9 %all-to-all-start.3 = ((f32[32,128,128]{2,1,0:T(8,128)}), f32[32,128,128]{2,1,0:T(8,128)S(1)}, u32[]{:S(2)}, u32[]{:S(2)}) async-start(f32[32,128,128]{2,1,0:T(8,128)} %shard_map.55), calls=%async_computation.3 | async-start | bytes 4194304 | tf_op jit(solution)/shard_map/all_to_all | solution.py:535
  81.7 1.3 collective-permute-start.14
  83.0 3.8 %collective-permute-start.13 = (f32[4,2,128,128]{3,2,1,0:T(8,128)S(1)}, f32[4,2,128,128]{3,2,1,0:T(8,128)}, u32[]{:S(2)}, u32[]{:S(2)}) collective-permute-start(f32[4,2,128,128]{3,2,1,0:T(8,128)S(1)} %get-tuple-element.130.held_ref.x_ref), channel_id=1, source_target_pairs={{0,1},{1,2},{2,3},{3,4},{4,5},{5,6},{6,7},{7,8},{8,9},{9,10},{10,1... | collective-permute-start | bytes 1572872 | tf_op jit(solution)/shard_map/ppermute | solution.py:390
  86.9 0.8 collective-permute-done.13.below_ref
  87.7 1.5 shard_map.53.own_ref
  89.6 2.9 %collective-permute-start.15 = (f32[4,2,128,128]{3,2,1,0:T(8,128)}, f32[4,2,128,128]{3,2,1,0:T(8,128)S(1)}, u32[]{:S(2)}, u32[]{:S(2)}) collective-permute-start(f32[4,2,128,128]{3,2,1,0:T(8,128)} %shard_map.53.own_ref), channel_id=1, source_target_pairs={{0,96},{32,0},{64,32},{96,64},{1,97},{33,1},{65,33},{97,65},{2,98}... | collective-permute-start | bytes 1572872 | tf_op jit(solution)/shard_map/ppermute | solution.py:524
  92.6 7.4 %collective-permute-done.16.behind_ref = f32[4,2,128,128]{3,2,1,0:T(8,128)S(1)} collective-permute-done((f32[4,2,128,128]{3,2,1,0:T(8,128)}, f32[4,2,128,128]{3,2,1,0:T(8,128)S(1)}, u32[]{:S(2)}, u32[]{:S(2)}) %collective-permute-start.16) | collective-permute-done | bytes 524320 | tf_op jit(solution)/shard_map/ppermute | solution.py:523
  100.7 0.8 copy-done.4
  102.3 3.2 %collective-permute-start.18 = (f32[2,2,128,128]{3,2,1,0:T(8,128)}, f32[2,2,128,128]{3,2,1,0:T(8,128)}, u32[]{:S(2)}, u32[]{:S(2)}) collective-permute-start(f32[2,2,128,128]{3,2,1,0:T(8,128)} %slice.27), channel_id=1, source_target_pairs={{0,96},{32,0},{64,32},{96,64},{1,97},{33,1},{65,33},{97,65},{2,98}... | collective-permute-start | bytes 786440 | tf_op jit(solution)/shard_map/ppermute | solution.py:526
  106.6 2.8 %shard_map.47 = s32[128]{0:T(128)S(1)} custom-call(s32[32]{0:T(128)} %order_ref.9, s32[8,128]{1,0:T(8,128)S(1)} %get-tuple-element.125.plan_ref, s32[8,128]{1,0:T(8,128)} %bitcast.9, s32[8,128]{1,0:T(8,128)} %bitcast.10), custom_call_target="tpu_custom_call" | custom-call | flops 268435456 | bytes 16384 | tf_op jit(solution)/shard_map/pallas_call | solution.py:311
  110.1 6.1 %shard_map.54 = (f32[4,2,128,128]{3,2,1,0:T(8,128)S(1)}, f32[4,128]{1,0:T(4,128)S(1)}, f32[4,8,128,128]{3,2,1,0:T(8,128)}) custom-call(s32[32]{0:T(128)} %order_ref.9, s32[8,128]{1,0:T(8,128)} %bitcast.11, s32[8,128]{1,0:T(8,128)} %bitcast.12, f32[4,2,128,128]{3,2,1,0:T(8,128)} %shard_map.53.own_ref, f32[4,2,128,128]{3,2,1,0:T(8,128)} %copy-done.4, ...), custom_call_target="tpu_custom_call" | custom-call | flops 67108864 | bytes 5242880 | tf_op jit(solution)/shard_map/pallas_call | solution.py:361
  116.2 45.1 %conditional.3 = ((f32[4,2,128,128]{3,2,1,0:T(8,128)S(1)}, f32[4,128]{1,0:T(4,128)S(1)})) conditional(s32[]{:T(128)} %bitcast.3, (s32[128]{0:T(128)S(1)}, f32[4,2,128,128]{3,2,1,0:T(8,128)S(1)}, f32[4,8,128,128]{3,2,1,0:T(8,128)}, f32[32,128,128]{2,1,0:T(8,128)S(1)}, s32[8,128]{1,0:T(8,128)S(1)}, /*index=5*/f32[4,128]{1,0:T(4,128)S(1)}) %tuple.19, ...), branch_computations={%region_2.0_spmd, %region_3.0_spmd} | conditional | flops 1090650112 | bytes 14680104 | solution.py:555
  116.2 1.6 branch_0_fun.10
  117.8 33.3 %collective-permute-start.3 = (f32[128,128]{1,0:T(8,128)}, f32[128,128]{1,0:T(8,128)S(1)}, u32[]{:S(2)}, u32[]{:S(2)}) collective-permute-start(f32[128,128]{1,0:T(8,128)} %get-tuple-element.99), channel_id=1, source_target_pairs={{0,8},{1,9},{2,10},{3,11},{4,12},{5,13},{6,14},{7,15},{8,16},{9,17... | collective-permute-start | bytes 196616 | tf_op jit(solution)/shard_map/cond/branch_0_fun/ppermute | solution.py:543
  151.1 2.9 %collective-permute-start.4 = (f32[128,128]{1,0:T(8,128)}, f32[128,128]{1,0:T(8,128)S(1)}, u32[]{:S(2)}, u32[]{:S(2)}) collective-permute-start(f32[128,128]{1,0:T(8,128)} %get-tuple-element.100), channel_id=1, source_target_pairs={{0,16},{1,17},{2,18},{3,19},{4,20},{5,21},{6,22},{7,23},{8,24},{9,... | collective-permute-start | bytes 196616 | tf_op jit(solution)/shard_map/cond/branch_0_fun/ppermute | solution.py:543
  153.9 3.5 %branch_0_fun.9.acc_in_ref = f32[4,2,128,128]{3,2,1,0:T(8,128)} custom-call(s32[128]{0:T(128)S(1)} %get-tuple-element.93.list_ref, f32[4,2,128,128]{3,2,1,0:T(8,128)S(1)} %get-tuple-element.94.base_ref, f32[4,8,128,128]{3,2,1,0:T(8,128)} %get-tuple-element.95.right_ref, f32[32,128,128]{2,1,0:T(8,128)S(1)} %get-tuple-element.96.got_ref), custom_call_target="tpu_custom_call" | custom-call | flops 1073741824 | bytes 3145728 | tf_op jit(solution)/shard_map/cond/branch_0_fun/pallas_call | solution.py:478
  157.5 0.9 collective-permute-done.5.rest_2_
  159.0 2.2 %branch_0_fun.11 = (f32[4,2,128,128]{3,2,1,0:T(8,128)S(1)}, f32[4,128]{1,0:T(4,128)S(1)}) custom-call(s32[128]{0:T(128)S(1)} %get-tuple-element.93.list_ref, f32[4,2,128,128]{3,2,1,0:T(8,128)} %branch_0_fun.9.acc_in_ref, f32[4,128]{1,0:T(4,128)S(1)} %get-tuple-element.97.totals_ref, f32[4,8,128,128]{3,2,1,0:T(8,128)} %get-tuple-element.95.right_ref, ...), custom_call_target="tpu_custom_call" | custom-call | flops 16777216 | bytes 2097152 | tf_op jit(solution)/shard_map/cond/branch_0_fun/pallas_call | solution.py:490
  161.3 5.9 %collective-permute-start.24 = (f32[4,128]{1,0:T(4,128)S(1)}, f32[4,128]{1,0:T(4,128)S(1)}, u32[]{:S(2)}, u32[]{:S(2)}) collective-permute-start(f32[4,128]{1,0:T(4,128)S(1)} %get-tuple-element.136.rest_0_), channel_id=1, source_target_pairs={{0,96},{32,0},{64,32},{96,64},{1,97},{33,1},{65,33},{97,65},{2,98}... | collective-permute-start | bytes 6152 | tf_op jit(solution)/shard_map/ppermute | solution.py:27
  167.2 0.9 collective-permute-start.22
  168.5 3.8 %collective-permute-done.23.rest_2_ = f32[4,128]{1,0:T(4,128)S(1)} collective-permute-done((f32[4,128]{1,0:T(4,128)S(1)}, f32[4,128]{1,0:T(4,128)S(1)}, u32[]{:S(2)}, u32[]{:S(2)}) %collective-permute-start.23) | collective-permute-done | bytes 2080 | tf_op jit(solution)/shard_map/ppermute | solution.py:27
  172.9 1.5 shard_map.56
  (65 shorter events, 9.7 us)
Async XLA Ops:
  1.1 5.7 %collective-permute-start.12 = (f32[4,128]{1,0:T(4,128)S(1)}, f32[4,128]{1,0:T(4,128)S(1)}, u32[]{:S(2)}, u32[]{:S(2)}) collective-permute-start(f32[4,128]{1,0:T(4,128)S(1)} %shard_map.51.rest_0_), channel_id=1, source_target_pairs={{0,96},{32,0},{64,32},{96,64},{1,97},{33,1},{65,33},{97,65},{2,98}... | collective-permute-start | bytes 6152 | tf_op jit(solution)/shard_map/ppermute | solution.py:27
  4.0 5.1 %collective-permute-start.11 = (f32[4,128]{1,0:T(4,128)S(1)}, f32[4,128]{1,0:T(4,128)S(1)}, u32[]{:S(2)}, u32[]{:S(2)}) collective-permute-start(f32[4,128]{1,0:T(4,128)S(1)} %shard_map.51.rest_0_), channel_id=1, source_target_pairs={{0,64},{32,96},{64,0},{96,32},{1,65},{33,97},{65,1},{97,33},{2,66}... | collective-permute-start | bytes 6152 | tf_op jit(solution)/shard_map/ppermute | solution.py:27
  4.8 4.8 %collective-permute-start.10 = (f32[4,128]{1,0:T(4,128)S(1)}, f32[4,128]{1,0:T(4,128)S(1)}, u32[]{:S(2)}, u32[]{:S(2)}) collective-permute-start(f32[4,128]{1,0:T(4,128)S(1)} %shard_map.51.rest_0_), channel_id=1, source_target_pairs={{0,32},{32,64},{64,96},{96,0},{1,33},{33,65},{65,97},{97,1},{2,34}... | collective-permute-start | bytes 6152 | tf_op jit(solution)/shard_map/ppermute | solution.py:27
  12.1 8.3 %copy-start = (f32[4,2,128,128]{3,2,1,0:T(8,128)S(1)}, f32[4,2,128,128]{3,2,1,0:T(8,128)}, u32[]{:S(2)}) copy-start(f32[4,2,128,128]{3,2,1,0:T(8,128)} %x_ref.3) | copy-start | bytes 1572868
  12.1 41.7 %all-to-all-start.2 = ((f32[32,128,128]{2,1,0:T(8,128)}), f32[32,128,128]{2,1,0:T(8,128)S(1)}, u32[]{:S(2)}, u32[]{:S(2)}) async-start(f32[32,128,128]{2,1,0:T(8,128)} %shard_map.52), calls=%async_computation.2 | async-start | bytes 4194304 | tf_op jit(solution)/shard_map/all_to_all | solution.py:535
  20.4 15.4 %collective-permute-start.7 = (f32[4,2,128,128]{3,2,1,0:T(8,128)S(1)}, f32[4,2,128,128]{3,2,1,0:T(8,128)S(1)}, u32[]{:S(2)}, u32[]{:S(2)}) collective-permute-start(f32[4,2,128,128]{3,2,1,0:T(8,128)S(1)} %copy-done), channel_id=1, source_target_pairs={{0,32},{32,64},{64,96},{96,0},{1,33},{33,65},{65,97},{97,1},{2,34}... | collective-permute-start | bytes 1572872 | tf_op jit(solution)/shard_map/ppermute | solution.py:523
  20.5 15.4 %collective-permute-start.6 = (f32[4,2,128,128]{3,2,1,0:T(8,128)S(1)}, f32[4,2,128,128]{3,2,1,0:T(8,128)S(1)}, u32[]{:S(2)}, u32[]{:S(2)}) collective-permute-start(f32[4,2,128,128]{3,2,1,0:T(8,128)S(1)} %copy-done), channel_id=1, source_target_pairs={{0,96},{32,0},{64,32},{96,64},{1,97},{33,1},{65,33},{97,65},{2,98}... | collective-permute-start | bytes 1572872 | tf_op jit(solution)/shard_map/ppermute | solution.py:524
  35.8 0.8 copy-start.1
  35.8 11.2 %collective-permute-start.8 = (f32[2,2,128,128]{3,2,1,0:T(8,128)S(1)}, f32[2,2,128,128]{3,2,1,0:T(8,128)S(1)}, u32[]{:S(2)}, u32[]{:S(2)}) collective-permute-start(f32[2,2,128,128]{3,2,1,0:T(8,128)S(1)} %slice.24), channel_id=1, source_target_pairs={{0,32},{32,64},{64,96},{96,0},{1,33},{33,65},{65,97},{97,1},{2,34}... | collective-permute-start | bytes 786440 | tf_op jit(solution)/shard_map/ppermute | solution.py:525
  36.6 0.8 copy-start.3
  37.4 9.7 %collective-permute-start.9 = (f32[2,2,128,128]{3,2,1,0:T(8,128)S(1)}, f32[2,2,128,128]{3,2,1,0:T(8,128)}, u32[]{:S(2)}, u32[]{:S(2)}) collective-permute-start(f32[2,2,128,128]{3,2,1,0:T(8,128)S(1)} %slice.25), channel_id=1, source_target_pairs={{0,96},{32,0},{64,32},{96,64},{1,97},{33,1},{65,33},{97,65},{2,98}... | collective-permute-start | bytes 786440 | tf_op jit(solution)/shard_map/ppermute | solution.py:526
  47.1 0.7 copy-start.6
  55.4 8.2 %collective-permute-start = (f32[128,128]{1,0:T(8,128)}, f32[128,128]{1,0:T(8,128)S(1)}, u32[]{:S(2)}, u32[]{:S(2)}) collective-permute-start(f32[128,128]{1,0:T(8,128)} %get-tuple-element.79), channel_id=1, source_target_pairs={{0,8},{1,9},{2,10},{3,11},{4,12},{5,13},{6,14},{7,15},{8,16},{9,17... | collective-permute-start | bytes 196616 | tf_op jit(solution)/shard_map/cond/branch_0_fun/ppermute | solution.py:543
  55.8 7.8 %collective-permute-start.1 = (f32[128,128]{1,0:T(8,128)}, f32[128,128]{1,0:T(8,128)S(1)}, u32[]{:S(2)}, u32[]{:S(2)}) collective-permute-start(f32[128,128]{1,0:T(8,128)} %get-tuple-element.80), channel_id=1, source_target_pairs={{0,16},{1,17},{2,18},{3,19},{4,20},{5,21},{6,22},{7,23},{8,24},{9,... | collective-permute-start | bytes 196616 | tf_op jit(solution)/shard_map/cond/branch_0_fun/ppermute | solution.py:543
  58.5 5.1 %collective-permute-start.2 = (f32[128,128]{1,0:T(8,128)}, f32[128,128]{1,0:T(8,128)S(1)}, u32[]{:S(2)}, u32[]{:S(2)}) collective-permute-start(f32[128,128]{1,0:T(8,128)} %get-tuple-element.81), channel_id=1, source_target_pairs={{0,24},{1,25},{2,26},{3,27},{4,28},{5,29},{6,30},{7,31},{8,0},{9,1... | collective-permute-start | bytes 196616 | tf_op jit(solution)/shard_map/cond/branch_0_fun/ppermute | solution.py:543
  63.6 0.6 copy-start.8
  63.6 0.6 copy-start.10
  63.6 0.7 copy-start.12
  66.5 3.7 %collective-permute-start.21 = (f32[4,128]{1,0:T(4,128)S(1)}, f32[4,128]{1,0:T(4,128)S(1)}, u32[]{:S(2)}, u32[]{:S(2)}) collective-permute-start(f32[4,128]{1,0:T(4,128)S(1)} %get-tuple-element.133.rest_0_), channel_id=1, source_target_pairs={{0,96},{32,0},{64,32},{96,64},{1,97},{33,1},{65,33},{97,65},{2,98}... | collective-permute-start | bytes 6152 | tf_op jit(solution)/shard_map/ppermute | solution.py:27
  67.9 5.1 %collective-permute-start.20 = (f32[4,128]{1,0:T(4,128)S(1)}, f32[4,128]{1,0:T(4,128)S(1)}, u32[]{:S(2)}, u32[]{:S(2)}) collective-permute-start(f32[4,128]{1,0:T(4,128)S(1)} %get-tuple-element.133.rest_0_), channel_id=1, source_target_pairs={{0,64},{32,96},{64,0},{96,32},{1,65},{33,97},{65,1},{97,33},{2,66}... | collective-permute-start | bytes 6152 | tf_op jit(solution)/shard_map/ppermute | solution.py:27
  68.8 4.8 %collective-permute-start.19 = (f32[4,128]{1,0:T(4,128)S(1)}, f32[4,128]{1,0:T(4,128)S(1)}, u32[]{:S(2)}, u32[]{:S(2)}) collective-permute-start(f32[4,128]{1,0:T(4,128)S(1)} %get-tuple-element.133.rest_0_), channel_id=1, source_target_pairs={{0,32},{32,64},{64,96},{96,0},{1,33},{33,65},{65,97},{97,1},{2,34}... | collective-permute-start | bytes 6152 | tf_op jit(solution)/shard_map/ppermute | solution.py:27
  75.8 40.4 %all-to-all-start.3 = ((f32[32,128,128]{2,1,0:T(8,128)}), f32[32,128,128]{2,1,0:T(8,128)S(1)}, u32[]{:S(2)}, u32[]{:S(2)}) async-start(f32[32,128,128]{2,1,0:T(8,128)} %shard_map.55), calls=%async_computation.3 | async-start | bytes 4194304 | tf_op jit(solution)/shard_map/all_to_all | solution.py:535
  81.7 5.1 %collective-permute-start.14 = (f32[4,2,128,128]{3,2,1,0:T(8,128)S(1)}, f32[4,2,128,128]{3,2,1,0:T(8,128)S(1)}, u32[]{:S(2)}, u32[]{:S(2)}) collective-permute-start(f32[4,2,128,128]{3,2,1,0:T(8,128)S(1)} %get-tuple-element.130.held_ref.x_ref), channel_id=1, source_target_pairs={{1,0},{2,1},{3,2},{4,3},{5,4},{6,5},{7,6},{8,7},{9,8},{10,9},{11,1... | collective-permute-start | bytes 1572872 | tf_op jit(solution)/shard_map/ppermute | solution.py:391
  83.0 4.7 %collective-permute-start.13 = (f32[4,2,128,128]{3,2,1,0:T(8,128)S(1)}, f32[4,2,128,128]{3,2,1,0:T(8,128)}, u32[]{:S(2)}, u32[]{:S(2)}) collective-permute-start(f32[4,2,128,128]{3,2,1,0:T(8,128)S(1)} %get-tuple-element.130.held_ref.x_ref), channel_id=1, source_target_pairs={{0,1},{1,2},{2,3},{3,4},{4,5},{5,6},{6,7},{7,8},{8,9},{9,10},{10,1... | collective-permute-start | bytes 1572872 | tf_op jit(solution)/shard_map/ppermute | solution.py:390
  86.9 0.8 copy-start.5
  89.3 10.7 %collective-permute-start.16 = (f32[4,2,128,128]{3,2,1,0:T(8,128)}, f32[4,2,128,128]{3,2,1,0:T(8,128)S(1)}, u32[]{:S(2)}, u32[]{:S(2)}) collective-permute-start(f32[4,2,128,128]{3,2,1,0:T(8,128)} %shard_map.53.own_ref), channel_id=1, source_target_pairs={{0,32},{32,64},{64,96},{96,0},{1,33},{33,65},{65,97},{97,1},{2,34}... | collective-permute-start | bytes 1572872 | tf_op jit(solution)/shard_map/ppermute | solution.py:523
  89.6 11.1 %collective-permute-start.15 = (f32[4,2,128,128]{3,2,1,0:T(8,128)}, f32[4,2,128,128]{3,2,1,0:T(8,128)S(1)}, u32[]{:S(2)}, u32[]{:S(2)}) collective-permute-start(f32[4,2,128,128]{3,2,1,0:T(8,128)} %shard_map.53.own_ref), channel_id=1, source_target_pairs={{0,96},{32,0},{64,32},{96,64},{1,97},{33,1},{65,33},{97,65},{2,98}... | collective-permute-start | bytes 1572872 | tf_op jit(solution)/shard_map/ppermute | solution.py:524
  99.9 9.4 %copy-start.2 = (f32[4,2,128,128]{3,2,1,0:T(8,128)}, f32[4,2,128,128]{3,2,1,0:T(8,128)S(1)}, u32[]{:S(2)}) copy-start(f32[4,2,128,128]{3,2,1,0:T(8,128)S(1)} %collective-permute-done.16.behind_ref) | copy-start | bytes 1572868
  100.7 8.6 %collective-permute-start.17 = (f32[2,2,128,128]{3,2,1,0:T(8,128)}, f32[2,2,128,128]{3,2,1,0:T(8,128)S(1)}, u32[]{:S(2)}, u32[]{:S(2)}) collective-permute-start(f32[2,2,128,128]{3,2,1,0:T(8,128)} %slice.26), channel_id=1, source_target_pairs={{0,32},{32,64},{64,96},{96,0},{1,33},{33,65},{65,97},{97,1},{2,34}... | collective-permute-start | bytes 786440 | tf_op jit(solution)/shard_map/ppermute | solution.py:525
  100.7 0.8 copy-start.4
  102.3 7.4 %collective-permute-start.18 = (f32[2,2,128,128]{3,2,1,0:T(8,128)}, f32[2,2,128,128]{3,2,1,0:T(8,128)}, u32[]{:S(2)}, u32[]{:S(2)}) collective-permute-start(f32[2,2,128,128]{3,2,1,0:T(8,128)} %slice.27), channel_id=1, source_target_pairs={{0,96},{32,0},{64,32},{96,64},{1,97},{33,1},{65,33},{97,65},{2,98}... | collective-permute-start | bytes 786440 | tf_op jit(solution)/shard_map/ppermute | solution.py:526
  109.4 0.7 copy-start.7
  117.8 39.6 %collective-permute-start.3 = (f32[128,128]{1,0:T(8,128)}, f32[128,128]{1,0:T(8,128)S(1)}, u32[]{:S(2)}, u32[]{:S(2)}) collective-permute-start(f32[128,128]{1,0:T(8,128)} %get-tuple-element.99), channel_id=1, source_target_pairs={{0,8},{1,9},{2,10},{3,11},{4,12},{5,13},{6,14},{7,15},{8,16},{9,17... | collective-permute-start | bytes 196616 | tf_op jit(solution)/shard_map/cond/branch_0_fun/ppermute | solution.py:543
  151.1 6.4 %collective-permute-start.4 = (f32[128,128]{1,0:T(8,128)}, f32[128,128]{1,0:T(8,128)S(1)}, u32[]{:S(2)}, u32[]{:S(2)}) collective-permute-start(f32[128,128]{1,0:T(8,128)} %get-tuple-element.100), channel_id=1, source_target_pairs={{0,16},{1,17},{2,18},{3,19},{4,20},{5,21},{6,22},{7,23},{8,24},{9,... | collective-permute-start | bytes 196616 | tf_op jit(solution)/shard_map/cond/branch_0_fun/ppermute | solution.py:543
  153.9 4.5 %collective-permute-start.5 = (f32[128,128]{1,0:T(8,128)}, f32[128,128]{1,0:T(8,128)S(1)}, u32[]{:S(2)}, u32[]{:S(2)}) collective-permute-start(f32[128,128]{1,0:T(8,128)} %get-tuple-element.101), channel_id=1, source_target_pairs={{0,24},{1,25},{2,26},{3,27},{4,28},{5,29},{6,30},{7,31},{8,0},{9,1... | collective-permute-start | bytes 196616 | tf_op jit(solution)/shard_map/cond/branch_0_fun/ppermute | solution.py:543
  157.4 1.0 copy-start.9
  157.4 1.0 copy-start.11
  158.4 0.6 copy-start.13
  161.3 7.2 %collective-permute-start.24 = (f32[4,128]{1,0:T(4,128)S(1)}, f32[4,128]{1,0:T(4,128)S(1)}, u32[]{:S(2)}, u32[]{:S(2)}) collective-permute-start(f32[4,128]{1,0:T(4,128)S(1)} %get-tuple-element.136.rest_0_), channel_id=1, source_target_pairs={{0,96},{32,0},{64,32},{96,64},{1,97},{33,1},{65,33},{97,65},{2,98}... | collective-permute-start | bytes 6152 | tf_op jit(solution)/shard_map/ppermute | solution.py:27
  167.2 5.1 %collective-permute-start.23 = (f32[4,128]{1,0:T(4,128)S(1)}, f32[4,128]{1,0:T(4,128)S(1)}, u32[]{:S(2)}, u32[]{:S(2)}) collective-permute-start(f32[4,128]{1,0:T(4,128)S(1)} %get-tuple-element.136.rest_0_), channel_id=1, source_target_pairs={{0,64},{32,96},{64,0},{96,32},{1,65},{33,97},{65,1},{97,33},{2,66}... | collective-permute-start | bytes 6152 | tf_op jit(solution)/shard_map/ppermute | solution.py:27
  167.2 5.1 %collective-permute-start.22 = (f32[4,128]{1,0:T(4,128)S(1)}, f32[4,128]{1,0:T(4,128)S(1)}, u32[]{:S(2)}, u32[]{:S(2)}) collective-permute-start(f32[4,128]{1,0:T(4,128)S(1)} %get-tuple-element.136.rest_0_), channel_id=1, source_target_pairs={{0,32},{32,64},{64,96},{96,0},{1,33},{33,65},{65,97},{97,1},{2,34}... | collective-permute-start | bytes 6152 | tf_op jit(solution)/shard_map/ppermute | solution.py:27
  168.5 3.8 %copy-start.14 = (f32[4,128]{1,0:T(4,128)}, f32[4,128]{1,0:T(4,128)S(1)}, u32[]{:S(2)}) copy-start(f32[4,128]{1,0:T(4,128)S(1)} %collective-permute-done.24.rest_3_) | copy-start | bytes 6148
  172.3 0.6 copy-start.15
  172.3 0.6 copy-start.16

commit v3 on v2

--- a/solution.py
+++ b/solution.py
@@ -324,28 +324,34 @@
 ):
     cols, share, tile, _ = own_ref.shape
     row = lax.axis_index("prow")
-    rows = right_ref.shape[1] // share
+    rows = in_ref.shape[0] // share
     panel = held_panel(moved, order_ref)
     home = panel // (order_ref.shape[0] // rows)
     half = cols // 2
 
-    for rel in range(4):
-        first = lax.rem(row + rel, rows) * share
-        for j in range(cols):
-            far = far_low_ref.at[j] if j < half else far_high_ref.at[j - half]
-            piece = (own_ref.at[j], ahead_ref.at[j], far, behind_ref.at[j])[rel]
-            right_ref[j, pl.ds(first, share)] = piece[...]
+    def piece(rel, j):
+        far = far_low_ref.at[j] if j < half else far_high_ref.at[j - half]
+        return (own_ref.at[j], ahead_ref.at[j], far, behind_ref.at[j])[rel]
+
     for j in range(cols):
-        whole = right_ref[j].reshape(rows * share * tile, tile)
-        totals_ref[pl.ds(j, 1), :] = jnp.sum(whole, axis=0, keepdims=True)
+        total = jnp.zeros((1, tile), jnp.float32)
+        for rel in range(rows):
+            whole = piece(rel, j)[...].reshape(share * tile, tile)
+            total += jnp.sum(whole, axis=0, keepdims=True)
+        totals_ref[pl.ds(j, 1), :] = total
+    for rel in range(rows):
+
+        @pl.when(lax.rem(row + rel, rows) == home)
+        def _():
+            for j in range(cols):
+                right_ref[j] = piece(rel, j)[...]
 
     @pl.loop(0, cols)
     def _(j):
         base_ref[j] = jnp.zeros((share, tile, tile), jnp.float32)
         for s in range(share):
-            k = home * share + s
             own_column = panel * cols + j
-            column = in_ref[k, own_column]
+            column = in_ref[home * share + s, own_column]
             local = lax.rem(column, cols)
             for t in range(share):
                 hit, at = matched(in_ref, out_pat_ref, row, share, own_column, column, t)
@@ -353,22 +359,23 @@
                 @pl.when(jnp.logical_and(hit, column // cols == panel))
                 def _():
                     left = own_ref[local, at] / totals_ref[pl.ds(local, 1), :]
-                    base_ref[j, t] += dot_exactly(left, right_ref[j, k])
-
-
-def own_products(moved, order, in_pattern, out_pattern, own, gathered):
-    cols, share, tile, _ = own.shape
+                    base_ref[j, t] += dot_exactly(left, right_ref[j, s])
+
+
+def own_products(moved, order, in_pattern, out_pattern, pieces):
+    own = pieces[0]
+    cols, _, tile, _ = own.shape
     return pl.pallas_call(
         functools.partial(own_kernel, moved),
         out_shape=(
             jax.ShapeDtypeStruct(own.shape, jnp.float32),
             jax.ShapeDtypeStruct((cols, tile), jnp.float32),
-            jax.ShapeDtypeStruct((cols, 4 * share, tile, tile), jnp.float32),
         ),
         in_specs=[SMEM] * 3 + [VMEM] * 5,
-        out_specs=(VMEM, VMEM, VMEM),
-        cost_estimate=pl.CostEstimate(flops=1 << 26, bytes_accessed=5 << 20, transcendentals=0),
-    )(order, in_pattern, out_pattern, own, *gathered)
+        out_specs=(VMEM, VMEM),
+        scratch_shapes=[pltpu.VMEM(own.shape, jnp.float32)],
+        cost_estimate=pl.CostEstimate(flops=1 << 26, bytes_accessed=3 << 20, transcendentals=0),
+    )(order, in_pattern, out_pattern, *pieces)
 
 
 def pick_kernel(order_ref, held_ref, below_ref, above_ref, out_ref, sem):
@@ -399,9 +406,12 @@
     )(order, x, from_below, from_above)
 
 
-def add_listed(list_ref, number, first, right_ref, acc_ref, fetch, lefts, rights, sems):
+def add_listed(list_ref, number, first, right_refs, acc_ref, fetch, lefts, rights, sems):
+    own_ref, ahead_ref, behind_ref, far_low_ref, far_high_ref = right_refs
+    row, rows = lax.axis_index("prow"), lax.axis_size("prow")
     share = acc_ref.shape[1]
-    names = right_ref.shape[1]
+    names = rows * share
+    half = far_low_ref.shape[0]
     count = list_ref[number]
 
     def where(i):
@@ -413,34 +423,47 @@
             lax.rem(entry, 32),
         )
 
-    def right_copy(i, j, k):
-        return pltpu.make_async_copy(right_ref.at[j, k], rights.at[i], sems.at[1, i])
+    def wait_for(which, buffers, i):
+        pltpu.make_async_copy(own_ref.at[0, 0], buffers.at[i], sems.at[which, i]).wait()
 
     @pl.loop(0, count)
     def _(i):
         j, k, _, origin = where(i)
-        right_copy(i, j, k).start()
         fetch(i, origin)
+        rel = lax.rem(k // share - row + rows, rows)
+        s = lax.rem(k, share)
+        low = j < half
+        for chosen, ref, at in (
+            (rel == 0, own_ref, j), (rel == 1, ahead_ref, j), (rel == 3, behind_ref, j),
+            (jnp.logical_and(rel == 2, low), far_low_ref, j),
+            (jnp.logical_and(rel == 2, jnp.logical_not(low)), far_high_ref, j - half),
+        ):
+
+            @pl.when(chosen)
+            def _():
+                pltpu.make_async_copy(ref.at[at, s], rights.at[i], sems.at[1, i]).start()
 
     @pl.loop(0, count)
     def _(i):
-        j, k, t, _ = where(i)
-        right_copy(i, j, k).wait()
-        pltpu.make_async_copy(right_ref.at[j, k], lefts.at[i], sems.at[0, i]).wait()
+        j, _, t, _ = where(i)
+        wait_for(1, rights, i)
+        wait_for(0, lefts, i)
         acc_ref[j, t] += dot_exactly(lefts[i], rights[i])
 
 
-def main_kernel(list_ref, base_ref, right_ref, got_ref, acc_ref, lefts, rights, sems):
+def main_kernel(list_ref, base_ref, got_ref, *rest):
+    *right_refs, acc_ref, lefts, rights, sems = rest
     acc_ref[...] = base_ref[...]
 
     def fetch(i, origin):
         pltpu.make_async_copy(got_ref.at[origin], lefts.at[i], sems.at[0, i]).start()
 
-    add_listed(list_ref, 0, FIRSTS, right_ref, acc_ref, fetch, lefts, rights, sems)
-
-
-def last_kernel(depth, list_ref, acc_in_ref, totals_ref, right_ref, *rest):
-    *extra_refs, sq_ref, part_ref, lefts, rights, sems = rest
+    add_listed(list_ref, 0, FIRSTS, right_refs, acc_ref, fetch, lefts, rights, sems)
+
+
+def last_kernel(depth, list_ref, acc_in_ref, totals_ref, *rest):
+    right_refs = rest[:5]
+    *extra_refs, sq_ref, part_ref, lefts, rights, sems = rest[5:]
     cols, share, tile, _ = acc_in_ref.shape
     place = lax.axis_index("pcol")
     sq_ref[...] = acc_in_ref[...]
@@ -456,7 +479,7 @@
             def _():
                 pltpu.make_async_copy(ref, lefts.at[i], sems.at[0, i]).start()
 
-    add_listed(list_ref, 1, SECONDS, right_ref, sq_ref, fetch, lefts, rights, sems)
+    add_listed(list_ref, 1, SECONDS, right_refs, sq_ref, fetch, lefts, rights, sems)
     for j in range(cols):
         value = sq_ref[j].reshape(share * tile, tile) / totals_ref[pl.ds(j, 1), :]
         square = value * value
@@ -464,8 +487,7 @@
         part_ref[pl.ds(j, 1), :] = jnp.sum(square, axis=0, keepdims=True)
 
 
-def list_scratch(right):
-    _, _, tile, _ = right.shape
+def list_scratch(tile):
     most = SECONDS - FIRSTS - 2
     return [
         pltpu.VMEM((most, tile, tile), jnp.float32),
@@ -474,18 +496,18 @@
     ]
 
 
-def main_products(tiles, base, right, got):
+def main_products(tiles, base, pieces, got):
     return pl.pallas_call(
         main_kernel,
         out_shape=jax.ShapeDtypeStruct(base.shape, jnp.float32),
-        in_specs=[SMEM, VMEM, ANY, ANY],
+        in_specs=[SMEM, VMEM, ANY] + [ANY] * 5,
         out_specs=VMEM,
-        scratch_shapes=list_scratch(right),
+        scratch_shapes=list_scratch(base.shape[-1]),
         cost_estimate=pl.CostEstimate(flops=1 << 30, bytes_accessed=3 << 20, transcendentals=0),
-    )(tiles, base, right, got)
-
-
-def last_products(depth, tiles, acc, totals, right, extra):
+    )(tiles, base, got, *pieces)
+
+
+def last_products(depth, tiles, acc, totals, pieces, extra):
     cols, _, tile, _ = acc.shape
     return pl.pallas_call(
         functools.partial(last_kernel, depth),
@@ -493,11 +515,11 @@
             jax.ShapeDtypeStruct(acc.shape, jnp.float32),
             jax.ShapeDtypeStruct((cols, tile), jnp.float32),
         ),
-        in_specs=[SMEM, VMEM, VMEM, ANY] + [ANY] * len(extra),
+        in_specs=[SMEM, VMEM, VMEM] + [ANY] * (5 + len(extra)),
         out_specs=(VMEM, VMEM),
-        scratch_shapes=list_scratch(right),
+        scratch_shapes=list_scratch(tile),
         cost_estimate=pl.CostEstimate(flops=1 << 24, bytes_accessed=2 << 20, transcendentals=0),
-    )(tiles, acc, totals, right, *extra)
+    )(tiles, acc, totals, *pieces, *extra)
 
 
 def divide_kernel(x_ref, *rest):
@@ -534,8 +556,8 @@
     send = prepare(SEND, steps, x, sums, panels)
     got = lax.all_to_all(send, "pcol", 0, 0, tiled=True)
     tiles = tile_list(moved, cols, share, order, steps, in_pattern, out_pattern)
-    gathered = gather_rows(own, rows)
-    base, totals, right = own_products(moved, order, in_pattern, out_pattern, own, gathered)
+    pieces = (own,) + gather_rows(own, rows)
+    base, totals = own_products(moved, order, in_pattern, out_pattern, pieces)
 
     def by_level(_):
         hops = hop_tiles(steps, got)
@@ -543,14 +565,14 @@
             lax.ppermute(tile, "pcol", ring(panels, (step + 1) * depth))
             for step, tile in enumerate(hops)
         )
-        acc = main_products(tiles, base, right, got)
-        return last_products(depth, tiles, acc, totals, right, extra)
+        acc = main_products(tiles, base, pieces, got)
+        return last_products(depth, tiles, acc, totals, pieces, extra)
 
     def by_second(_):
         more = prepare(SECOND, steps, x, sums, panels)
         extra = (lax.all_to_all(more, "pcol", 0, 0, tiled=True),)
-        acc = main_products(tiles, base, right, got)
-        return last_products(depth, tiles, acc, totals, right, extra)
+        acc = main_products(tiles, base, pieces, got)
+        return last_products(depth, tiles, acc, totals, pieces, extra)
 
     return lax.cond(misfit > 0, by_second, by_level, 0)
 

time: 176 us -> 178 us (1.011)
  starting transfers between devices: 86.7 us -> 89.8 us
    ppermute x9, starting transfers between devices: 14.2 us -> 16.9 us  [row_sums(): sums.append(lax.ppermute(partial_value, 'prow', ring(size, step)))]
    pallas_call x2, Pallas kernels: 12.1 us -> 9.99 us  [own_products(): pl.pallas_call(functools.partial(own_kernel, moved), out_shape=(jax.Shape...]
  transfers between devices with their start and end apart: 27 -> 27, of which waited for: 12 -> 10; matrix products, arithmetic and copies ran while one was open for 2% -> 3% of each run, Pallas kernels for 17% -> 16%
where the time goes in v3:
time: 178 us; the launch traced here: 176 us
  starting transfers between devices  89.8 us (50%)
  Pallas kernels  44.5 us (25%)
  waiting for transfers between devices  31.1 us (17%)
  local copies, waits for them, and re-layouts  8.76 us (5%)
    ppermute x6, starting transfers between devices, by_level(): lax.ppermute(tile, 'pcol', ring(panels, (step + 1) * depth))  40.7 us
    ppermute x2, waiting for transfers between devices, gather_rows(): behind = lax.ppermute(own, 'prow', ring(size, 1))  19.2 us
    ppermute x9, starting transfers between devices, row_sums(): sums.append(lax.ppermute(partial_value, 'prow', ring(size, step)))  16.9 us
    all_to_all x2, starting transfers between devices, expand(): got = lax.all_to_all(send, 'pcol', 0, 0, tiled=True)  13.9 us
    ppermute x9, waiting for transfers between devices, row_sums(): sums.append(lax.ppermute(partial_value, 'prow', ring(size, step)))  10.6 us
    pallas_call x2, Pallas kernels, own_products(): pl.pallas_call(functools.partial(own_kernel, moved), out_shape=(jax.Shape...  9.99 us
    pallas_call x2, Pallas kernels, main_products(): pl.pallas_call(main_kernel, out_shape=jax.ShapeDtypeStruct(base.shape, jn...  8.4 us
    ppermute x2, starting transfers between devices, gather_rows(): far_high = lax.ppermute(ahead[half:], 'prow', ring(size, -1))  6.47 us
  transfers between devices with their start and end apart: 27, of which 10 were waited for; matrix products, arithmetic and copies ran while one was open for 3% of the time, Pallas kernels for 16%

profile of v3, /device:TPU:0, one launch (start us, length us, event | category | flops | bytes accessed | tf_op | source)
XLA Modules:
  0.0 175.8 jit_solution(17263244587234534908)
XLA Ops:
  0.0 1.1 shard_map.51.rest_0_
  1.1 2.9 %collective-permute-start.12 = (f32[4,128]{1,0:T(4,128)S(1)}, f32[4,128]{1,0:T(4,128)S(1)}, u32[]{:S(2)}, u32[]{:S(2)}) collective-permute-start(f32[4,128]{1,0:T(4,128)S(1)} %shard_map.51.rest_0_), channel_id=1, source_target_pairs={{0,96},{32,0},{64,32},{96,64},{1,97},{33,1},{65,33},{97,65},{2,98}... | collective-permute-start | bytes 6152 | tf_op jit(solution)/shard_map/ppermute | solution.py:27
  4.0 0.8 collective-permute-start.11
  4.8 0.9 collective-permute-start.10
  5.7 1.1 shard_map.48.plan_ref
  6.8 2.3 %collective-permute-done.11.rest_2_ = f32[4,128]{1,0:T(4,128)S(1)} collective-permute-done((f32[4,128]{1,0:T(4,128)S(1)}, f32[4,128]{1,0:T(4,128)S(1)}, u32[]{:S(2)}, u32[]{:S(2)}) %collective-permute-start.11) | collective-permute-done | bytes 2080 | tf_op jit(solution)/shard_map/ppermute | solution.py:27
  10.3 2.5 %shard_map.52 = f32[32,128,128]{2,1,0:T(8,128)} custom-call(s32[8,128]{1,0:T(8,128)S(1)} %shard_map.48.plan_ref, f32[4,2,128,128]{3,2,1,0:T(8,128)} %x_ref.3, f32[4,128]{1,0:T(4,128)S(1)} %shard_map.51.rest_0_, f32[4,128]{1,0:T(4,128)S(1)} %collective-permute-done.10.rest_1_, f32[4,128]{1,0:T(4,128)S(1)} %collective-permute-done.11.rest_2_, ...), custom_call_target="tpu_custom_call" | custom-call | flops 131072 | bytes 3145728 | tf_op jit(solution)/shard_map/pallas_call | solution.py:204
  12.8 8.3 %all-to-all-start.2 = ((f32[32,128,128]{2,1,0:T(8,128)}), f32[32,128,128]{2,1,0:T(8,128)S(1)}, u32[]{:S(2)}, u32[]{:S(2)}) async-start(f32[32,128,128]{2,1,0:T(8,128)} %shard_map.52), calls=%async_computation.2 | async-start | bytes 4194304 | tf_op jit(solution)/shard_map/all_to_all | solution.py:557
  21.2 3.2 %collective-permute-start.6 = (f32[4,2,128,128]{3,2,1,0:T(8,128)S(1)}, f32[4,2,128,128]{3,2,1,0:T(8,128)S(1)}, u32[]{:S(2)}, u32[]{:S(2)}) collective-permute-start(f32[4,2,128,128]{3,2,1,0:T(8,128)S(1)} %copy-done), channel_id=1, source_target_pairs={{0,96},{32,0},{64,32},{96,64},{1,97},{33,1},{65,33},{97,65},{2,98}... | collective-permute-start | bytes 1572872 | tf_op jit(solution)/shard_map/ppermute | solution.py:546
  24.4 12.1 %collective-permute-done.7.behind_ref = f32[4,2,128,128]{3,2,1,0:T(8,128)S(1)} collective-permute-done((f32[4,2,128,128]{3,2,1,0:T(8,128)S(1)}, f32[4,2,128,128]{3,2,1,0:T(8,128)S(1)}, u32[]{:S(2)}, u32[]{:S(2)}) %collective-permute-start.7) | collective-permute-done | bytes 524320 | tf_op jit(solution)/shard_map/ppermute | solution.py:545
  38.7 3.2 %collective-permute-start.9 = (f32[2,2,128,128]{3,2,1,0:T(8,128)}, f32[2,2,128,128]{3,2,1,0:T(8,128)}, u32[]{:S(2)}, u32[]{:S(2)}) collective-permute-start(f32[2,2,128,128]{3,2,1,0:T(8,128)} %slice.25), channel_id=1, source_target_pairs={{0,96},{32,0},{64,32},{96,64},{1,97},{33,1},{65,33},{97,65},{2,98}... | collective-permute-start | bytes 786440 | tf_op jit(solution)/shard_map/ppermute | solution.py:548
  42.0 2.4 %shard_map.46 = (s32[8,128]{1,0:T(8,128)}, s32[8,128]{1,0:T(8,128)S(1)}) custom-call(s32[1,32]{1,0:T(1,128)} %bitcast.14, s32[8,128]{1,0:T(8,128)} %bitcast.16, s32[8,128]{1,0:T(8,128)} %bitcast.6), custom_call_target="tpu_custom_call" | custom-call | flops 75497472 | bytes 16384 | tf_op jit(solution)/shard_map/pallas_call | solution.py:151
  44.3 1.2 slice.19
  46.1 2.7 %shard_map.49 = s32[128]{0:T(128)} custom-call(s32[32]{0:T(128)} %order_ref.9, s32[8,128]{1,0:T(8,128)S(1)} %shard_map.48.plan_ref, s32[8,128]{1,0:T(8,128)} %bitcast.17, s32[8,128]{1,0:T(8,128)} %bitcast.7), custom_call_target="tpu_custom_call" | custom-call | flops 268435456 | bytes 16384 | tf_op jit(solution)/shard_map/pallas_call | solution.py:311
  48.8 5.0 %shard_map.50 = (f32[4,2,128,128]{3,2,1,0:T(8,128)}, f32[4,128]{1,0:T(4,128)}) custom-call(s32[32]{0:T(128)} %order_ref.9, s32[8,128]{1,0:T(8,128)} %bitcast.18, s32[8,128]{1,0:T(8,128)} %bitcast.8, f32[4,2,128,128]{3,2,1,0:T(8,128)S(1)} %copy-done, f32[4,2,128,128]{3,2,1,0:T(8,128)} %copy-done.1, f32[4,2,128,128]{3,2,1,0:T(8,128)S(1)} %collective-permute-done.7.behind_ref, ...), custom_call_target="tpu_custom_call" | custom-call | flops 67108864 | bytes 3145728 | tf_op jit(solution)/shard_map/pallas_call | solution.py:368
  53.8 13.4 %conditional.2 = ((f32[4,2,128,128]{3,2,1,0:T(8,128)S(1)}, f32[4,128]{1,0:T(4,128)S(1)})) conditional(s32[]{:T(128)} %bitcast.4, (s32[128]{0:T(128)}, f32[4,2,128,128]{3,2,1,0:T(8,128)}, f32[32,128,128]{2,1,0:T(8,128)S(1)}, f32[4,2,128,128]{3,2,1,0:T(8,128)S(1)}, f32[4,2,128,128]{3,2,1,0:T(8,128)}, /*index=5*/f32[4,2,128,128]{3,2,1,0:T(8,128)S(1)}, ...), branch_computations={%region_0.0_spmd, %region_1.0_spmd} | conditional | flops 1090650112 | bytes 14690400 | solution.py:577
  53.8 1.6 branch_0_fun.7
  55.8 2.7 %collective-permute-start.1 = (f32[128,128]{1,0:T(8,128)}, f32[128,128]{1,0:T(8,128)S(1)}, u32[]{:S(2)}, u32[]{:S(2)}) collective-permute-start(f32[128,128]{1,0:T(8,128)} %get-tuple-element.114), channel_id=1, source_target_pairs={{0,16},{1,17},{2,18},{3,19},{4,20},{5,21},{6,22},{7,23},{8,24},{9,... | collective-permute-start | bytes 196616 | tf_op jit(solution)/shard_map/cond/branch_0_fun/ppermute | solution.py:565
  58.5 1.4 collective-permute-start.2
  59.9 4.3 %branch_0_fun.6.acc_in_ref = f32[4,2,128,128]{3,2,1,0:T(8,128)} custom-call(s32[128]{0:T(128)S(1)} %copy-done.18, f32[4,2,128,128]{3,2,1,0:T(8,128)} %get-tuple-element.104.base_ref, f32[32,128,128]{2,1,0:T(8,128)S(1)} %get-tuple-element.105.got_ref, f32[4,2,128,128]{3,2,1,0:T(8,128)S(1)} %get-tuple-element.106.rest_0_, ...), custom_call_target="tpu_custom_call" | custom-call | flops 1073741824 | bytes 3145728 | tf_op jit(solution)/shard_map/cond/branch_0_fun/pallas_call | solution.py:500
  64.9 2.3 %branch_0_fun.8 = (f32[4,2,128,128]{3,2,1,0:T(8,128)S(1)}, f32[4,128]{1,0:T(4,128)S(1)}) custom-call(s32[128]{0:T(128)S(1)} %copy-done.18, f32[4,2,128,128]{3,2,1,0:T(8,128)} %branch_0_fun.6.acc_in_ref, f32[4,128]{1,0:T(4,128)S(1)} %copy-done.14, f32[4,2,128,128]{3,2,1,0:T(8,128)S(1)} %get-tuple-element.106.rest_0_, ...), custom_call_target="tpu_custom_call" | custom-call | flops 16777216 | bytes 2097152 | tf_op jit(solution)/shard_map/cond/branch_0_fun/pallas_call | solution.py:512
  67.2 1.5 collective-permute-start.21
  68.7 1.4 collective-permute-start.20
  70.1 1.3 collective-permute-start.19
  71.4 2.3 %collective-permute-done.20.rest_2_ = f32[4,128]{1,0:T(4,128)S(1)} collective-permute-done((f32[4,128]{1,0:T(4,128)S(1)}, f32[4,128]{1,0:T(4,128)S(1)}, u32[]{:S(2)}, u32[]{:S(2)}) %collective-permute-start.20) | collective-permute-done | bytes 2080 | tf_op jit(solution)/shard_map/ppermute | solution.py:27
  73.7 1.2 collective-permute-done.19.rest_1_
  74.9 2.2 %shard_map.55 = f32[32,128,128]{2,1,0:T(8,128)} custom-call(s32[8,128]{1,0:T(8,128)S(1)} %get-tuple-element.168.plan_ref, f32[4,2,128,128]{3,2,1,0:T(8,128)S(1)} %get-tuple-element.172.held_ref.x_ref, f32[4,128]{1,0:T(4,128)S(1)} %get-tuple-element.174.rest_0_, f32[4,128]{1,0:T(4,128)S(1)} %collective-permute-done.19.rest_1_, ...), custom_call_target="tpu_custom_call" | custom-call | flops 131072 | bytes 3145728 | tf_op jit(solution)/shard_map/pallas_call | solution.py:204
  77.1 5.6 %all-to-all-start.3 = ((f32[32,128,128]{2,1,0:T(8,128)}), f32[32,128,128]{2,1,0:T(8,128)S(1)}, u32[]{:S(2)}, u32[]{:S(2)}) async-start(f32[32,128,128]{2,1,0:T(8,128)} %shard_map.55), calls=%async_computation.3 | async-start | bytes 4194304 | tf_op jit(solution)/shard_map/all_to_all | solution.py:557
  82.7 1.3 collective-permute-start.14
  84.0 3.8 %collective-permute-start.13 = (f32[4,2,128,128]{3,2,1,0:T(8,128)}, f32[4,2,128,128]{3,2,1,0:T(8,128)}, u32[]{:S(2)}, u32[]{:S(2)}) collective-permute-start(f32[4,2,128,128]{3,2,1,0:T(8,128)} %copy-done.3), channel_id=1, source_target_pairs={{0,1},{1,2},{2,3},{3,4},{4,5},{5,6},{6,7},{7,8},{8,9},{9,10},{10,1... | collective-permute-start | bytes 1572872 | tf_op jit(solution)/shard_map/ppermute | solution.py:397
  87.9 1.1 collective-permute-done.13.below_ref
  88.9 1.7 shard_map.53.own_ref
  91.2 2.8 %collective-permute-start.15 = (f32[4,2,128,128]{3,2,1,0:T(8,128)S(1)}, f32[4,2,128,128]{3,2,1,0:T(8,128)S(1)}, u32[]{:S(2)}, u32[]{:S(2)}) collective-permute-start(f32[4,2,128,128]{3,2,1,0:T(8,128)S(1)} %shard_map.53.own_ref), channel_id=1, source_target_pairs={{0,96},{32,0},{64,32},{96,64},{1,97},{33,1},{65,33},{97,65},{2,98}... | collective-permute-start | bytes 1572872 | tf_op jit(solution)/shard_map/ppermute | solution.py:546
  94.0 7.2 %collective-permute-done.16.behind_ref = f32[4,2,128,128]{3,2,1,0:T(8,128)S(1)} collective-permute-done((f32[4,2,128,128]{3,2,1,0:T(8,128)S(1)}, f32[4,2,128,128]{3,2,1,0:T(8,128)S(1)}, u32[]{:S(2)}, u32[]{:S(2)}) %collective-permute-start.16) | collective-permute-done | bytes 524320 | tf_op jit(solution)/shard_map/ppermute | solution.py:545
  101.9 0.8 copy-done.2
  103.4 3.2 %collective-permute-start.18 = (f32[2,2,128,128]{3,2,1,0:T(8,128)}, f32[2,2,128,128]{3,2,1,0:T(8,128)}, u32[]{:S(2)}, u32[]{:S(2)}) collective-permute-start(f32[2,2,128,128]{3,2,1,0:T(8,128)} %slice.27), channel_id=1, source_target_pairs={{0,96},{32,0},{64,32},{96,64},{1,97},{33,1},{65,33},{97,65},{2,98}... | collective-permute-start | bytes 786440 | tf_op jit(solution)/shard_map/ppermute | solution.py:548
  107.9 2.7 %shard_map.47 = s32[128]{0:T(128)} custom-call(s32[32]{0:T(128)} %order_ref.9, s32[8,128]{1,0:T(8,128)S(1)} %get-tuple-element.168.plan_ref, s32[8,128]{1,0:T(8,128)} %bitcast.9, s32[8,128]{1,0:T(8,128)} %bitcast.10), custom_call_target="tpu_custom_call" | custom-call | flops 268435456 | bytes 16384 | tf_op jit(solution)/shard_map/pallas_call | solution.py:311
  110.8 5.0 %shard_map.54 = (f32[4,2,128,128]{3,2,1,0:T(8,128)}, f32[4,128]{1,0:T(4,128)}) custom-call(s32[32]{0:T(128)} %order_ref.9, s32[8,128]{1,0:T(8,128)} %bitcast.11, s32[8,128]{1,0:T(8,128)} %bitcast.12, f32[4,2,128,128]{3,2,1,0:T(8,128)S(1)} %shard_map.53.own_ref, f32[4,2,128,128]{3,2,1,0:T(8,128)} %copy-done.2, ...), custom_call_target="tpu_custom_call" | custom-call | flops 67108864 | bytes 3145728 | tf_op jit(solution)/shard_map/pallas_call | solution.py:368
  115.8 45.4 %conditional.3 = ((f32[4,2,128,128]{3,2,1,0:T(8,128)S(1)}, f32[4,128]{1,0:T(4,128)})) conditional(s32[]{:T(128)} %bitcast.3, (s32[128]{0:T(128)}, f32[4,2,128,128]{3,2,1,0:T(8,128)}, f32[32,128,128]{2,1,0:T(8,128)S(1)}, f32[4,2,128,128]{3,2,1,0:T(8,128)S(1)}, f32[4,2,128,128]{3,2,1,0:T(8,128)}, /*index=5*/f32[4,2,128,128]{3,2,1,0:T(8,128)S(1)}, ...), branch_computations={%region_2.0_spmd, %region_3.0_spmd} | conditional | flops 1090650112 | bytes 14690400 | solution.py:577
  115.8 1.6 branch_0_fun.10
  117.4 33.4 %collective-permute-start.3 = (f32[128,128]{1,0:T(8,128)}, f32[128,128]{1,0:T(8,128)S(1)}, u32[]{:S(2)}, u32[]{:S(2)}) collective-permute-start(f32[128,128]{1,0:T(8,128)} %get-tuple-element.140), channel_id=1, source_target_pairs={{0,8},{1,9},{2,10},{3,11},{4,12},{5,13},{6,14},{7,15},{8,16},{9,17... | collective-permute-start | bytes 196616 | tf_op jit(solution)/shard_map/cond/branch_0_fun/ppermute | solution.py:565
  150.8 2.3 %collective-permute-start.4 = (f32[128,128]{1,0:T(8,128)}, f32[128,128]{1,0:T(8,128)S(1)}, u32[]{:S(2)}, u32[]{:S(2)}) collective-permute-start(f32[128,128]{1,0:T(8,128)} %get-tuple-element.141), channel_id=1, source_target_pairs={{0,16},{1,17},{2,18},{3,19},{4,20},{5,21},{6,22},{7,23},{8,24},{9,... | collective-permute-start | bytes 196616 | tf_op jit(solution)/shard_map/cond/branch_0_fun/ppermute | solution.py:565
  153.6 4.1 %branch_0_fun.9.acc_in_ref = f32[4,2,128,128]{3,2,1,0:T(8,128)} custom-call(s32[128]{0:T(128)S(1)} %copy-done.16, f32[4,2,128,128]{3,2,1,0:T(8,128)} %get-tuple-element.131.base_ref, f32[32,128,128]{2,1,0:T(8,128)S(1)} %get-tuple-element.132.got_ref, f32[4,2,128,128]{3,2,1,0:T(8,128)S(1)} %get-tuple-element.133.rest_0_, ...), custom_call_target="tpu_custom_call" | custom-call | flops 1073741824 | bytes 3145728 | tf_op jit(solution)/shard_map/cond/branch_0_fun/pallas_call | solution.py:500
  158.4 2.8 %branch_0_fun.11 = (f32[4,2,128,128]{3,2,1,0:T(8,128)S(1)}, f32[4,128]{1,0:T(4,128)}) custom-call(s32[128]{0:T(128)S(1)} %copy-done.16, f32[4,2,128,128]{3,2,1,0:T(8,128)} %branch_0_fun.9.acc_in_ref, f32[4,128]{1,0:T(4,128)S(1)} %copy-done.12, f32[4,2,128,128]{3,2,1,0:T(8,128)S(1)} %get-tuple-element.133.rest_0_, ...), custom_call_target="tpu_custom_call" | custom-call | flops 16777216 | bytes 2097152 | tf_op jit(solution)/shard_map/cond/branch_0_fun/pallas_call | solution.py:512
  161.2 7.1 %collective-permute-start.24 = (f32[4,128]{1,0:T(4,128)}, f32[4,128]{1,0:T(4,128)S(1)}, u32[]{:S(2)}, u32[]{:S(2)}) collective-permute-start(f32[4,128]{1,0:T(4,128)} %get-tuple-element.177.rest_0_), channel_id=1, source_target_pairs={{0,96},{32,0},{64,32},{96,64},{1,97},{33,1},{65,33},{97,65},{2,98}... | collective-permute-start | bytes 6152 | tf_op jit(solution)/shard_map/ppermute | solution.py:27
  168.4 0.9 collective-permute-start.22
  169.9 3.8 %collective-permute-done.23.rest_2_ = f32[4,128]{1,0:T(4,128)S(1)} collective-permute-done((f32[4,128]{1,0:T(4,128)}, f32[4,128]{1,0:T(4,128)S(1)}, u32[]{:S(2)}, u32[]{:S(2)}) %collective-permute-start.23) | collective-permute-done | bytes 2080 | tf_op jit(solution)/shard_map/ppermute | solution.py:27
  174.3 1.5 shard_map.56
  (69 shorter events, 9.5 us)
Async XLA Ops:
  1.1 5.7 %collective-permute-start.12 = (f32[4,128]{1,0:T(4,128)S(1)}, f32[4,128]{1,0:T(4,128)S(1)}, u32[]{:S(2)}, u32[]{:S(2)}) collective-permute-start(f32[4,128]{1,0:T(4,128)S(1)} %shard_map.51.rest_0_), channel_id=1, source_target_pairs={{0,96},{32,0},{64,32},{96,64},{1,97},{33,1},{65,33},{97,65},{2,98}... | collective-permute-start | bytes 6152 | tf_op jit(solution)/shard_map/ppermute | solution.py:27
  4.0 5.1 %collective-permute-start.11 = (f32[4,128]{1,0:T(4,128)S(1)}, f32[4,128]{1,0:T(4,128)S(1)}, u32[]{:S(2)}, u32[]{:S(2)}) collective-permute-start(f32[4,128]{1,0:T(4,128)S(1)} %shard_map.51.rest_0_), channel_id=1, source_target_pairs={{0,64},{32,96},{64,0},{96,32},{1,65},{33,97},{65,1},{97,33},{2,66}... | collective-permute-start | bytes 6152 | tf_op jit(solution)/shard_map/ppermute | solution.py:27
  4.8 4.8 %collective-permute-start.10 = (f32[4,128]{1,0:T(4,128)S(1)}, f32[4,128]{1,0:T(4,128)S(1)}, u32[]{:S(2)}, u32[]{:S(2)}) collective-permute-start(f32[4,128]{1,0:T(4,128)S(1)} %shard_map.51.rest_0_), channel_id=1, source_target_pairs={{0,32},{32,64},{64,96},{96,0},{1,33},{33,65},{65,97},{97,1},{2,34}... | collective-permute-start | bytes 6152 | tf_op jit(solution)/shard_map/ppermute | solution.py:27
  9.1 0.6 copy-start.9
  9.7 0.6 copy-start.10
  12.8 8.3 %copy-start = (f32[4,2,128,128]{3,2,1,0:T(8,128)S(1)}, f32[4,2,128,128]{3,2,1,0:T(8,128)}, u32[]{:S(2)}) copy-start(f32[4,2,128,128]{3,2,1,0:T(8,128)} %x_ref.3) | copy-start | bytes 1572868
  12.8 41.0 %all-to-all-start.2 = ((f32[32,128,128]{2,1,0:T(8,128)}), f32[32,128,128]{2,1,0:T(8,128)S(1)}, u32[]{:S(2)}, u32[]{:S(2)}) async-start(f32[32,128,128]{2,1,0:T(8,128)} %shard_map.52), calls=%async_computation.2 | async-start | bytes 4194304 | tf_op jit(solution)/shard_map/all_to_all | solution.py:557
  21.1 15.4 %collective-permute-start.7 = (f32[4,2,128,128]{3,2,1,0:T(8,128)S(1)}, f32[4,2,128,128]{3,2,1,0:T(8,128)S(1)}, u32[]{:S(2)}, u32[]{:S(2)}) collective-permute-start(f32[4,2,128,128]{3,2,1,0:T(8,128)S(1)} %copy-done), channel_id=1, source_target_pairs={{0,32},{32,64},{64,96},{96,0},{1,33},{33,65},{65,97},{97,1},{2,34}... | collective-permute-start | bytes 1572872 | tf_op jit(solution)/shard_map/ppermute | solution.py:545
  21.2 16.0 %collective-permute-start.6 = (f32[4,2,128,128]{3,2,1,0:T(8,128)S(1)}, f32[4,2,128,128]{3,2,1,0:T(8,128)S(1)}, u32[]{:S(2)}, u32[]{:S(2)}) collective-permute-start(f32[4,2,128,128]{3,2,1,0:T(8,128)S(1)} %copy-done), channel_id=1, source_target_pairs={{0,96},{32,0},{64,32},{96,64},{1,97},{33,1},{65,33},{97,65},{2,98}... | collective-permute-start | bytes 1572872 | tf_op jit(solution)/shard_map/ppermute | solution.py:546
  37.2 11.5 %collective-permute-start.8 = (f32[2,2,128,128]{3,2,1,0:T(8,128)}, f32[2,2,128,128]{3,2,1,0:T(8,128)S(1)}, u32[]{:S(2)}, u32[]{:S(2)}) collective-permute-start(f32[2,2,128,128]{3,2,1,0:T(8,128)} %slice.24), channel_id=1, source_target_pairs={{0,32},{32,64},{64,96},{96,0},{1,33},{33,65},{65,97},{97,1},{2,34}... | collective-permute-start | bytes 786440 | tf_op jit(solution)/shard_map/ppermute | solution.py:547
  37.2 0.8 copy-start.1
  38.7 10.0 %collective-permute-start.9 = (f32[2,2,128,128]{3,2,1,0:T(8,128)}, f32[2,2,128,128]{3,2,1,0:T(8,128)}, u32[]{:S(2)}, u32[]{:S(2)}) collective-permute-start(f32[2,2,128,128]{3,2,1,0:T(8,128)} %slice.25), channel_id=1, source_target_pairs={{0,96},{32,0},{64,32},{96,64},{1,97},{33,1},{65,33},{97,65},{2,98}... | collective-permute-start | bytes 786440 | tf_op jit(solution)/shard_map/ppermute | solution.py:548
  53.8 6.1 %copy-start.18 = (s32[128]{0:T(128)S(1)}, s32[128]{0:T(128)}, u32[]{:S(2)}) copy-start(s32[128]{0:T(128)} %get-tuple-element.103.list_ref) | copy-start | bytes 1540 | tf_op jit(solution)/shard_map/cond
  55.4 8.9 %collective-permute-start = (f32[128,128]{1,0:T(8,128)}, f32[128,128]{1,0:T(8,128)S(1)}, u32[]{:S(2)}, u32[]{:S(2)}) collective-permute-start(f32[128,128]{1,0:T(8,128)} %get-tuple-element.113), channel_id=1, source_target_pairs={{0,8},{1,9},{2,10},{3,11},{4,12},{5,13},{6,14},{7,15},{8,16},{9,17... | collective-permute-start | bytes 196616 | tf_op jit(solution)/shard_map/cond/branch_0_fun/ppermute | solution.py:565
  55.8 8.5 %collective-permute-start.1 = (f32[128,128]{1,0:T(8,128)}, f32[128,128]{1,0:T(8,128)S(1)}, u32[]{:S(2)}, u32[]{:S(2)}) collective-permute-start(f32[128,128]{1,0:T(8,128)} %get-tuple-element.114), channel_id=1, source_target_pairs={{0,16},{1,17},{2,18},{3,19},{4,20},{5,21},{6,22},{7,23},{8,24},{9,... | collective-permute-start | bytes 196616 | tf_op jit(solution)/shard_map/cond/branch_0_fun/ppermute | solution.py:565
  58.5 5.8 %collective-permute-start.2 = (f32[128,128]{1,0:T(8,128)}, f32[128,128]{1,0:T(8,128)}, u32[]{:S(2)}, u32[]{:S(2)}) collective-permute-start(f32[128,128]{1,0:T(8,128)} %get-tuple-element.115), channel_id=1, source_target_pairs={{0,24},{1,25},{2,26},{3,27},{4,28},{5,29},{6,30},{7,31},{8,0},{9,1... | collective-permute-start | bytes 196616 | tf_op jit(solution)/shard_map/cond/branch_0_fun/ppermute | solution.py:565
  59.9 5.0 %copy-start.14 = (f32[4,128]{1,0:T(4,128)S(1)}, f32[4,128]{1,0:T(4,128)}, u32[]{:S(2)}) copy-start(f32[4,128]{1,0:T(4,128)} %get-tuple-element.111.totals_ref) | copy-start | bytes 6148 | tf_op jit(solution)/shard_map/cond
  64.2 0.6 copy-start.5
  64.3 0.6 copy-start.7
  67.2 10.0 %copy-start.3 = (f32[4,2,128,128]{3,2,1,0:T(8,128)}, f32[4,2,128,128]{3,2,1,0:T(8,128)S(1)}, u32[]{:S(2)}) copy-start(f32[4,2,128,128]{3,2,1,0:T(8,128)S(1)} %get-tuple-element.172.held_ref.x_ref) | copy-start | bytes 1572868
  67.2 10.0 %copy-start.11 = (f32[4,128]{1,0:T(4,128)}, f32[4,128]{1,0:T(4,128)S(1)}, u32[]{:S(2)}) copy-start(f32[4,128]{1,0:T(4,128)S(1)} %get-tuple-element.174.rest_0_) | copy-start | bytes 6148
  67.2 4.3 %collective-permute-start.21 = (f32[4,128]{1,0:T(4,128)S(1)}, f32[4,128]{1,0:T(4,128)S(1)}, u32[]{:S(2)}, u32[]{:S(2)}) collective-permute-start(f32[4,128]{1,0:T(4,128)S(1)} %get-tuple-element.174.rest_0_), channel_id=1, source_target_pairs={{0,96},{32,0},{64,32},{96,64},{1,97},{33,1},{65,33},{97,65},{2,98}... | collective-permute-start | bytes 6152 | tf_op jit(solution)/shard_map/ppermute | solution.py:27
  68.7 5.1 %collective-permute-start.20 = (f32[4,128]{1,0:T(4,128)S(1)}, f32[4,128]{1,0:T(4,128)S(1)}, u32[]{:S(2)}, u32[]{:S(2)}) collective-permute-start(f32[4,128]{1,0:T(4,128)S(1)} %get-tuple-element.174.rest_0_), channel_id=1, source_target_pairs={{0,64},{32,96},{64,0},{96,32},{1,65},{33,97},{65,1},{97,33},{2,66}... | collective-permute-start | bytes 6152 | tf_op jit(solution)/shard_map/ppermute | solution.py:27
  70.1 4.8 %collective-permute-start.19 = (f32[4,128]{1,0:T(4,128)S(1)}, f32[4,128]{1,0:T(4,128)S(1)}, u32[]{:S(2)}, u32[]{:S(2)}) collective-permute-start(f32[4,128]{1,0:T(4,128)S(1)} %get-tuple-element.174.rest_0_), channel_id=1, source_target_pairs={{0,32},{32,64},{64,96},{96,0},{1,33},{33,65},{65,97},{97,1},{2,34}... | collective-permute-start | bytes 6152 | tf_op jit(solution)/shard_map/ppermute | solution.py:27
  77.1 38.7 %all-to-all-start.3 = ((f32[32,128,128]{2,1,0:T(8,128)}), f32[32,128,128]{2,1,0:T(8,128)S(1)}, u32[]{:S(2)}, u32[]{:S(2)}) async-start(f32[32,128,128]{2,1,0:T(8,128)} %shard_map.55), calls=%async_computation.3 | async-start | bytes 4194304 | tf_op jit(solution)/shard_map/all_to_all | solution.py:557
  82.7 5.1 %collective-permute-start.14 = (f32[4,2,128,128]{3,2,1,0:T(8,128)}, f32[4,2,128,128]{3,2,1,0:T(8,128)S(1)}, u32[]{:S(2)}, u32[]{:S(2)}) collective-permute-start(f32[4,2,128,128]{3,2,1,0:T(8,128)} %copy-done.3), channel_id=1, source_target_pairs={{1,0},{2,1},{3,2},{4,3},{5,4},{6,5},{7,6},{8,7},{9,8},{10,9},{11,1... | collective-permute-start | bytes 1572872 | tf_op jit(solution)/shard_map/ppermute | solution.py:398
  84.0 4.9 %collective-permute-start.13 = (f32[4,2,128,128]{3,2,1,0:T(8,128)}, f32[4,2,128,128]{3,2,1,0:T(8,128)}, u32[]{:S(2)}, u32[]{:S(2)}) collective-permute-start(f32[4,2,128,128]{3,2,1,0:T(8,128)} %copy-done.3), channel_id=1, source_target_pairs={{0,1},{1,2},{2,3},{3,4},{4,5},{5,6},{6,7},{7,8},{8,9},{9,10},{10,1... | collective-permute-start | bytes 1572872 | tf_op jit(solution)/shard_map/ppermute | solution.py:397
  87.9 1.1 copy-start.4
  90.7 10.5 %collective-permute-start.16 = (f32[4,2,128,128]{3,2,1,0:T(8,128)S(1)}, f32[4,2,128,128]{3,2,1,0:T(8,128)S(1)}, u32[]{:S(2)}, u32[]{:S(2)}) collective-permute-start(f32[4,2,128,128]{3,2,1,0:T(8,128)S(1)} %shard_map.53.own_ref), channel_id=1, source_target_pairs={{0,32},{32,64},{64,96},{96,0},{1,33},{33,65},{65,97},{97,1},{2,34}... | collective-permute-start | bytes 1572872 | tf_op jit(solution)/shard_map/ppermute | solution.py:545
  91.2 10.7 %collective-permute-start.15 = (f32[4,2,128,128]{3,2,1,0:T(8,128)S(1)}, f32[4,2,128,128]{3,2,1,0:T(8,128)S(1)}, u32[]{:S(2)}, u32[]{:S(2)}) collective-permute-start(f32[4,2,128,128]{3,2,1,0:T(8,128)S(1)} %shard_map.53.own_ref), channel_id=1, source_target_pairs={{0,96},{32,0},{64,32},{96,64},{1,97},{33,1},{65,33},{97,65},{2,98}... | collective-permute-start | bytes 1572872 | tf_op jit(solution)/shard_map/ppermute | solution.py:546
  101.8 8.8 %collective-permute-start.17 = (f32[2,2,128,128]{3,2,1,0:T(8,128)}, f32[2,2,128,128]{3,2,1,0:T(8,128)S(1)}, u32[]{:S(2)}, u32[]{:S(2)}) collective-permute-start(f32[2,2,128,128]{3,2,1,0:T(8,128)} %slice.26), channel_id=1, source_target_pairs={{0,32},{32,64},{64,96},{96,0},{1,33},{33,65},{65,97},{97,1},{2,34}... | collective-permute-start | bytes 786440 | tf_op jit(solution)/shard_map/ppermute | solution.py:547
  101.9 0.8 copy-start.2
  103.4 7.4 %collective-permute-start.18 = (f32[2,2,128,128]{3,2,1,0:T(8,128)}, f32[2,2,128,128]{3,2,1,0:T(8,128)}, u32[]{:S(2)}, u32[]{:S(2)}) collective-permute-start(f32[2,2,128,128]{3,2,1,0:T(8,128)} %slice.27), channel_id=1, source_target_pairs={{0,96},{32,0},{64,32},{96,64},{1,97},{33,1},{65,33},{97,65},{2,98}... | collective-permute-start | bytes 786440 | tf_op jit(solution)/shard_map/ppermute | solution.py:548
  115.8 37.8 %copy-start.16 = (s32[128]{0:T(128)S(1)}, s32[128]{0:T(128)}, u32[]{:S(2)}) copy-start(s32[128]{0:T(128)} %get-tuple-element.130.list_ref) | copy-start | bytes 1540 | tf_op jit(solution)/shard_map/cond
  117.4 40.3 %collective-permute-start.3 = (f32[128,128]{1,0:T(8,128)}, f32[128,128]{1,0:T(8,128)S(1)}, u32[]{:S(2)}, u32[]{:S(2)}) collective-permute-start(f32[128,128]{1,0:T(8,128)} %get-tuple-element.140), channel_id=1, source_target_pairs={{0,8},{1,9},{2,10},{3,11},{4,12},{5,13},{6,14},{7,15},{8,16},{9,17... | collective-permute-start | bytes 196616 | tf_op jit(solution)/shard_map/cond/branch_0_fun/ppermute | solution.py:565
  150.8 6.9 %collective-permute-start.4 = (f32[128,128]{1,0:T(8,128)}, f32[128,128]{1,0:T(8,128)S(1)}, u32[]{:S(2)}, u32[]{:S(2)}) collective-permute-start(f32[128,128]{1,0:T(8,128)} %get-tuple-element.141), channel_id=1, source_target_pairs={{0,16},{1,17},{2,18},{3,19},{4,20},{5,21},{6,22},{7,23},{8,24},{9,... | collective-permute-start | bytes 196616 | tf_op jit(solution)/shard_map/cond/branch_0_fun/ppermute | solution.py:565
  153.2 4.6 %collective-permute-start.5 = (f32[128,128]{1,0:T(8,128)}, f32[128,128]{1,0:T(8,128)}, u32[]{:S(2)}, u32[]{:S(2)}) collective-permute-start(f32[128,128]{1,0:T(8,128)} %get-tuple-element.142), channel_id=1, source_target_pairs={{0,24},{1,25},{2,26},{3,27},{4,28},{5,29},{6,30},{7,31},{8,0},{9,1... | collective-permute-start | bytes 196616 | tf_op jit(solution)/shard_map/cond/branch_0_fun/ppermute | solution.py:565
  153.6 4.8 %copy-start.12 = (f32[4,128]{1,0:T(4,128)S(1)}, f32[4,128]{1,0:T(4,128)}, u32[]{:S(2)}) copy-start(f32[4,128]{1,0:T(4,128)} %get-tuple-element.138.totals_ref) | copy-start | bytes 6148 | tf_op jit(solution)/shard_map/cond
  157.7 0.6 copy-start.6
  157.8 0.6 copy-start.8
  161.2 8.6 %collective-permute-start.24 = (f32[4,128]{1,0:T(4,128)}, f32[4,128]{1,0:T(4,128)S(1)}, u32[]{:S(2)}, u32[]{:S(2)}) collective-permute-start(f32[4,128]{1,0:T(4,128)} %get-tuple-element.177.rest_0_), channel_id=1, source_target_pairs={{0,96},{32,0},{64,32},{96,64},{1,97},{33,1},{65,33},{97,65},{2,98}... | collective-permute-start | bytes 6152 | tf_op jit(solution)/shard_map/ppermute | solution.py:27
  168.4 5.3 %collective-permute-start.23 = (f32[4,128]{1,0:T(4,128)}, f32[4,128]{1,0:T(4,128)S(1)}, u32[]{:S(2)}, u32[]{:S(2)}) collective-permute-start(f32[4,128]{1,0:T(4,128)} %get-tuple-element.177.rest_0_), channel_id=1, source_target_pairs={{0,64},{32,96},{64,0},{96,32},{1,65},{33,97},{65,1},{97,33},{2,66}... | collective-permute-start | bytes 6152 | tf_op jit(solution)/shard_map/ppermute | solution.py:27
  168.4 5.3 %collective-permute-start.22 = (f32[4,128]{1,0:T(4,128)}, f32[4,128]{1,0:T(4,128)S(1)}, u32[]{:S(2)}, u32[]{:S(2)}) collective-permute-start(f32[4,128]{1,0:T(4,128)} %get-tuple-element.177.rest_0_), channel_id=1, source_target_pairs={{0,32},{32,64},{64,96},{96,0},{1,33},{33,65},{65,97},{97,1},{2,34}... | collective-permute-start | bytes 6152 | tf_op jit(solution)/shard_map/ppermute | solution.py:27
  169.9 3.8 %copy-start.20 = (f32[4,128]{1,0:T(4,128)}, f32[4,128]{1,0:T(4,128)S(1)}, u32[]{:S(2)}) copy-start(f32[4,128]{1,0:T(4,128)S(1)} %collective-permute-done.24.rest_3_) | copy-start | bytes 6148
  173.7 0.6 copy-start.21
  173.7 0.6 copy-start.22

commit v4 on v2

--- a/solution.py
+++ b/solution.py
@@ -29,7 +29,7 @@
 
 
 def plan_kernel(
-    moved, steps, whole, order_ref, in_ref, out_ref, plan_ref, grid_ref, line_ref
+    permuted, steps, whole, order_ref, in_ref, out_ref, plan_ref, grid_ref, line_ref
 ):
     place, row = lax.axis_index("pcol"), lax.axis_index("prow")
     panels_all = order_ref.shape[1]
@@ -38,13 +38,15 @@
     shape = (LANES, LANES)
     down = lax.broadcasted_iota(jnp.int32, shape, 0)
     along = lax.broadcasted_iota(jnp.int32, shape, 1)
-    if moved:
-        line_ref[...] = jnp.full(line_ref.shape, -2, jnp.int32)
-        line_ref[:1, :panels_all] = order_ref[...]
-        held = jnp.broadcast_to(line_ref[:1, :], shape)
+    line_ref[...] = jnp.full(line_ref.shape, -2, jnp.int32)
+    line_ref[:1, :panels_all] = order_ref[...]
+    held = jnp.broadcast_to(line_ref[:1, :], shape)
+    if permuted:
+        diagonal = jnp.where(down == along, held, 0)
+        source = jnp.broadcast_to(jnp.sum(diagonal, axis=1, keepdims=True), shape)
+        source = jnp.where(down < panels_all, source, -1)
     else:
-        held = jnp.where(along < panels_all, along, -2)
-    source = jnp.where(down < panels_all, down, -1)
+        source = jnp.where(down < panels_all, down, -1)
     names = in_ref[...]
     panels, inside = names // 4, lax.rem(names, 4)
     groups = (down // 4 == held).astype(jnp.bfloat16)
@@ -139,10 +141,10 @@
 
 def plans_kernel(parts, order_ref, first_ref, second_ref, *rest):
     *plan_refs, grid_ref, line_ref = rest
-    for (moved, steps, whole), plan_ref in zip(parts, plan_refs):
-        in_ref = second_ref if moved else first_ref
+    for (permuted, steps, whole), plan_ref in zip(parts, plan_refs):
+        in_ref = second_ref if permuted else first_ref
         plan_kernel(
-            moved, steps, whole, order_ref, in_ref, second_ref, plan_ref, grid_ref, line_ref
+            permuted, steps, whole, order_ref, in_ref, second_ref, plan_ref, grid_ref, line_ref
         )
 
 
@@ -268,24 +270,20 @@
     return hit, at
 
 
-def held_panel(moved, order_ref):
-    place = lax.axis_index("pcol")
-    return order_ref[place] if moved else place
-
-
-def list_kernel(moved, cols, share, order_ref, plan_ref, in_ref, out_pat_ref, list_ref):
+def list_kernel(permuted, cols, share, order_ref, plan_ref, in_ref, out_pat_ref, list_ref):
     row = lax.axis_index("prow")
-    panel = held_panel(moved, order_ref)
+    panel = order_ref[lax.axis_index("pcol")]
     names = in_ref.shape[0]
 
     def remote(place_of, counts):
         own_column = panel * cols + place_of // names
         column = in_ref[lax.rem(place_of, names), own_column]
-        origin = column // cols
+        source = column // cols
+        origin = order_ref[source] if permuted else source
         firsts, seconds = counts
         for t in range(share):
             hit, at = matched(in_ref, out_pat_ref, row, share, own_column, column, t)
-            hit = jnp.logical_and(hit, origin != panel)
+            hit = jnp.logical_and(hit, source != panel)
             extra = jnp.logical_and(hit, jnp.logical_and(at == 1, plan_ref[FIRST, origin] > 0))
             simple = jnp.logical_and(hit, jnp.logical_not(extra))
             entry = (place_of * share + t) * 32 + origin
@@ -307,9 +305,9 @@
     list_ref[1] = seconds
 
 
-def tile_list(moved, cols, share, order, steps, in_pattern, out_pattern):
-    return pl.pallas_call(
-        functools.partial(list_kernel, moved, cols, share),
+def tile_list(permuted, cols, share, order, steps, in_pattern, out_pattern):
+    return pl.pallas_call(
+        functools.partial(list_kernel, permuted, cols, share),
         out_shape=jax.ShapeDtypeStruct((LIST,), jnp.int32),
         in_specs=[SMEM] * 4,
         out_specs=SMEM,
@@ -318,14 +316,14 @@
 
 
 def own_kernel(
-    moved, order_ref, in_ref, out_pat_ref,
+    order_ref, in_ref, out_pat_ref,
     own_ref, ahead_ref, behind_ref, far_low_ref, far_high_ref,
     base_ref, totals_ref, right_ref,
 ):
     cols, share, tile, _ = own_ref.shape
     row = lax.axis_index("prow")
     rows = right_ref.shape[1] // share
-    panel = held_panel(moved, order_ref)
+    panel = order_ref[lax.axis_index("pcol")]
     home = panel // (order_ref.shape[0] // rows)
     half = cols // 2
 
@@ -356,10 +354,10 @@
                     base_ref[j, t] += dot_exactly(left, right_ref[j, k])
 
 
-def own_products(moved, order, in_pattern, out_pattern, own, gathered):
+def own_products(order, in_pattern, out_pattern, own, gathered):
     cols, share, tile, _ = own.shape
     return pl.pallas_call(
-        functools.partial(own_kernel, moved),
+        own_kernel,
         out_shape=(
             jax.ShapeDtypeStruct(own.shape, jnp.float32),
             jax.ShapeDtypeStruct((cols, tile), jnp.float32),
@@ -527,15 +525,15 @@
     return ahead, behind, far_low, far_high
 
 
-def expand(moved, order, steps, misfit, in_pattern, out_pattern, x, sums, own, rows):
+def expand(permuted, order, steps, misfit, in_pattern, out_pattern, x, sums, own, rows):
     cols, share = x.shape[:2]
     panels = order.shape[0]
     depth = panels // 4
     send = prepare(SEND, steps, x, sums, panels)
     got = lax.all_to_all(send, "pcol", 0, 0, tiled=True)
-    tiles = tile_list(moved, cols, share, order, steps, in_pattern, out_pattern)
+    tiles = tile_list(permuted, cols, share, order, steps, in_pattern, out_pattern)
     gathered = gather_rows(own, rows)
-    base, totals, right = own_products(moved, order, in_pattern, out_pattern, own, gathered)
+    base, totals, right = own_products(order, in_pattern, out_pattern, own, gathered)
 
     def by_level(_):
         hops = hop_tiles(steps, got)
@@ -566,12 +564,12 @@
     check, second_plan = plans(((False, False, True), (True, True, True)), *tables)
     square, part = expand(
         False, order, first_plan, check[MISFIT, 0], pattern_rows, kept_rows,
-        match_tiles, sums, match_tiles, rows,
+        match_tiles, sums, shifted(order, match_tiles), rows,
     )
     sums = row_sums(part, rows)
     square, part = expand(
         True, order, second_plan, second_plan[MISFIT, 0], kept_rows, kept_rows,
-        square, sums, shifted(order, square), rows,
+        square, sums, square, rows,
     )
     return divided(square, row_sums(part, rows))
 

time: 176 us -> 177 us (level)
  transfers between devices with their start and end apart: 27 -> 27, of which waited for: 12 -> 11; matrix products, arithmetic and copies ran while one was open for 2% -> 2% of each run, Pallas kernels for 17% -> 17%
where the time goes in v4:
time: 177 us; the launch traced here: 175 us
  starting transfers between devices  87.1 us (49%)
  Pallas kernels  44.8 us (25%)
  waiting for transfers between devices  32.7 us (18%)
  local copies, waits for them, and re-layouts  8.3 us (5%)
    ppermute x6, starting transfers between devices, by_level(): lax.ppermute(tile, 'pcol', ring(panels, (step + 1) * depth))  39.8 us
    ppermute x2, waiting for transfers between devices, gather_rows(): behind = lax.ppermute(own, 'prow', ring(size, 1))  19.4 us
    ppermute x9, starting transfers between devices, row_sums(): sums.append(lax.ppermute(partial_value, 'prow', ring(size, step)))  15 us
    all_to_all x2, starting transfers between devices, expand(): got = lax.all_to_all(send, 'pcol', 0, 0, tiled=True)  13.9 us
    pallas_call x2, Pallas kernels, own_products(): pl.pallas_call(own_kernel, out_shape=(jax.ShapeDtypeStruct(own.shape, jnp...  12.1 us
    ppermute x9, waiting for transfers between devices, row_sums(): sums.append(lax.ppermute(partial_value, 'prow', ring(size, step)))  11.1 us
    pallas_call x2, Pallas kernels, main_products(): pl.pallas_call(main_kernel, out_shape=jax.ShapeDtypeStruct(base.shape, jn...  7.14 us
    ppermute x2, starting transfers between devices, gather_rows(): far_high = lax.ppermute(ahead[half:], 'prow', ring(size, -1))  6.52 us
  transfers between devices with their start and end apart: 27, of which 11 were waited for; matrix products, arithmetic and copies ran while one was open for 2% of the time, Pallas kernels for 17%

profile of v4, /device:TPU:0, one launch (start us, length us, event | category | flops | bytes accessed | tf_op | source)
XLA Modules:
  0.0 174.5 jit_solution(17760310395937497296)
XLA Ops:
  0.0 1.1 shard_map.52.rest_0_
  1.1 2.9 %collective-permute-start.14 = (f32[4,128]{1,0:T(4,128)S(1)}, f32[4,128]{1,0:T(4,128)S(1)}, u32[]{:S(2)}, u32[]{:S(2)}) collective-permute-start(f32[4,128]{1,0:T(4,128)S(1)} %shard_map.52.rest_0_), channel_id=1, source_target_pairs={{0,96},{32,0},{64,32},{96,64},{1,97},{33,1},{65,33},{97,65},{2,98}... | collective-permute-start | bytes 6152 | tf_op jit(solution)/shard_map/ppermute | solution.py:27
  4.0 0.8 collective-permute-start.13
  4.8 0.9 collective-permute-start.12
  5.7 1.1 shard_map.48.plan_ref
  6.8 2.3 %collective-permute-done.13.rest_2_ = f32[4,128]{1,0:T(4,128)S(1)} collective-permute-done((f32[4,128]{1,0:T(4,128)S(1)}, f32[4,128]{1,0:T(4,128)S(1)}, u32[]{:S(2)}, u32[]{:S(2)}) %collective-permute-start.13) | collective-permute-done | bytes 2080 | tf_op jit(solution)/shard_map/ppermute | solution.py:27
  9.6 2.5 %shard_map.53 = f32[32,128,128]{2,1,0:T(8,128)} custom-call(s32[8,128]{1,0:T(8,128)S(1)} %shard_map.48.plan_ref, f32[4,2,128,128]{3,2,1,0:T(8,128)} %x_ref.3, f32[4,128]{1,0:T(4,128)S(1)} %shard_map.52.rest_0_, f32[4,128]{1,0:T(4,128)S(1)} %collective-permute-done.12.rest_1_, f32[4,128]{1,0:T(4,128)S(1)} %collective-permute-done.13.rest_2_, ...), custom_call_target="tpu_custom_call" | custom-call | flops 131072 | bytes 3145728 | tf_op jit(solution)/shard_map/pallas_call | solution.py:206
  12.1 8.3 %all-to-all-start.2 = ((f32[32,128,128]{2,1,0:T(8,128)}), f32[32,128,128]{2,1,0:T(8,128)S(1)}, u32[]{:S(2)}, u32[]{:S(2)}) async-start(f32[32,128,128]{2,1,0:T(8,128)} %shard_map.53), calls=%async_computation.2 | async-start | bytes 4194304 | tf_op jit(solution)/shard_map/all_to_all | solution.py:533
  20.4 1.3 collective-permute-start.7
  21.7 3.8 %collective-permute-start.6 = (f32[4,2,128,128]{3,2,1,0:T(8,128)S(1)}, f32[4,2,128,128]{3,2,1,0:T(8,128)}, u32[]{:S(2)}, u32[]{:S(2)}) collective-permute-start(f32[4,2,128,128]{3,2,1,0:T(8,128)S(1)} %copy-done), channel_id=1, source_target_pairs={{0,1},{1,2},{2,3},{3,4},{4,5},{5,6},{6,7},{7,8},{8,9},{9,10},{10,1... | collective-permute-start | bytes 1572872 | tf_op jit(solution)/shard_map/ppermute | solution.py:388
  25.6 0.8 collective-permute-done.6.below_ref
  26.4 1.5 shard_map.50.own_ref
  28.1 3.2 %collective-permute-start.8 = (f32[4,2,128,128]{3,2,1,0:T(8,128)}, f32[4,2,128,128]{3,2,1,0:T(8,128)S(1)}, u32[]{:S(2)}, u32[]{:S(2)}) collective-permute-start(f32[4,2,128,128]{3,2,1,0:T(8,128)} %shard_map.50.own_ref), channel_id=1, source_target_pairs={{0,96},{32,0},{64,32},{96,64},{1,97},{33,1},{65,33},{97,65},{2,98}... | collective-permute-start | bytes 1572872 | tf_op jit(solution)/shard_map/ppermute | solution.py:522
  31.3 7.4 %collective-permute-done.9.behind_ref = f32[4,2,128,128]{3,2,1,0:T(8,128)S(1)} collective-permute-done((f32[4,2,128,128]{3,2,1,0:T(8,128)}, f32[4,2,128,128]{3,2,1,0:T(8,128)S(1)}, u32[]{:S(2)}, u32[]{:S(2)}) %collective-permute-start.9) | collective-permute-done | bytes 524320 | tf_op jit(solution)/shard_map/ppermute | solution.py:521
  40.4 3.3 %collective-permute-start.11 = (f32[2,2,128,128]{3,2,1,0:T(8,128)S(1)}, f32[2,2,128,128]{3,2,1,0:T(8,128)}, u32[]{:S(2)}, u32[]{:S(2)}) collective-permute-start(f32[2,2,128,128]{3,2,1,0:T(8,128)S(1)} %slice.25), channel_id=1, source_target_pairs={{0,96},{32,0},{64,32},{96,64},{1,97},{33,1},{65,33},{97,65},{2,98}... | collective-permute-start | bytes 786440 | tf_op jit(solution)/shard_map/ppermute | solution.py:524
  43.7 2.4 %shard_map.46 = (s32[8,128]{1,0:T(8,128)}, s32[8,128]{1,0:T(8,128)S(1)}) custom-call(s32[1,32]{1,0:T(1,128)} %bitcast.14, s32[8,128]{1,0:T(8,128)} %bitcast.16, s32[8,128]{1,0:T(8,128)} %bitcast.6), custom_call_target="tpu_custom_call" | custom-call | flops 75497472 | bytes 16384 | tf_op jit(solution)/shard_map/pallas_call | solution.py:153
  46.0 1.3 slice.19
  48.0 2.8 %shard_map.49 = s32[128]{0:T(128)S(1)} custom-call(s32[32]{0:T(128)} %order_ref.9, s32[8,128]{1,0:T(8,128)S(1)} %shard_map.48.plan_ref, s32[8,128]{1,0:T(8,128)} %bitcast.17, s32[8,128]{1,0:T(8,128)} %bitcast.7), custom_call_target="tpu_custom_call" | custom-call | flops 268435456 | bytes 16384 | tf_op jit(solution)/shard_map/pallas_call | solution.py:309
  51.5 6.1 %shard_map.51 = (f32[4,2,128,128]{3,2,1,0:T(8,128)S(1)}, f32[4,128]{1,0:T(4,128)S(1)}, f32[4,8,128,128]{3,2,1,0:T(8,128)}) custom-call(s32[32]{0:T(128)} %order_ref.9, s32[8,128]{1,0:T(8,128)} %bitcast.18, s32[8,128]{1,0:T(8,128)} %bitcast.8, f32[4,2,128,128]{3,2,1,0:T(8,128)} %shard_map.50.own_ref, f32[4,2,128,128]{3,2,1,0:T(8,128)} %copy-done.2, ...), custom_call_target="tpu_custom_call" | custom-call | flops 67108864 | bytes 5242880 | tf_op jit(solution)/shard_map/pallas_call | solution.py:359
  57.6 43.6 %conditional.2 = ((f32[4,2,128,128]{3,2,1,0:T(8,128)S(1)}, f32[4,128]{1,0:T(4,128)S(1)})) conditional(s32[]{:T(128)} %bitcast.4, (s32[128]{0:T(128)S(1)}, f32[4,2,128,128]{3,2,1,0:T(8,128)S(1)}, f32[4,8,128,128]{3,2,1,0:T(8,128)}, f32[32,128,128]{2,1,0:T(8,128)S(1)}, s32[8,128]{1,0:T(8,128)S(1)}, /*index=5*/f32[4,128]{1,0:T(4,128)S(1)}) %tuple.17, ...), branch_computations={%region_0.0_spmd, %region_1.0_spmd} | conditional | flops 1090650112 | bytes 14680104 | solution.py:553
  57.6 1.6 branch_0_fun.7
  59.2 32.0 %collective-permute-start = (f32[128,128]{1,0:T(8,128)}, f32[128,128]{1,0:T(8,128)S(1)}, u32[]{:S(2)}, u32[]{:S(2)}) collective-permute-start(f32[128,128]{1,0:T(8,128)} %get-tuple-element.79), channel_id=1, source_target_pairs={{0,8},{1,9},{2,10},{3,11},{4,12},{5,13},{6,14},{7,15},{8,16},{9,17... | collective-permute-start | bytes 196616 | tf_op jit(solution)/shard_map/cond/branch_0_fun/ppermute | solution.py:541
  91.2 2.5 %collective-permute-start.1 = (f32[128,128]{1,0:T(8,128)}, f32[128,128]{1,0:T(8,128)S(1)}, u32[]{:S(2)}, u32[]{:S(2)}) collective-permute-start(f32[128,128]{1,0:T(8,128)} %get-tuple-element.80), channel_id=1, source_target_pairs={{0,16},{1,17},{2,18},{3,19},{4,20},{5,21},{6,22},{7,23},{8,24},{9,... | collective-permute-start | bytes 196616 | tf_op jit(solution)/shard_map/cond/branch_0_fun/ppermute | solution.py:541
  93.7 0.9 collective-permute-start.2
  94.6 3.7 %branch_0_fun.6.acc_in_ref = f32[4,2,128,128]{3,2,1,0:T(8,128)} custom-call(s32[128]{0:T(128)S(1)} %get-tuple-element.73.list_ref, f32[4,2,128,128]{3,2,1,0:T(8,128)S(1)} %get-tuple-element.74.base_ref, f32[4,8,128,128]{3,2,1,0:T(8,128)} %get-tuple-element.75.right_ref, f32[32,128,128]{2,1,0:T(8,128)S(1)} %get-tuple-element.76.got_ref), custom_call_target="tpu_custom_call" | custom-call | flops 1073741824 | bytes 3145728 | tf_op jit(solution)/shard_map/cond/branch_0_fun/pallas_call | solution.py:476
  99.0 2.2 %branch_0_fun.8 = (f32[4,2,128,128]{3,2,1,0:T(8,128)S(1)}, f32[4,128]{1,0:T(4,128)S(1)}) custom-call(s32[128]{0:T(128)S(1)} %get-tuple-element.73.list_ref, f32[4,2,128,128]{3,2,1,0:T(8,128)} %branch_0_fun.6.acc_in_ref, f32[4,128]{1,0:T(4,128)S(1)} %get-tuple-element.77.totals_ref, f32[4,8,128,128]{3,2,1,0:T(8,128)} %get-tuple-element.75.right_ref, ...), custom_call_target="tpu_custom_call" | custom-call | flops 16777216 | bytes 2097152 | tf_op jit(solution)/shard_map/cond/branch_0_fun/pallas_call | solution.py:488
  101.3 3.1 %collective-permute-start.21 = (f32[4,128]{1,0:T(4,128)S(1)}, f32[4,128]{1,0:T(4,128)S(1)}, u32[]{:S(2)}, u32[]{:S(2)}) collective-permute-start(f32[4,128]{1,0:T(4,128)S(1)} %get-tuple-element.133.rest_0_), channel_id=1, source_target_pairs={{0,96},{32,0},{64,32},{96,64},{1,97},{33,1},{65,33},{97,65},{2,98}... | collective-permute-start | bytes 6152 | tf_op jit(solution)/shard_map/ppermute | solution.py:27
  104.3 0.9 collective-permute-start.19
  105.6 3.8 %collective-permute-done.20.rest_2_ = f32[4,128]{1,0:T(4,128)S(1)} collective-permute-done((f32[4,128]{1,0:T(4,128)S(1)}, f32[4,128]{1,0:T(4,128)S(1)}, u32[]{:S(2)}, u32[]{:S(2)}) %collective-permute-start.20) | collective-permute-done | bytes 2080 | tf_op jit(solution)/shard_map/ppermute | solution.py:27
  109.4 2.2 %shard_map.55 = f32[32,128,128]{2,1,0:T(8,128)} custom-call(s32[8,128]{1,0:T(8,128)S(1)} %get-tuple-element.125.plan_ref, f32[4,2,128,128]{3,2,1,0:T(8,128)S(1)} %get-tuple-element.130.own_ref.x_ref, f32[4,128]{1,0:T(4,128)S(1)} %get-tuple-element.133.rest_0_, f32[4,128]{1,0:T(4,128)S(1)} %collective-permute-done.19.rest_1_, ...), custom_call_target="tpu_custom_call" | custom-call | flops 131072 | bytes 3145728 | tf_op jit(solution)/shard_map/pallas_call | solution.py:206
  111.6 5.6 %all-to-all-start.3 = ((f32[32,128,128]{2,1,0:T(8,128)}), f32[32,128,128]{2,1,0:T(8,128)S(1)}, u32[]{:S(2)}, u32[]{:S(2)}) async-start(f32[32,128,128]{2,1,0:T(8,128)} %shard_map.55), calls=%async_computation.3 | async-start | bytes 4194304 | tf_op jit(solution)/shard_map/all_to_all | solution.py:533
  117.4 3.2 %collective-permute-start.15 = (f32[4,2,128,128]{3,2,1,0:T(8,128)S(1)}, f32[4,2,128,128]{3,2,1,0:T(8,128)S(1)}, u32[]{:S(2)}, u32[]{:S(2)}) collective-permute-start(f32[4,2,128,128]{3,2,1,0:T(8,128)S(1)} %get-tuple-element.130.own_ref.x_ref), channel_id=1, source_target_pairs={{0,96},{32,0},{64,32},{96,64},{1,97},{33,1},{65,33},{97,65},{2,98}... | collective-permute-start | bytes 1572872 | tf_op jit(solution)/shard_map/ppermute | solution.py:522
  120.6 12.1 %collective-permute-done.16.behind_ref = f32[4,2,128,128]{3,2,1,0:T(8,128)S(1)} collective-permute-done((f32[4,2,128,128]{3,2,1,0:T(8,128)S(1)}, f32[4,2,128,128]{3,2,1,0:T(8,128)S(1)}, u32[]{:S(2)}, u32[]{:S(2)}) %collective-permute-start.16) | collective-permute-done | bytes 524320 | tf_op jit(solution)/shard_map/ppermute | solution.py:521
  132.7 0.8 slice.26
  135.0 3.2 %collective-permute-start.18 = (f32[2,2,128,128]{3,2,1,0:T(8,128)}, f32[2,2,128,128]{3,2,1,0:T(8,128)}, u32[]{:S(2)}, u32[]{:S(2)}) collective-permute-start(f32[2,2,128,128]{3,2,1,0:T(8,128)} %slice.27), channel_id=1, source_target_pairs={{0,96},{32,0},{64,32},{96,64},{1,97},{33,1},{65,33},{97,65},{2,98}... | collective-permute-start | bytes 786440 | tf_op jit(solution)/shard_map/ppermute | solution.py:524
  139.3 2.8 %shard_map.47 = s32[128]{0:T(128)S(1)} custom-call(s32[32]{0:T(128)} %order_ref.9, s32[8,128]{1,0:T(8,128)S(1)} %get-tuple-element.125.plan_ref, s32[8,128]{1,0:T(8,128)} %bitcast.9, s32[8,128]{1,0:T(8,128)} %bitcast.10), custom_call_target="tpu_custom_call" | custom-call | flops 268435456 | bytes 16384 | tf_op jit(solution)/shard_map/pallas_call | solution.py:309
  142.5 0.9 collective-permute-done.18.far_high_ref
  143.4 6.0 %shard_map.54 = (f32[4,2,128,128]{3,2,1,0:T(8,128)S(1)}, f32[4,128]{1,0:T(4,128)S(1)}, f32[4,8,128,128]{3,2,1,0:T(8,128)}) custom-call(s32[32]{0:T(128)} %order_ref.9, s32[8,128]{1,0:T(8,128)} %bitcast.11, s32[8,128]{1,0:T(8,128)} %bitcast.12, f32[4,2,128,128]{3,2,1,0:T(8,128)S(1)} %get-tuple-element.130.own_ref.x_ref, f32[4,2,128,128]{3,2,1,0:T(8,128)} %copy-done.4, ...), custom_call_target="tpu_custom_call" | custom-call | flops 67108864 | bytes 5242880 | tf_op jit(solution)/shard_map/pallas_call | solution.py:359
  149.4 12.4 %conditional.3 = ((f32[4,2,128,128]{3,2,1,0:T(8,128)S(1)}, f32[4,128]{1,0:T(4,128)S(1)})) conditional(s32[]{:T(128)} %bitcast.3, (s32[128]{0:T(128)S(1)}, f32[4,2,128,128]{3,2,1,0:T(8,128)S(1)}, f32[4,8,128,128]{3,2,1,0:T(8,128)}, f32[32,128,128]{2,1,0:T(8,128)S(1)}, s32[8,128]{1,0:T(8,128)S(1)}, /*index=5*/f32[4,128]{1,0:T(4,128)S(1)}) %tuple.19, ...), branch_computations={%region_2.0_spmd, %region_3.0_spmd} | conditional | flops 1090650112 | bytes 14680104 | solution.py:553
  149.4 1.6 branch_0_fun.10
  151.2 2.7 %collective-permute-start.4 = (f32[128,128]{1,0:T(8,128)}, f32[128,128]{1,0:T(8,128)S(1)}, u32[]{:S(2)}, u32[]{:S(2)}) collective-permute-start(f32[128,128]{1,0:T(8,128)} %get-tuple-element.100), channel_id=1, source_target_pairs={{0,16},{1,17},{2,18},{3,19},{4,20},{5,21},{6,22},{7,23},{8,24},{9,... | collective-permute-start | bytes 196616 | tf_op jit(solution)/shard_map/cond/branch_0_fun/ppermute | solution.py:541
  154.0 1.4 collective-permute-start.5
  155.4 3.5 %branch_0_fun.9.acc_in_ref = f32[4,2,128,128]{3,2,1,0:T(8,128)} custom-call(s32[128]{0:T(128)S(1)} %get-tuple-element.93.list_ref, f32[4,2,128,128]{3,2,1,0:T(8,128)S(1)} %get-tuple-element.94.base_ref, f32[4,8,128,128]{3,2,1,0:T(8,128)} %get-tuple-element.95.right_ref, f32[32,128,128]{2,1,0:T(8,128)S(1)} %get-tuple-element.96.got_ref), custom_call_target="tpu_custom_call" | custom-call | flops 1073741824 | bytes 3145728 | tf_op jit(solution)/shard_map/cond/branch_0_fun/pallas_call | solution.py:476
  159.6 2.2 %branch_0_fun.11 = (f32[4,2,128,128]{3,2,1,0:T(8,128)S(1)}, f32[4,128]{1,0:T(4,128)S(1)}) custom-call(s32[128]{0:T(128)S(1)} %get-tuple-element.93.list_ref, f32[4,2,128,128]{3,2,1,0:T(8,128)} %branch_0_fun.9.acc_in_ref, f32[4,128]{1,0:T(4,128)S(1)} %get-tuple-element.97.totals_ref, f32[4,8,128,128]{3,2,1,0:T(8,128)} %get-tuple-element.95.right_ref, ...), custom_call_target="tpu_custom_call" | custom-call | flops 16777216 | bytes 2097152 | tf_op jit(solution)/shard_map/cond/branch_0_fun/pallas_call | solution.py:488
  161.8 5.5 %collective-permute-start.24 = (f32[4,128]{1,0:T(4,128)S(1)}, f32[4,128]{1,0:T(4,128)S(1)}, u32[]{:S(2)}, u32[]{:S(2)}) collective-permute-start(f32[4,128]{1,0:T(4,128)S(1)} %get-tuple-element.136.rest_0_), channel_id=1, source_target_pairs={{0,96},{32,0},{64,32},{96,64},{1,97},{33,1},{65,33},{97,65},{2,98}... | collective-permute-start | bytes 6152 | tf_op jit(solution)/shard_map/ppermute | solution.py:27
  167.3 0.9 collective-permute-start.22
  168.6 3.8 %collective-permute-done.23.rest_2_ = f32[4,128]{1,0:T(4,128)S(1)} collective-permute-done((f32[4,128]{1,0:T(4,128)S(1)}, f32[4,128]{1,0:T(4,128)S(1)}, u32[]{:S(2)}, u32[]{:S(2)}) %collective-permute-start.23) | collective-permute-done | bytes 2080 | tf_op jit(solution)/shard_map/ppermute | solution.py:27
  173.0 1.5 shard_map.56
  (65 shorter events, 8.4 us)
Async XLA Ops:
  1.1 5.7 %collective-permute-start.14 = (f32[4,128]{1,0:T(4,128)S(1)}, f32[4,128]{1,0:T(4,128)S(1)}, u32[]{:S(2)}, u32[]{:S(2)}) collective-permute-start(f32[4,128]{1,0:T(4,128)S(1)} %shard_map.52.rest_0_), channel_id=1, source_target_pairs={{0,96},{32,0},{64,32},{96,64},{1,97},{33,1},{65,33},{97,65},{2,98}... | collective-permute-start | bytes 6152 | tf_op jit(solution)/shard_map/ppermute | solution.py:27
  4.0 5.1 %collective-permute-start.13 = (f32[4,128]{1,0:T(4,128)S(1)}, f32[4,128]{1,0:T(4,128)S(1)}, u32[]{:S(2)}, u32[]{:S(2)}) collective-permute-start(f32[4,128]{1,0:T(4,128)S(1)} %shard_map.52.rest_0_), channel_id=1, source_target_pairs={{0,64},{32,96},{64,0},{96,32},{1,65},{33,97},{65,1},{97,33},{2,66}... | collective-permute-start | bytes 6152 | tf_op jit(solution)/shard_map/ppermute | solution.py:27
  4.8 4.8 %collective-permute-start.12 = (f32[4,128]{1,0:T(4,128)S(1)}, f32[4,128]{1,0:T(4,128)S(1)}, u32[]{:S(2)}, u32[]{:S(2)}) collective-permute-start(f32[4,128]{1,0:T(4,128)S(1)} %shard_map.52.rest_0_), channel_id=1, source_target_pairs={{0,32},{32,64},{64,96},{96,0},{1,33},{33,65},{65,97},{97,1},{2,34}... | collective-permute-start | bytes 6152 | tf_op jit(solution)/shard_map/ppermute | solution.py:27
  12.1 8.3 %copy-start = (f32[4,2,128,128]{3,2,1,0:T(8,128)S(1)}, f32[4,2,128,128]{3,2,1,0:T(8,128)}, u32[]{:S(2)}) copy-start(f32[4,2,128,128]{3,2,1,0:T(8,128)} %x_ref.3) | copy-start | bytes 1572868
  12.1 45.5 %all-to-all-start.2 = ((f32[32,128,128]{2,1,0:T(8,128)}), f32[32,128,128]{2,1,0:T(8,128)S(1)}, u32[]{:S(2)}, u32[]{:S(2)}) async-start(f32[32,128,128]{2,1,0:T(8,128)} %shard_map.53), calls=%async_computation.2 | async-start | bytes 4194304 | tf_op jit(solution)/shard_map/all_to_all | solution.py:533
  20.4 5.1 %collective-permute-start.7 = (f32[4,2,128,128]{3,2,1,0:T(8,128)S(1)}, f32[4,2,128,128]{3,2,1,0:T(8,128)S(1)}, u32[]{:S(2)}, u32[]{:S(2)}) collective-permute-start(f32[4,2,128,128]{3,2,1,0:T(8,128)S(1)} %copy-done), channel_id=1, source_target_pairs={{1,0},{2,1},{3,2},{4,3},{5,4},{6,5},{7,6},{8,7},{9,8},{10,9},{11,1... | collective-permute-start | bytes 1572872 | tf_op jit(solution)/shard_map/ppermute | solution.py:389
  21.7 4.7 %collective-permute-start.6 = (f32[4,2,128,128]{3,2,1,0:T(8,128)S(1)}, f32[4,2,128,128]{3,2,1,0:T(8,128)}, u32[]{:S(2)}, u32[]{:S(2)}) collective-permute-start(f32[4,2,128,128]{3,2,1,0:T(8,128)S(1)} %copy-done), channel_id=1, source_target_pairs={{0,1},{1,2},{2,3},{3,4},{4,5},{5,6},{6,7},{7,8},{8,9},{9,10},{10,1... | collective-permute-start | bytes 1572872 | tf_op jit(solution)/shard_map/ppermute | solution.py:388
  25.6 0.8 copy-start.5
  28.0 10.7 %collective-permute-start.9 = (f32[4,2,128,128]{3,2,1,0:T(8,128)}, f32[4,2,128,128]{3,2,1,0:T(8,128)S(1)}, u32[]{:S(2)}, u32[]{:S(2)}) collective-permute-start(f32[4,2,128,128]{3,2,1,0:T(8,128)} %shard_map.50.own_ref), channel_id=1, source_target_pairs={{0,32},{32,64},{64,96},{96,0},{1,33},{33,65},{65,97},{97,1},{2,34}... | collective-permute-start | bytes 1572872 | tf_op jit(solution)/shard_map/ppermute | solution.py:521
  28.1 11.5 %collective-permute-start.8 = (f32[4,2,128,128]{3,2,1,0:T(8,128)}, f32[4,2,128,128]{3,2,1,0:T(8,128)S(1)}, u32[]{:S(2)}, u32[]{:S(2)}) collective-permute-start(f32[4,2,128,128]{3,2,1,0:T(8,128)} %shard_map.50.own_ref), channel_id=1, source_target_pairs={{0,96},{32,0},{64,32},{96,64},{1,97},{33,1},{65,33},{97,65},{2,98}... | collective-permute-start | bytes 1572872 | tf_op jit(solution)/shard_map/ppermute | solution.py:522
  38.6 0.8 copy-start.1
  39.5 11.3 %collective-permute-start.10 = (f32[2,2,128,128]{3,2,1,0:T(8,128)S(1)}, f32[2,2,128,128]{3,2,1,0:T(8,128)S(1)}, u32[]{:S(2)}, u32[]{:S(2)}) collective-permute-start(f32[2,2,128,128]{3,2,1,0:T(8,128)S(1)} %slice.24), channel_id=1, source_target_pairs={{0,32},{32,64},{64,96},{96,0},{1,33},{33,65},{65,97},{97,1},{2,34}... | collective-permute-start | bytes 786440 | tf_op jit(solution)/shard_map/ppermute | solution.py:523
  39.6 0.8 copy-start.2
  40.4 10.4 %collective-permute-start.11 = (f32[2,2,128,128]{3,2,1,0:T(8,128)S(1)}, f32[2,2,128,128]{3,2,1,0:T(8,128)}, u32[]{:S(2)}, u32[]{:S(2)}) collective-permute-start(f32[2,2,128,128]{3,2,1,0:T(8,128)S(1)} %slice.25), channel_id=1, source_target_pairs={{0,96},{32,0},{64,32},{96,64},{1,97},{33,1},{65,33},{97,65},{2,98}... | collective-permute-start | bytes 786440 | tf_op jit(solution)/shard_map/ppermute | solution.py:524
  50.8 0.7 copy-start.6
  59.2 39.1 %collective-permute-start = (f32[128,128]{1,0:T(8,128)}, f32[128,128]{1,0:T(8,128)S(1)}, u32[]{:S(2)}, u32[]{:S(2)}) collective-permute-start(f32[128,128]{1,0:T(8,128)} %get-tuple-element.79), channel_id=1, source_target_pairs={{0,8},{1,9},{2,10},{3,11},{4,12},{5,13},{6,14},{7,15},{8,16},{9,17... | collective-permute-start | bytes 196616 | tf_op jit(solution)/shard_map/cond/branch_0_fun/ppermute | solution.py:541
  91.2 7.1 %collective-permute-start.1 = (f32[128,128]{1,0:T(8,128)}, f32[128,128]{1,0:T(8,128)S(1)}, u32[]{:S(2)}, u32[]{:S(2)}) collective-permute-start(f32[128,128]{1,0:T(8,128)} %get-tuple-element.80), channel_id=1, source_target_pairs={{0,16},{1,17},{2,18},{3,19},{4,20},{5,21},{6,22},{7,23},{8,24},{9,... | collective-permute-start | bytes 196616 | tf_op jit(solution)/shard_map/cond/branch_0_fun/ppermute | solution.py:541
  93.7 4.6 %collective-permute-start.2 = (f32[128,128]{1,0:T(8,128)}, f32[128,128]{1,0:T(8,128)S(1)}, u32[]{:S(2)}, u32[]{:S(2)}) collective-permute-start(f32[128,128]{1,0:T(8,128)} %get-tuple-element.81), channel_id=1, source_target_pairs={{0,24},{1,25},{2,26},{3,27},{4,28},{5,29},{6,30},{7,31},{8,0},{9,1... | collective-permute-start | bytes 196616 | tf_op jit(solution)/shard_map/cond/branch_0_fun/ppermute | solution.py:541
  98.3 0.6 copy-start.8
  98.3 0.6 copy-start.10
  98.4 0.7 copy-start.12
  101.3 4.4 %collective-permute-start.21 = (f32[4,128]{1,0:T(4,128)S(1)}, f32[4,128]{1,0:T(4,128)S(1)}, u32[]{:S(2)}, u32[]{:S(2)}) collective-permute-start(f32[4,128]{1,0:T(4,128)S(1)} %get-tuple-element.133.rest_0_), channel_id=1, source_target_pairs={{0,96},{32,0},{64,32},{96,64},{1,97},{33,1},{65,33},{97,65},{2,98}... | collective-permute-start | bytes 6152 | tf_op jit(solution)/shard_map/ppermute | solution.py:27
  104.3 5.1 %collective-permute-start.20 = (f32[4,128]{1,0:T(4,128)S(1)}, f32[4,128]{1,0:T(4,128)S(1)}, u32[]{:S(2)}, u32[]{:S(2)}) collective-permute-start(f32[4,128]{1,0:T(4,128)S(1)} %get-tuple-element.133.rest_0_), channel_id=1, source_target_pairs={{0,64},{32,96},{64,0},{96,32},{1,65},{33,97},{65,1},{97,33},{2,66}... | collective-permute-start | bytes 6152 | tf_op jit(solution)/shard_map/ppermute | solution.py:27
  104.3 5.1 %collective-permute-start.19 = (f32[4,128]{1,0:T(4,128)S(1)}, f32[4,128]{1,0:T(4,128)S(1)}, u32[]{:S(2)}, u32[]{:S(2)}) collective-permute-start(f32[4,128]{1,0:T(4,128)S(1)} %get-tuple-element.133.rest_0_), channel_id=1, source_target_pairs={{0,32},{32,64},{64,96},{96,0},{1,33},{33,65},{65,97},{97,1},{2,34}... | collective-permute-start | bytes 6152 | tf_op jit(solution)/shard_map/ppermute | solution.py:27
  111.6 37.8 %all-to-all-start.3 = ((f32[32,128,128]{2,1,0:T(8,128)}), f32[32,128,128]{2,1,0:T(8,128)S(1)}, u32[]{:S(2)}, u32[]{:S(2)}) async-start(f32[32,128,128]{2,1,0:T(8,128)} %shard_map.55), calls=%async_computation.3 | async-start | bytes 4194304 | tf_op jit(solution)/shard_map/all_to_all | solution.py:533
  117.3 15.4 %collective-permute-start.16 = (f32[4,2,128,128]{3,2,1,0:T(8,128)S(1)}, f32[4,2,128,128]{3,2,1,0:T(8,128)S(1)}, u32[]{:S(2)}, u32[]{:S(2)}) collective-permute-start(f32[4,2,128,128]{3,2,1,0:T(8,128)S(1)} %get-tuple-element.130.own_ref.x_ref), channel_id=1, source_target_pairs={{0,32},{32,64},{64,96},{96,0},{1,33},{33,65},{65,97},{97,1},{2,34}... | collective-permute-start | bytes 1572872 | tf_op jit(solution)/shard_map/ppermute | solution.py:521
  117.4 16.1 %collective-permute-start.15 = (f32[4,2,128,128]{3,2,1,0:T(8,128)S(1)}, f32[4,2,128,128]{3,2,1,0:T(8,128)S(1)}, u32[]{:S(2)}, u32[]{:S(2)}) collective-permute-start(f32[4,2,128,128]{3,2,1,0:T(8,128)S(1)} %get-tuple-element.130.own_ref.x_ref), channel_id=1, source_target_pairs={{0,96},{32,0},{64,32},{96,64},{1,97},{33,1},{65,33},{97,65},{2,98}... | collective-permute-start | bytes 1572872 | tf_op jit(solution)/shard_map/ppermute | solution.py:522
  132.7 9.9 %copy-start.3 = (f32[4,2,128,128]{3,2,1,0:T(8,128)}, f32[4,2,128,128]{3,2,1,0:T(8,128)S(1)}, u32[]{:S(2)}) copy-start(f32[4,2,128,128]{3,2,1,0:T(8,128)S(1)} %collective-permute-done.16.behind_ref) | copy-start | bytes 1572868
  133.5 9.1 %collective-permute-start.17 = (f32[2,2,128,128]{3,2,1,0:T(8,128)}, f32[2,2,128,128]{3,2,1,0:T(8,128)S(1)}, u32[]{:S(2)}, u32[]{:S(2)}) collective-permute-start(f32[2,2,128,128]{3,2,1,0:T(8,128)} %slice.26), channel_id=1, source_target_pairs={{0,32},{32,64},{64,96},{96,0},{1,33},{33,65},{65,97},{97,1},{2,34}... | collective-permute-start | bytes 786440 | tf_op jit(solution)/shard_map/ppermute | solution.py:523
  133.5 0.8 copy-start.4
  135.0 8.4 %collective-permute-start.18 = (f32[2,2,128,128]{3,2,1,0:T(8,128)}, f32[2,2,128,128]{3,2,1,0:T(8,128)}, u32[]{:S(2)}, u32[]{:S(2)}) collective-permute-start(f32[2,2,128,128]{3,2,1,0:T(8,128)} %slice.27), channel_id=1, source_target_pairs={{0,96},{32,0},{64,32},{96,64},{1,97},{33,1},{65,33},{97,65},{2,98}... | collective-permute-start | bytes 786440 | tf_op jit(solution)/shard_map/ppermute | solution.py:524
  142.5 0.9 copy-start.7
  151.0 7.9 %collective-permute-start.3 = (f32[128,128]{1,0:T(8,128)}, f32[128,128]{1,0:T(8,128)S(1)}, u32[]{:S(2)}, u32[]{:S(2)}) collective-permute-start(f32[128,128]{1,0:T(8,128)} %get-tuple-element.99), channel_id=1, source_target_pairs={{0,8},{1,9},{2,10},{3,11},{4,12},{5,13},{6,14},{7,15},{8,16},{9,17... | collective-permute-start | bytes 196616 | tf_op jit(solution)/shard_map/cond/branch_0_fun/ppermute | solution.py:541
  151.2 7.6 %collective-permute-start.4 = (f32[128,128]{1,0:T(8,128)}, f32[128,128]{1,0:T(8,128)S(1)}, u32[]{:S(2)}, u32[]{:S(2)}) collective-permute-start(f32[128,128]{1,0:T(8,128)} %get-tuple-element.100), channel_id=1, source_target_pairs={{0,16},{1,17},{2,18},{3,19},{4,20},{5,21},{6,22},{7,23},{8,24},{9,... | collective-permute-start | bytes 196616 | tf_op jit(solution)/shard_map/cond/branch_0_fun/ppermute | solution.py:541
  154.0 4.9 %collective-permute-start.5 = (f32[128,128]{1,0:T(8,128)}, f32[128,128]{1,0:T(8,128)S(1)}, u32[]{:S(2)}, u32[]{:S(2)}) collective-permute-start(f32[128,128]{1,0:T(8,128)} %get-tuple-element.101), channel_id=1, source_target_pairs={{0,24},{1,25},{2,26},{3,27},{4,28},{5,29},{6,30},{7,31},{8,0},{9,1... | collective-permute-start | bytes 196616 | tf_op jit(solution)/shard_map/cond/branch_0_fun/ppermute | solution.py:541
  158.9 0.6 copy-start.9
  158.9 0.6 copy-start.11
  158.9 0.7 copy-start.13
  161.8 6.8 %collective-permute-start.24 = (f32[4,128]{1,0:T(4,128)S(1)}, f32[4,128]{1,0:T(4,128)S(1)}, u32[]{:S(2)}, u32[]{:S(2)}) collective-permute-start(f32[4,128]{1,0:T(4,128)S(1)} %get-tuple-element.136.rest_0_), channel_id=1, source_target_pairs={{0,96},{32,0},{64,32},{96,64},{1,97},{33,1},{65,33},{97,65},{2,98}... | collective-permute-start | bytes 6152 | tf_op jit(solution)/shard_map/ppermute | solution.py:27
  167.3 5.1 %collective-permute-start.23 = (f32[4,128]{1,0:T(4,128)S(1)}, f32[4,128]{1,0:T(4,128)S(1)}, u32[]{:S(2)}, u32[]{:S(2)}) collective-permute-start(f32[4,128]{1,0:T(4,128)S(1)} %get-tuple-element.136.rest_0_), channel_id=1, source_target_pairs={{0,64},{32,96},{64,0},{96,32},{1,65},{33,97},{65,1},{97,33},{2,66}... | collective-permute-start | bytes 6152 | tf_op jit(solution)/shard_map/ppermute | solution.py:27
  167.3 5.1 %collective-permute-start.22 = (f32[4,128]{1,0:T(4,128)S(1)}, f32[4,128]{1,0:T(4,128)S(1)}, u32[]{:S(2)}, u32[]{:S(2)}) collective-permute-start(f32[4,128]{1,0:T(4,128)S(1)} %get-tuple-element.136.rest_0_), channel_id=1, source_target_pairs={{0,32},{32,64},{64,96},{96,0},{1,33},{33,65},{65,97},{97,1},{2,34}... | collective-permute-start | bytes 6152 | tf_op jit(solution)/shard_map/ppermute | solution.py:27
  168.6 3.8 %copy-start.14 = (f32[4,128]{1,0:T(4,128)}, f32[4,128]{1,0:T(4,128)S(1)}, u32[]{:S(2)}) copy-start(f32[4,128]{1,0:T(4,128)S(1)} %collective-permute-done.24.rest_3_) | copy-start | bytes 6148
  172.4 0.6 copy-start.15
  172.4 0.6 copy-start.16

commit v5 on v4

--- a/solution.py
+++ b/solution.py
@@ -369,32 +369,11 @@
     )(order, in_pattern, out_pattern, own, *gathered)
 
 
-def pick_kernel(order_ref, held_ref, below_ref, above_ref, out_ref, sem):
-    place = lax.axis_index("pcol")
-    panel = order_ref[place]
-    for chosen, ref in (
-        (panel == place, held_ref), (panel < place, below_ref), (panel > place, above_ref)
-    ):
-
-        @pl.when(chosen)
-        def _():
-            pltpu.make_async_copy(ref, out_ref, sem).start()
-
-    pltpu.make_async_copy(held_ref, out_ref, sem).wait()
-
-
-def shifted(order, x):
-    up = [(i, i + 1) for i in range(order.shape[0] - 1)]
+def shifts(x, panels):
+    up = [(i, i + 1) for i in range(panels - 1)]
     from_below = lax.ppermute(x, "pcol", up)
     from_above = lax.ppermute(x, "pcol", [(j, i) for i, j in up])
-    return pl.pallas_call(
-        pick_kernel,
-        out_shape=jax.ShapeDtypeStruct(x.shape, jnp.float32),
-        in_specs=[SMEM, ANY, ANY, ANY],
-        out_specs=VMEM,
-        scratch_shapes=[pltpu.SemaphoreType.DMA],
-        cost_estimate=pl.CostEstimate(flops=0, bytes_accessed=1 << 20, transcendentals=0),
-    )(order, x, from_below, from_above)
+    return from_below, from_above
 
 
 def add_listed(list_ref, number, first, right_ref, acc_ref, fetch, lefts, rights, sems):
@@ -560,11 +539,16 @@
     kept_rows = kept.T
     tables = (order[None], pattern_rows, kept_rows)
     (first_plan,) = plans(((False, True, False),), *tables)
+    from_below, from_above = shifts(match_tiles, order.shape[0])
     sums = row_sums(column_partial(match_tiles), rows)
+    place = lax.axis_index("pcol")
+    step = order[place] - place
+    sums, step = lax.optimization_barrier((sums, step))
+    own = jnp.where(step == 0, match_tiles, jnp.where(step < 0, from_below, from_above))
     check, second_plan = plans(((False, False, True), (True, True, True)), *tables)
     square, part = expand(
         False, order, first_plan, check[MISFIT, 0], pattern_rows, kept_rows,
-        match_tiles, sums, shifted(order, match_tiles), rows,
+        match_tiles, sums, own, rows,
     )
     sums = row_sums(part, rows)
     square, part = expand(

time: 177 us -> 175 us (0.989)
  waiting for transfers between devices: 32.7 us -> 29.7 us
  local copies, waits for them, and re-layouts: 8.3 us -> 10.4 us
    ppermute x9, waiting for transfers between devices: 11.1 us -> 9.17 us  [row_sums(): sums.append(lax.ppermute(partial_value, 'prow', ring(size, step)))]
    unnamed x22 -> x24, local copies, waits for them, and re-layouts: 3.66 us -> 3.09 us
  transfers between devices with their start and end apart: 27 -> 27, of which waited for: 11 -> 10; matrix products, arithmetic and copies ran while one was open for 2% -> 4% of each run, Pallas kernels for 17% -> 16%
where the time goes in v5:
time: 175 us; the launch traced here: 173 us
  starting transfers between devices  85.9 us (49%)
  Pallas kernels  43.4 us (25%)
  waiting for transfers between devices  29.7 us (17%)
  local copies, waits for them, and re-layouts  10.4 us (6%)
  between operations  2.13 us (1%)
    ppermute x6, starting transfers between devices, by_level(): lax.ppermute(tile, 'pcol', ring(panels, (step + 1) * depth))  39.8 us
    ppermute x2, waiting for transfers between devices, gather_rows(): behind = lax.ppermute(own, 'prow', ring(size, 1))  19.2 us
    ppermute x9, starting transfers between devices, row_sums(): sums.append(lax.ppermute(partial_value, 'prow', ring(size, step)))  14.8 us
    all_to_all x2, starting transfers between devices, expand(): got = lax.all_to_all(send, 'pcol', 0, 0, tiled=True)  13.2 us
    pallas_call x2, Pallas kernels, own_products(): pl.pallas_call(own_kernel, out_shape=(jax.ShapeDtypeStruct(own.shape, jnp...  12.2 us
    ppermute x9, waiting for transfers between devices, row_sums(): sums.append(lax.ppermute(partial_value, 'prow', ring(size, step)))  9.17 us
    pallas_call x2, Pallas kernels, main_products(): pl.pallas_call(main_kernel, out_shape=jax.ShapeDtypeStruct(base.shape, jn...  7.14 us
    ppermute x2, starting transfers between devices, gather_rows(): far_high = lax.ppermute(ahead[half:], 'prow', ring(size, -1))  6.36 us
  transfers between devices with their start and end apart: 27, of which 10 were waited for; matrix products, arithmetic and copies ran while one was open for 4% of the time, Pallas kernels for 16%

profile of v5, /device:TPU:0, one launch (start us, length us, event | category | flops | bytes accessed | tf_op | source)
XLA Modules:
  0.0 172.8 jit_solution(10619384722496683510)
XLA Ops:
  0.0 1.1 shard_map.50.rest_0_
  1.1 2.9 %collective-permute-start.8 = (f32[4,128]{1,0:T(4,128)S(1)}, f32[4,128]{1,0:T(4,128)S(1)}, u32[]{:S(2)}, u32[]{:S(2)}) collective-permute-start(f32[4,128]{1,0:T(4,128)S(1)} %shard_map.50.rest_0_), channel_id=1, source_target_pairs={{0,96},{32,0},{64,32},{96,64},{1,97},{33,1},{65,33},{97,65},{2,98}... | collective-permute-start | bytes 6152 | tf_op jit(solution)/shard_map/ppermute | solution.py:27
  4.0 0.8 collective-permute-start.7
  4.8 0.9 collective-permute-start.6
  5.7 1.2 dynamic_slice.3
  7.6 1.1 shard_map.48.plan_ref
  9.6 2.5 %shard_map.52 = f32[32,128,128]{2,1,0:T(8,128)} custom-call(s32[8,128]{1,0:T(8,128)S(1)} %shard_map.48.plan_ref, f32[4,2,128,128]{3,2,1,0:T(8,128)} %x_ref.3, f32[4,128]{1,0:T(4,128)S(1)} %shard_map.50.rest_0_, f32[4,128]{1,0:T(4,128)S(1)} %collective-permute-done.6.rest_1_, f32[4,128]{1,0:T(4,128)S(1)} %collective-permute-done.7.rest_2_, ...), custom_call_target="tpu_custom_call" | custom-call | flops 131072 | bytes 3145728 | tf_op jit(solution)/shard_map/pallas_call | solution.py:206
  12.1 8.3 %all-to-all-start.2 = ((f32[32,128,128]{2,1,0:T(8,128)}), f32[32,128,128]{2,1,0:T(8,128)S(1)}, u32[]{:S(2)}, u32[]{:S(2)}) async-start(f32[32,128,128]{2,1,0:T(8,128)} %shard_map.52), calls=%async_computation.2 | async-start | bytes 4194304 | tf_op jit(solution)/shard_map/all_to_all | solution.py:512
  20.4 1.3 collective-permute-start.10
  21.7 3.8 %collective-permute-start.9 = (f32[4,2,128,128]{3,2,1,0:T(8,128)S(1)}, f32[4,2,128,128]{3,2,1,0:T(8,128)}, u32[]{:S(2)}, u32[]{:S(2)}) collective-permute-start(f32[4,2,128,128]{3,2,1,0:T(8,128)S(1)} %copy-done), channel_id=1, source_target_pairs={{0,1},{1,2},{2,3},{3,4},{4,5},{5,6},{6,7},{7,8},{8,9},{9,10},{10,1... | collective-permute-start | bytes 1572872 | tf_op jit(solution)/shard_map/ppermute | solution.py:374
  25.6 0.8 copy-done.8
  26.4 1.1 select_select_fusion.own_ref
  27.5 0.9 collective-permute-start.12
  28.5 2.4 %collective-permute-start.11 = (f32[4,2,128,128]{3,2,1,0:T(8,128)S(1)}, f32[4,2,128,128]{3,2,1,0:T(8,128)S(1)}, u32[]{:S(2)}, u32[]{:S(2)}) collective-permute-start(f32[4,2,128,128]{3,2,1,0:T(8,128)S(1)} %select_select_fusion.own_ref), channel_id=1, source_target_pairs={{0,96},{32,0},{64,32},{96,64},{1,97},{33,1},{65,33},{97,65},{2,98}... | collective-permute-start | bytes 1572872 | tf_op jit(solution)/shard_map/ppermute | solution.py:501
  30.8 7.2 %collective-permute-done.12.behind_ref = f32[4,2,128,128]{3,2,1,0:T(8,128)S(1)} collective-permute-done((f32[4,2,128,128]{3,2,1,0:T(8,128)S(1)}, f32[4,2,128,128]{3,2,1,0:T(8,128)S(1)}, u32[]{:S(2)}, u32[]{:S(2)}) %collective-permute-start.12) | collective-permute-done | bytes 524320 | tf_op jit(solution)/shard_map/ppermute | solution.py:500
  39.8 3.1 %collective-permute-start.14 = (f32[2,2,128,128]{3,2,1,0:T(8,128)}, f32[2,2,128,128]{3,2,1,0:T(8,128)}, u32[]{:S(2)}, u32[]{:S(2)}) collective-permute-start(f32[2,2,128,128]{3,2,1,0:T(8,128)} %slice.25), channel_id=1, source_target_pairs={{0,96},{32,0},{64,32},{96,64},{1,97},{33,1},{65,33},{97,65},{2,98}... | collective-permute-start | bytes 786440 | tf_op jit(solution)/shard_map/ppermute | solution.py:503
  42.9 2.4 %shard_map.46 = (s32[8,128]{1,0:T(8,128)}, s32[8,128]{1,0:T(8,128)S(1)}) custom-call(s32[1,32]{1,0:T(1,128)} %bitcast.19, s32[8,128]{1,0:T(8,128)} %bitcast.15, s32[8,128]{1,0:T(8,128)} %bitcast.7), custom_call_target="tpu_custom_call" | custom-call | flops 75497472 | bytes 16384 | tf_op jit(solution)/shard_map/pallas_call | solution.py:153
  45.3 1.2 slice.19
  47.2 2.8 %shard_map.49 = s32[128]{0:T(128)S(1)} custom-call(s32[32]{0:T(128)} %order_ref.7, s32[8,128]{1,0:T(8,128)S(1)} %shard_map.48.plan_ref, s32[8,128]{1,0:T(8,128)} %bitcast.16, s32[8,128]{1,0:T(8,128)} %bitcast.8), custom_call_target="tpu_custom_call" | custom-call | flops 268435456 | bytes 16384 | tf_op jit(solution)/shard_map/pallas_call | solution.py:309
  50.7 6.3 %shard_map.51 = (f32[4,2,128,128]{3,2,1,0:T(8,128)}, f32[4,128]{1,0:T(4,128)S(1)}, f32[4,8,128,128]{3,2,1,0:T(8,128)}) custom-call(s32[32]{0:T(128)} %order_ref.7, s32[8,128]{1,0:T(8,128)} %bitcast.17, s32[8,128]{1,0:T(8,128)} %bitcast.9, f32[4,2,128,128]{3,2,1,0:T(8,128)} %copy-done.1, f32[4,2,128,128]{3,2,1,0:T(8,128)} %copy-done.5, ...), custom_call_target="tpu_custom_call" | custom-call | flops 67108864 | bytes 5242880 | tf_op jit(solution)/shard_map/pallas_call | solution.py:359
  57.0 43.6 %conditional.2 = ((f32[4,2,128,128]{3,2,1,0:T(8,128)S(1)}, f32[4,128]{1,0:T(4,128)S(1)})) conditional(s32[]{:T(128)} %bitcast.4, (s32[128]{0:T(128)S(1)}, f32[4,2,128,128]{3,2,1,0:T(8,128)}, f32[4,8,128,128]{3,2,1,0:T(8,128)}, f32[32,128,128]{2,1,0:T(8,128)S(1)}, s32[8,128]{1,0:T(8,128)S(1)}, /*index=5*/f32[4,128]{1,0:T(4,128)S(1)}) %tuple.19, ...), branch_computations={%region_0.1_spmd, %region_1.2_spmd} | conditional | flops 1090650112 | bytes 16777284 | solution.py:532
  57.0 1.6 branch_0_fun.7
  58.6 32.0 %collective-permute-start = (f32[128,128]{1,0:T(8,128)}, f32[128,128]{1,0:T(8,128)S(1)}, u32[]{:S(2)}, u32[]{:S(2)}) collective-permute-start(f32[128,128]{1,0:T(8,128)} %get-tuple-element.79), channel_id=1, source_target_pairs={{0,8},{1,9},{2,10},{3,11},{4,12},{5,13},{6,14},{7,15},{8,16},{9,17... | collective-permute-start | bytes 196616 | tf_op jit(solution)/shard_map/cond/branch_0_fun/ppermute | solution.py:520
  90.6 2.7 %collective-permute-start.1 = (f32[128,128]{1,0:T(8,128)}, f32[128,128]{1,0:T(8,128)S(1)}, u32[]{:S(2)}, u32[]{:S(2)}) collective-permute-start(f32[128,128]{1,0:T(8,128)} %get-tuple-element.80), channel_id=1, source_target_pairs={{0,16},{1,17},{2,18},{3,19},{4,20},{5,21},{6,22},{7,23},{8,24},{9,... | collective-permute-start | bytes 196616 | tf_op jit(solution)/shard_map/cond/branch_0_fun/ppermute | solution.py:520
  94.0 3.7 %branch_0_fun.6.acc_in_ref = f32[4,2,128,128]{3,2,1,0:T(8,128)} custom-call(s32[128]{0:T(128)S(1)} %get-tuple-element.73.list_ref, f32[4,2,128,128]{3,2,1,0:T(8,128)S(1)} %copy-done.2, f32[4,8,128,128]{3,2,1,0:T(8,128)} %get-tuple-element.75.right_ref, f32[32,128,128]{2,1,0:T(8,128)S(1)} %get-tuple-element.76.got_ref), custom_call_target="tpu_custom_call" | custom-call | flops 1073741824 | bytes 3145728 | tf_op jit(solution)/shard_map/cond/branch_0_fun/pallas_call | solution.py:455
  98.3 2.2 %branch_0_fun.8 = (f32[4,2,128,128]{3,2,1,0:T(8,128)S(1)}, f32[4,128]{1,0:T(4,128)S(1)}) custom-call(s32[128]{0:T(128)S(1)} %get-tuple-element.73.list_ref, f32[4,2,128,128]{3,2,1,0:T(8,128)} %branch_0_fun.6.acc_in_ref, f32[4,128]{1,0:T(4,128)S(1)} %get-tuple-element.77.totals_ref, f32[4,8,128,128]{3,2,1,0:T(8,128)} %get-tuple-element.75.right_ref, ...), custom_call_target="tpu_custom_call" | custom-call | flops 16777216 | bytes 2097152 | tf_op jit(solution)/shard_map/cond/branch_0_fun/pallas_call | solution.py:467
  100.6 2.8 %collective-permute-start.21 = (f32[4,128]{1,0:T(4,128)S(1)}, f32[4,128]{1,0:T(4,128)S(1)}, u32[]{:S(2)}, u32[]{:S(2)}) collective-permute-start(f32[4,128]{1,0:T(4,128)S(1)} %get-tuple-element.143.rest_0_), channel_id=1, source_target_pairs={{0,96},{32,0},{64,32},{96,64},{1,97},{33,1},{65,33},{97,65},{2,98}... | collective-permute-start | bytes 6152 | tf_op jit(solution)/shard_map/ppermute | solution.py:27
  103.5 0.8 collective-permute-start.19
  104.7 3.8 %collective-permute-done.20.rest_2_ = f32[4,128]{1,0:T(4,128)S(1)} collective-permute-done((f32[4,128]{1,0:T(4,128)S(1)}, f32[4,128]{1,0:T(4,128)S(1)}, u32[]{:S(2)}, u32[]{:S(2)}) %collective-permute-start.20) | collective-permute-done | bytes 2080 | tf_op jit(solution)/shard_map/ppermute | solution.py:27
  108.5 2.2 %shard_map.54 = f32[32,128,128]{2,1,0:T(8,128)} custom-call(s32[8,128]{1,0:T(8,128)S(1)} %get-tuple-element.130.plan_ref, f32[4,2,128,128]{3,2,1,0:T(8,128)S(1)} %get-tuple-element.140.own_ref.x_ref, f32[4,128]{1,0:T(4,128)S(1)} %get-tuple-element.143.rest_0_, f32[4,128]{1,0:T(4,128)S(1)} %collective-permute-done.19.rest_1_, ...), custom_call_target="tpu_custom_call" | custom-call | flops 131072 | bytes 3145728 | tf_op jit(solution)/shard_map/pallas_call | solution.py:206
  110.7 5.0 %all-to-all-start.3 = ((f32[32,128,128]{2,1,0:T(8,128)}), f32[32,128,128]{2,1,0:T(8,128)S(1)}, u32[]{:S(2)}, u32[]{:S(2)}) async-start(f32[32,128,128]{2,1,0:T(8,128)} %shard_map.54), calls=%async_computation.3 | async-start | bytes 4194304 | tf_op jit(solution)/shard_map/all_to_all | solution.py:512
  115.8 3.2 %collective-permute-start.15 = (f32[4,2,128,128]{3,2,1,0:T(8,128)S(1)}, f32[4,2,128,128]{3,2,1,0:T(8,128)S(1)}, u32[]{:S(2)}, u32[]{:S(2)}) collective-permute-start(f32[4,2,128,128]{3,2,1,0:T(8,128)S(1)} %get-tuple-element.140.own_ref.x_ref), channel_id=1, source_target_pairs={{0,96},{32,0},{64,32},{96,64},{1,97},{33,1},{65,33},{97,65},{2,98}... | collective-permute-start | bytes 1572872 | tf_op jit(solution)/shard_map/ppermute | solution.py:501
  119.0 12.1 %collective-permute-done.16.behind_ref = f32[4,2,128,128]{3,2,1,0:T(8,128)S(1)} collective-permute-done((f32[4,2,128,128]{3,2,1,0:T(8,128)S(1)}, f32[4,2,128,128]{3,2,1,0:T(8,128)S(1)}, u32[]{:S(2)}, u32[]{:S(2)}) %collective-permute-start.16) | collective-permute-done | bytes 524320 | tf_op jit(solution)/shard_map/ppermute | solution.py:500
  131.9 0.8 copy-done.7
  133.4 3.2 %collective-permute-start.18 = (f32[2,2,128,128]{3,2,1,0:T(8,128)}, f32[2,2,128,128]{3,2,1,0:T(8,128)}, u32[]{:S(2)}, u32[]{:S(2)}) collective-permute-start(f32[2,2,128,128]{3,2,1,0:T(8,128)} %slice.27), channel_id=1, source_target_pairs={{0,96},{32,0},{64,32},{96,64},{1,97},{33,1},{65,33},{97,65},{2,98}... | collective-permute-start | bytes 786440 | tf_op jit(solution)/shard_map/ppermute | solution.py:503
  137.8 2.8 %shard_map.47 = s32[128]{0:T(128)S(1)} custom-call(s32[32]{0:T(128)} %order_ref.7, s32[8,128]{1,0:T(8,128)S(1)} %get-tuple-element.130.plan_ref, s32[8,128]{1,0:T(8,128)} %bitcast.10, s32[8,128]{1,0:T(8,128)} %bitcast.11), custom_call_target="tpu_custom_call" | custom-call | flops 268435456 | bytes 16384 | tf_op jit(solution)/shard_map/pallas_call | solution.py:309
  140.9 0.9 collective-permute-done.18.far_high_ref
  141.8 6.0 %shard_map.53 = (f32[4,2,128,128]{3,2,1,0:T(8,128)S(1)}, f32[4,128]{1,0:T(4,128)S(1)}, f32[4,8,128,128]{3,2,1,0:T(8,128)}) custom-call(s32[32]{0:T(128)} %order_ref.7, s32[8,128]{1,0:T(8,128)} %bitcast.12, s32[8,128]{1,0:T(8,128)} %bitcast.13, f32[4,2,128,128]{3,2,1,0:T(8,128)S(1)} %get-tuple-element.140.own_ref.x_ref, f32[4,2,128,128]{3,2,1,0:T(8,128)} %copy-done.7, ...), custom_call_target="tpu_custom_call" | custom-call | flops 67108864 | bytes 5242880 | tf_op jit(solution)/shard_map/pallas_call | solution.py:359
  147.8 12.4 %conditional.3 = ((f32[4,2,128,128]{3,2,1,0:T(8,128)S(1)}, f32[4,128]{1,0:T(4,128)S(1)})) conditional(s32[]{:T(128)} %bitcast.3, (s32[128]{0:T(128)S(1)}, f32[4,2,128,128]{3,2,1,0:T(8,128)S(1)}, f32[4,8,128,128]{3,2,1,0:T(8,128)}, f32[32,128,128]{2,1,0:T(8,128)S(1)}, s32[8,128]{1,0:T(8,128)S(1)}, /*index=5*/f32[4,128]{1,0:T(4,128)S(1)}) %tuple.21, ...), branch_computations={%region_2.3_spmd, %region_3.4_spmd} | conditional | flops 1090650112 | bytes 14680104 | solution.py:532
  147.8 1.6 branch_0_fun.10
  149.6 2.7 %collective-permute-start.4 = (f32[128,128]{1,0:T(8,128)}, f32[128,128]{1,0:T(8,128)S(1)}, u32[]{:S(2)}, u32[]{:S(2)}) collective-permute-start(f32[128,128]{1,0:T(8,128)} %get-tuple-element.100), channel_id=1, source_target_pairs={{0,16},{1,17},{2,18},{3,19},{4,20},{5,21},{6,22},{7,23},{8,24},{9,... | collective-permute-start | bytes 196616 | tf_op jit(solution)/shard_map/cond/branch_0_fun/ppermute | solution.py:520
  152.3 1.4 collective-permute-start.5
  153.7 3.5 %branch_0_fun.9.acc_in_ref = f32[4,2,128,128]{3,2,1,0:T(8,128)} custom-call(s32[128]{0:T(128)S(1)} %get-tuple-element.93.list_ref, f32[4,2,128,128]{3,2,1,0:T(8,128)S(1)} %get-tuple-element.94.base_ref, f32[4,8,128,128]{3,2,1,0:T(8,128)} %get-tuple-element.95.right_ref, f32[32,128,128]{2,1,0:T(8,128)S(1)} %get-tuple-element.96.got_ref), custom_call_target="tpu_custom_call" | custom-call | flops 1073741824 | bytes 3145728 | tf_op jit(solution)/shard_map/cond/branch_0_fun/pallas_call | solution.py:455
  157.9 2.2 %branch_0_fun.11 = (f32[4,2,128,128]{3,2,1,0:T(8,128)S(1)}, f32[4,128]{1,0:T(4,128)S(1)}) custom-call(s32[128]{0:T(128)S(1)} %get-tuple-element.93.list_ref, f32[4,2,128,128]{3,2,1,0:T(8,128)} %branch_0_fun.9.acc_in_ref, f32[4,128]{1,0:T(4,128)S(1)} %get-tuple-element.97.totals_ref, f32[4,8,128,128]{3,2,1,0:T(8,128)} %get-tuple-element.95.right_ref, ...), custom_call_target="tpu_custom_call" | custom-call | flops 16777216 | bytes 2097152 | tf_op jit(solution)/shard_map/cond/branch_0_fun/pallas_call | solution.py:467
  160.2 5.5 %collective-permute-start.24 = (f32[4,128]{1,0:T(4,128)S(1)}, f32[4,128]{1,0:T(4,128)S(1)}, u32[]{:S(2)}, u32[]{:S(2)}) collective-permute-start(f32[4,128]{1,0:T(4,128)S(1)} %get-tuple-element.146.rest_0_), channel_id=1, source_target_pairs={{0,96},{32,0},{64,32},{96,64},{1,97},{33,1},{65,33},{97,65},{2,98}... | collective-permute-start | bytes 6152 | tf_op jit(solution)/shard_map/ppermute | solution.py:27
  165.7 0.9 collective-permute-start.22
  167.0 3.8 %collective-permute-done.23.rest_2_ = f32[4,128]{1,0:T(4,128)S(1)} collective-permute-done((f32[4,128]{1,0:T(4,128)S(1)}, f32[4,128]{1,0:T(4,128)S(1)}, u32[]{:S(2)}, u32[]{:S(2)}) %collective-permute-start.23) | collective-permute-done | bytes 2080 | tf_op jit(solution)/shard_map/ppermute | solution.py:27
  171.3 1.5 shard_map.55
  (70 shorter events, 9.6 us)
Async XLA Ops:
  1.1 7.6 %collective-permute-start.8 = (f32[4,128]{1,0:T(4,128)S(1)}, f32[4,128]{1,0:T(4,128)S(1)}, u32[]{:S(2)}, u32[]{:S(2)}) collective-permute-start(f32[4,128]{1,0:T(4,128)S(1)} %shard_map.50.rest_0_), channel_id=1, source_target_pairs={{0,96},{32,0},{64,32},{96,64},{1,97},{33,1},{65,33},{97,65},{2,98}... | collective-permute-start | bytes 6152 | tf_op jit(solution)/shard_map/ppermute | solution.py:27
  4.0 5.1 %collective-permute-start.7 = (f32[4,128]{1,0:T(4,128)S(1)}, f32[4,128]{1,0:T(4,128)S(1)}, u32[]{:S(2)}, u32[]{:S(2)}) collective-permute-start(f32[4,128]{1,0:T(4,128)S(1)} %shard_map.50.rest_0_), channel_id=1, source_target_pairs={{0,64},{32,96},{64,0},{96,32},{1,65},{33,97},{65,1},{97,33},{2,66}... | collective-permute-start | bytes 6152 | tf_op jit(solution)/shard_map/ppermute | solution.py:27
  4.8 4.8 %collective-permute-start.6 = (f32[4,128]{1,0:T(4,128)S(1)}, f32[4,128]{1,0:T(4,128)S(1)}, u32[]{:S(2)}, u32[]{:S(2)}) collective-permute-start(f32[4,128]{1,0:T(4,128)S(1)} %shard_map.50.rest_0_), channel_id=1, source_target_pairs={{0,32},{32,64},{64,96},{96,0},{1,33},{33,65},{65,97},{97,1},{2,34}... | collective-permute-start | bytes 6152 | tf_op jit(solution)/shard_map/ppermute | solution.py:27
  12.1 8.3 %copy-start = (f32[4,2,128,128]{3,2,1,0:T(8,128)S(1)}, f32[4,2,128,128]{3,2,1,0:T(8,128)}, u32[]{:S(2)}) copy-start(f32[4,2,128,128]{3,2,1,0:T(8,128)} %x_ref.3) | copy-start | bytes 1572868
  12.1 44.9 %all-to-all-start.2 = ((f32[32,128,128]{2,1,0:T(8,128)}), f32[32,128,128]{2,1,0:T(8,128)S(1)}, u32[]{:S(2)}, u32[]{:S(2)}) async-start(f32[32,128,128]{2,1,0:T(8,128)} %shard_map.52), calls=%async_computation.2 | async-start | bytes 4194304 | tf_op jit(solution)/shard_map/all_to_all | solution.py:512
  20.4 5.2 %collective-permute-start.10 = (f32[4,2,128,128]{3,2,1,0:T(8,128)S(1)}, f32[4,2,128,128]{3,2,1,0:T(8,128)S(1)}, u32[]{:S(2)}, u32[]{:S(2)}) collective-permute-start(f32[4,2,128,128]{3,2,1,0:T(8,128)S(1)} %copy-done), channel_id=1, source_target_pairs={{1,0},{2,1},{3,2},{4,3},{5,4},{6,5},{7,6},{8,7},{9,8},{10,9},{11,1... | collective-permute-start | bytes 1572872 | tf_op jit(solution)/shard_map/ppermute | solution.py:375
  21.7 4.7 %collective-permute-start.9 = (f32[4,2,128,128]{3,2,1,0:T(8,128)S(1)}, f32[4,2,128,128]{3,2,1,0:T(8,128)}, u32[]{:S(2)}, u32[]{:S(2)}) collective-permute-start(f32[4,2,128,128]{3,2,1,0:T(8,128)S(1)} %copy-done), channel_id=1, source_target_pairs={{0,1},{1,2},{2,3},{3,4},{4,5},{5,6},{6,7},{7,8},{8,9},{9,10},{10,1... | collective-permute-start | bytes 1572872 | tf_op jit(solution)/shard_map/ppermute | solution.py:374
  25.6 0.8 copy-start.8
  27.5 22.5 %copy-start.1 = (f32[4,2,128,128]{3,2,1,0:T(8,128)}, f32[4,2,128,128]{3,2,1,0:T(8,128)S(1)}, u32[]{:S(2)}) copy-start(f32[4,2,128,128]{3,2,1,0:T(8,128)S(1)} %select_select_fusion.own_ref) | copy-start | bytes 1572868
  27.5 10.5 %collective-permute-start.12 = (f32[4,2,128,128]{3,2,1,0:T(8,128)S(1)}, f32[4,2,128,128]{3,2,1,0:T(8,128)S(1)}, u32[]{:S(2)}, u32[]{:S(2)}) collective-permute-start(f32[4,2,128,128]{3,2,1,0:T(8,128)S(1)} %select_select_fusion.own_ref), channel_id=1, source_target_pairs={{0,32},{32,64},{64,96},{96,0},{1,33},{33,65},{65,97},{97,1},{2,34}... | collective-permute-start | bytes 1572872 | tf_op jit(solution)/shard_map/ppermute | solution.py:500
  28.5 10.3 %collective-permute-start.11 = (f32[4,2,128,128]{3,2,1,0:T(8,128)S(1)}, f32[4,2,128,128]{3,2,1,0:T(8,128)S(1)}, u32[]{:S(2)}, u32[]{:S(2)}) collective-permute-start(f32[4,2,128,128]{3,2,1,0:T(8,128)S(1)} %select_select_fusion.own_ref), channel_id=1, source_target_pairs={{0,96},{32,0},{64,32},{96,64},{1,97},{33,1},{65,33},{97,65},{2,98}... | collective-permute-start | bytes 1572872 | tf_op jit(solution)/shard_map/ppermute | solution.py:501
  38.0 0.9 copy-start.4
  38.8 11.2 %collective-permute-start.13 = (f32[2,2,128,128]{3,2,1,0:T(8,128)}, f32[2,2,128,128]{3,2,1,0:T(8,128)S(1)}, u32[]{:S(2)}, u32[]{:S(2)}) collective-permute-start(f32[2,2,128,128]{3,2,1,0:T(8,128)} %slice.24), channel_id=1, source_target_pairs={{0,32},{32,64},{64,96},{96,0},{1,33},{33,65},{65,97},{97,1},{2,34}... | collective-permute-start | bytes 786440 | tf_op jit(solution)/shard_map/ppermute | solution.py:502
  38.9 0.9 copy-start.5
  39.8 10.2 %collective-permute-start.14 = (f32[2,2,128,128]{3,2,1,0:T(8,128)}, f32[2,2,128,128]{3,2,1,0:T(8,128)}, u32[]{:S(2)}, u32[]{:S(2)}) collective-permute-start(f32[2,2,128,128]{3,2,1,0:T(8,128)} %slice.25), channel_id=1, source_target_pairs={{0,96},{32,0},{64,32},{96,64},{1,97},{33,1},{65,33},{97,65},{2,98}... | collective-permute-start | bytes 786440 | tf_op jit(solution)/shard_map/ppermute | solution.py:503
  50.0 0.7 copy-start.9
  57.0 37.0 %copy-start.2 = (f32[4,2,128,128]{3,2,1,0:T(8,128)S(1)}, f32[4,2,128,128]{3,2,1,0:T(8,128)}, u32[]{:S(2)}) copy-start(f32[4,2,128,128]{3,2,1,0:T(8,128)} %get-tuple-element.74.base_ref) | copy-start | bytes 1572868 | tf_op jit(solution)/shard_map/cond
  58.6 39.1 %collective-permute-start = (f32[128,128]{1,0:T(8,128)}, f32[128,128]{1,0:T(8,128)S(1)}, u32[]{:S(2)}, u32[]{:S(2)}) collective-permute-start(f32[128,128]{1,0:T(8,128)} %get-tuple-element.79), channel_id=1, source_target_pairs={{0,8},{1,9},{2,10},{3,11},{4,12},{5,13},{6,14},{7,15},{8,16},{9,17... | collective-permute-start | bytes 196616 | tf_op jit(solution)/shard_map/cond/branch_0_fun/ppermute | solution.py:520
  90.6 7.1 %collective-permute-start.1 = (f32[128,128]{1,0:T(8,128)}, f32[128,128]{1,0:T(8,128)S(1)}, u32[]{:S(2)}, u32[]{:S(2)}) collective-permute-start(f32[128,128]{1,0:T(8,128)} %get-tuple-element.80), channel_id=1, source_target_pairs={{0,16},{1,17},{2,18},{3,19},{4,20},{5,21},{6,22},{7,23},{8,24},{9,... | collective-permute-start | bytes 196616 | tf_op jit(solution)/shard_map/cond/branch_0_fun/ppermute | solution.py:520
  93.2 4.5 %collective-permute-start.2 = (f32[128,128]{1,0:T(8,128)}, f32[128,128]{1,0:T(8,128)S(1)}, u32[]{:S(2)}, u32[]{:S(2)}) collective-permute-start(f32[128,128]{1,0:T(8,128)} %get-tuple-element.81), channel_id=1, source_target_pairs={{0,24},{1,25},{2,26},{3,27},{4,28},{5,29},{6,30},{7,31},{8,0},{9,1... | collective-permute-start | bytes 196616 | tf_op jit(solution)/shard_map/cond/branch_0_fun/ppermute | solution.py:520
  97.6 0.6 copy-start.11
  97.7 0.6 copy-start.13
  97.7 0.6 copy-start.15
  100.6 4.1 %collective-permute-start.21 = (f32[4,128]{1,0:T(4,128)S(1)}, f32[4,128]{1,0:T(4,128)S(1)}, u32[]{:S(2)}, u32[]{:S(2)}) collective-permute-start(f32[4,128]{1,0:T(4,128)S(1)} %get-tuple-element.143.rest_0_), channel_id=1, source_target_pairs={{0,96},{32,0},{64,32},{96,64},{1,97},{33,1},{65,33},{97,65},{2,98}... | collective-permute-start | bytes 6152 | tf_op jit(solution)/shard_map/ppermute | solution.py:27
  103.4 5.1 %collective-permute-start.20 = (f32[4,128]{1,0:T(4,128)S(1)}, f32[4,128]{1,0:T(4,128)S(1)}, u32[]{:S(2)}, u32[]{:S(2)}) collective-permute-start(f32[4,128]{1,0:T(4,128)S(1)} %get-tuple-element.143.rest_0_), channel_id=1, source_target_pairs={{0,64},{32,96},{64,0},{96,32},{1,65},{33,97},{65,1},{97,33},{2,66}... | collective-permute-start | bytes 6152 | tf_op jit(solution)/shard_map/ppermute | solution.py:27
  103.5 5.0 %collective-permute-start.19 = (f32[4,128]{1,0:T(4,128)S(1)}, f32[4,128]{1,0:T(4,128)S(1)}, u32[]{:S(2)}, u32[]{:S(2)}) collective-permute-start(f32[4,128]{1,0:T(4,128)S(1)} %get-tuple-element.143.rest_0_), channel_id=1, source_target_pairs={{0,32},{32,64},{64,96},{96,0},{1,33},{33,65},{65,97},{97,1},{2,34}... | collective-permute-start | bytes 6152 | tf_op jit(solution)/shard_map/ppermute | solution.py:27
  110.7 37.1 %all-to-all-start.3 = ((f32[32,128,128]{2,1,0:T(8,128)}), f32[32,128,128]{2,1,0:T(8,128)S(1)}, u32[]{:S(2)}, u32[]{:S(2)}) async-start(f32[32,128,128]{2,1,0:T(8,128)} %shard_map.54), calls=%async_computation.3 | async-start | bytes 4194304 | tf_op jit(solution)/shard_map/all_to_all | solution.py:512
  115.7 15.4 %collective-permute-start.16 = (f32[4,2,128,128]{3,2,1,0:T(8,128)S(1)}, f32[4,2,128,128]{3,2,1,0:T(8,128)S(1)}, u32[]{:S(2)}, u32[]{:S(2)}) collective-permute-start(f32[4,2,128,128]{3,2,1,0:T(8,128)S(1)} %get-tuple-element.140.own_ref.x_ref), channel_id=1, source_target_pairs={{0,32},{32,64},{64,96},{96,0},{1,33},{33,65},{65,97},{97,1},{2,34}... | collective-permute-start | bytes 1572872 | tf_op jit(solution)/shard_map/ppermute | solution.py:500
  115.8 16.1 %collective-permute-start.15 = (f32[4,2,128,128]{3,2,1,0:T(8,128)S(1)}, f32[4,2,128,128]{3,2,1,0:T(8,128)S(1)}, u32[]{:S(2)}, u32[]{:S(2)}) collective-permute-start(f32[4,2,128,128]{3,2,1,0:T(8,128)S(1)} %get-tuple-element.140.own_ref.x_ref), channel_id=1, source_target_pairs={{0,96},{32,0},{64,32},{96,64},{1,97},{33,1},{65,33},{97,65},{2,98}... | collective-permute-start | bytes 1572872 | tf_op jit(solution)/shard_map/ppermute | solution.py:501
  131.1 9.8 %copy-start.6 = (f32[4,2,128,128]{3,2,1,0:T(8,128)}, f32[4,2,128,128]{3,2,1,0:T(8,128)S(1)}, u32[]{:S(2)}) copy-start(f32[4,2,128,128]{3,2,1,0:T(8,128)S(1)} %collective-permute-done.16.behind_ref) | copy-start | bytes 1572868
  131.9 9.1 %collective-permute-start.17 = (f32[2,2,128,128]{3,2,1,0:T(8,128)}, f32[2,2,128,128]{3,2,1,0:T(8,128)S(1)}, u32[]{:S(2)}, u32[]{:S(2)}) collective-permute-start(f32[2,2,128,128]{3,2,1,0:T(8,128)} %slice.26), channel_id=1, source_target_pairs={{0,32},{32,64},{64,96},{96,0},{1,33},{33,65},{65,97},{97,1},{2,34}... | collective-permute-start | bytes 786440 | tf_op jit(solution)/shard_map/ppermute | solution.py:502
  131.9 0.8 copy-start.7
  133.4 8.4 %collective-permute-start.18 = (f32[2,2,128,128]{3,2,1,0:T(8,128)}, f32[2,2,128,128]{3,2,1,0:T(8,128)}, u32[]{:S(2)}, u32[]{:S(2)}) collective-permute-start(f32[2,2,128,128]{3,2,1,0:T(8,128)} %slice.27), channel_id=1, source_target_pairs={{0,96},{32,0},{64,32},{96,64},{1,97},{33,1},{65,33},{97,65},{2,98}... | collective-permute-start | bytes 786440 | tf_op jit(solution)/shard_map/ppermute | solution.py:503
  140.9 0.9 copy-start.10
  149.4 7.8 %collective-permute-start.3 = (f32[128,128]{1,0:T(8,128)}, f32[128,128]{1,0:T(8,128)S(1)}, u32[]{:S(2)}, u32[]{:S(2)}) collective-permute-start(f32[128,128]{1,0:T(8,128)} %get-tuple-element.99), channel_id=1, source_target_pairs={{0,8},{1,9},{2,10},{3,11},{4,12},{5,13},{6,14},{7,15},{8,16},{9,17... | collective-permute-start | bytes 196616 | tf_op jit(solution)/shard_map/cond/branch_0_fun/ppermute | solution.py:520
  149.6 7.6 %collective-permute-start.4 = (f32[128,128]{1,0:T(8,128)}, f32[128,128]{1,0:T(8,128)S(1)}, u32[]{:S(2)}, u32[]{:S(2)}) collective-permute-start(f32[128,128]{1,0:T(8,128)} %get-tuple-element.100), channel_id=1, source_target_pairs={{0,16},{1,17},{2,18},{3,19},{4,20},{5,21},{6,22},{7,23},{8,24},{9,... | collective-permute-start | bytes 196616 | tf_op jit(solution)/shard_map/cond/branch_0_fun/ppermute | solution.py:520
  152.3 4.9 %collective-permute-start.5 = (f32[128,128]{1,0:T(8,128)}, f32[128,128]{1,0:T(8,128)S(1)}, u32[]{:S(2)}, u32[]{:S(2)}) collective-permute-start(f32[128,128]{1,0:T(8,128)} %get-tuple-element.101), channel_id=1, source_target_pairs={{0,24},{1,25},{2,26},{3,27},{4,28},{5,29},{6,30},{7,31},{8,0},{9,1... | collective-permute-start | bytes 196616 | tf_op jit(solution)/shard_map/cond/branch_0_fun/ppermute | solution.py:520
  157.2 0.6 copy-start.12
  157.3 0.6 copy-start.14
  157.3 0.6 copy-start.16
  160.2 6.8 %collective-permute-start.24 = (f32[4,128]{1,0:T(4,128)S(1)}, f32[4,128]{1,0:T(4,128)S(1)}, u32[]{:S(2)}, u32[]{:S(2)}) collective-permute-start(f32[4,128]{1,0:T(4,128)S(1)} %get-tuple-element.146.rest_0_), channel_id=1, source_target_pairs={{0,96},{32,0},{64,32},{96,64},{1,97},{33,1},{65,33},{97,65},{2,98}... | collective-permute-start | bytes 6152 | tf_op jit(solution)/shard_map/ppermute | solution.py:27
  165.7 5.1 %collective-permute-start.23 = (f32[4,128]{1,0:T(4,128)S(1)}, f32[4,128]{1,0:T(4,128)S(1)}, u32[]{:S(2)}, u32[]{:S(2)}) collective-permute-start(f32[4,128]{1,0:T(4,128)S(1)} %get-tuple-element.146.rest_0_), channel_id=1, source_target_pairs={{0,64},{32,96},{64,0},{96,32},{1,65},{33,97},{65,1},{97,33},{2,66}... | collective-permute-start | bytes 6152 | tf_op jit(solution)/shard_map/ppermute | solution.py:27
  165.7 5.1 %collective-permute-start.22 = (f32[4,128]{1,0:T(4,128)S(1)}, f32[4,128]{1,0:T(4,128)S(1)}, u32[]{:S(2)}, u32[]{:S(2)}) collective-permute-start(f32[4,128]{1,0:T(4,128)S(1)} %get-tuple-element.146.rest_0_), channel_id=1, source_target_pairs={{0,32},{32,64},{64,96},{96,0},{1,33},{33,65},{65,97},{97,1},{2,34}... | collective-permute-start | bytes 6152 | tf_op jit(solution)/shard_map/ppermute | solution.py:27
  167.0 3.8 %copy-start.17 = (f32[4,128]{1,0:T(4,128)}, f32[4,128]{1,0:T(4,128)S(1)}, u32[]{:S(2)}) copy-start(f32[4,128]{1,0:T(4,128)S(1)} %collective-permute-done.24.rest_3_) | copy-start | bytes 6148
  170.7 0.6 copy-start.18
  170.8 0.6 copy-start.19
